TPU v7x, 768 devices: a whole 4x8x12 slice. The times are simulated.
768 devices in a mesh: curve: 96 (over z, x, core), level: 8 (over y).
Axes of the slice: x: 4, y: 8, z: 12, core: 2. Of those that a mesh axis runs over, the one named last changes fastest.
Arguments:
- right_side: float32 [512, 98304], P(None, ('curve', 'level')), may hold values from -6 to 6
- counts: int32 [768], replicated, may hold values from 96 to 128, as said below
- neighbours: int32 [6, 98304], P(None, ('curve', 'level')), may hold values from -1 to 98303, as said below
Outputs:
- solution: float32 [512, 98304], P(None, ('curve', 'level'))
- residual: float32 [512, 98304], P(None, ('curve', 'level'))
- residual_norm: float32 [], replicated
Inputs may be any that keep to these rules, and one draw needn't show every extreme that they name: `counts`: some device holds 128 live bricks and some device holds 96. `neighbours`: A slot's global number is its device times 128 plus its position. The relation is symmetric across opposite faces; padding slots have -1 on every face and no brick names them. Live bricks are numbered along the curve; the brick across face 0, 2 or 4 lies earlier on the curve and the one across face 1, 3 or 5 later, at most 256 live bricks away.
All inputs are finite; a program needn't handle non-finite values.
Results may differ from a plain program's by a relative error of at most 0.00027.
Values sent between devices are 32-bit elements; how exact they have to be, the bound alone decides.
No kernel may reach another device: no remote copies, remote signals or barrier semaphores. Data moves between devices by JAX's collectives and lax.ppermute only.
A program may use at most 32 MiB of HBM per device.

v0:
```python
import functools

import jax
import jax.numpy as jnp
from jax import lax
from jax.sharding import Mesh
from jax.sharding import PartitionSpec as P

MIN_LIVE = 96
LAYER = 256
HOPS = 3
CURVE_LEVEL = ("curve_0", "curve_1", "curve_2", "level")


OPPOSITE = (1, 0, 3, 2, 5, 4)
RELAXATION = 2.0 / 3.0


def from_behind(block, axis, distance):
    devices = range(lax.axis_size(axis))
    route = [(i - distance, i) for i in devices if i - distance in devices]
    return lax.ppermute(block, axis, route)


def one_axis_at_a_time(x, axes):
    return functools.reduce(lax.psum, axes, x)


def brick_faces(values, extent):
    volume = values.reshape(extent, extent, extent, -1)
    surfaces = [
        volume[0],
        volume[extent - 1],
        volume[:, 0],
        volume[:, extent - 1],
        volume[:, :, 0],
        volume[:, :, extent - 1],
    ]
    return jnp.stack([one_face.reshape(extent * extent, -1) for one_face in surfaces])


def apply_operator(values, ghosts, extent, weight):
    brick_count = values.shape[1]
    volume = values.reshape(extent, extent, extent, brick_count)
    padded = jnp.pad(volume, ((1, 1), (1, 1), (1, 1), (0, 0)))
    shaped = [ghost.reshape(extent, extent, brick_count) for ghost in ghosts]
    padded = padded.at[0, 1:-1, 1:-1].set(shaped[0])
    padded = padded.at[-1, 1:-1, 1:-1].set(shaped[1])
    padded = padded.at[1:-1, 0, 1:-1].set(shaped[2])
    padded = padded.at[1:-1, -1, 1:-1].set(shaped[3])
    padded = padded.at[1:-1, 1:-1, 0].set(shaped[4])
    padded = padded.at[1:-1, 1:-1, -1].set(shaped[5])
    beside = padded[2:, 1:-1, 1:-1] + padded[:-2, 1:-1, 1:-1]
    beside = beside + padded[1:-1, 2:, 1:-1] + padded[1:-1, :-2, 1:-1]
    beside = beside + padded[1:-1, 1:-1, 2:] + padded[1:-1, 1:-1, :-2]
    return ((6.0 * volume - beside) * weight).reshape(extent * extent * extent, brick_count)


def restrict(values):
    brick_count = values.shape[1]
    grouped = values.reshape(4, 2, 4, 2, 4, 2, brick_count)
    return jnp.mean(grouped, axis=(1, 3, 5)).reshape(64, brick_count)


def prolong(coarse):
    brick_count = coarse.shape[1]
    spread = jnp.broadcast_to(
        coarse.reshape(4, 1, 4, 1, 4, 1, brick_count), (4, 2, 4, 2, 4, 2, brick_count)
    )
    return spread.reshape(512, brick_count)


def precondition(residual_in, exchange):
    relax_fine = RELAXATION / 6.0
    relax_coarse = RELAXATION / 1.5
    sweep_one = relax_fine * residual_in
    sweep_two = sweep_one + relax_fine * (
        residual_in - apply_operator(sweep_one, exchange(brick_faces(sweep_one, 8)), 8, 1.0)
    )
    defect = residual_in - apply_operator(sweep_two, exchange(brick_faces(sweep_two, 8)), 8, 1.0)
    coarse_rhs = restrict(defect)
    coarse_one = relax_coarse * coarse_rhs
    coarse_two = coarse_one + relax_coarse * (
        coarse_rhs - apply_operator(coarse_one, exchange(brick_faces(coarse_one, 4)), 4, 0.25)
    )
    sweep_three = sweep_two + prolong(coarse_two)
    return sweep_three + relax_fine * (
        residual_in - apply_operator(sweep_three, exchange(brick_faces(sweep_three, 8)), 8, 1.0)
    )


def local(right_side, counts, neighbours):
    slot_count = right_side.shape[1]
    device = lax.axis_index(CURVE_LEVEL)
    own_count = counts[device]
    live_slot = jnp.arange(slot_count, dtype=jnp.int32) < own_count
    residual_in = jnp.where(live_slot[None, :], right_side, jnp.zeros_like(right_side))
    widths = [min(slot_count, LAYER - (hop - 1) * MIN_LIVE) for hop in range(1, HOPS + 1)]
    window_starts = []
    running = slot_count
    for width in widths:
        window_starts.append(running)
        running = running + width
    width_table = jnp.array(widths, dtype=jnp.int32)
    start_table = jnp.array(window_starts, dtype=jnp.int32)
    present = neighbours >= 0
    safe_slot = jnp.where(present, neighbours, 0)
    owner = safe_slot // slot_count
    offset = safe_slot % slot_count
    earlier = (jnp.arange(6, dtype=jnp.int32) % 2 == 0)[:, None]
    hop_index = jnp.clip(jnp.where(earlier, device - owner, owner - device), 1, HOPS) - 1
    skipped = jnp.where(earlier, jnp.maximum(counts[owner] - width_table[hop_index], 0), 0)
    position = jnp.where(owner == device, offset, start_table[hop_index] + offset - skipped)
    position = jnp.clip(jnp.where(present, position, 0), 0, running - 1)

    def exchange(surface):
        odd_faces = surface[1::2]
        even_faces = surface[0::2]
        lower = []
        upper = []
        carried_low = odd_faces
        carried_high = even_faces
        for hop in range(1, HOPS + 1):
            width = widths[hop - 1]
            anchor = jnp.maximum(device - (hop - 1), 0)
            anchor_count = counts[anchor]
            start = jnp.maximum(anchor_count - width, 0)
            if hop > 1:
                start = start - jnp.maximum(anchor_count - widths[hop - 2], 0)
            piece = lax.dynamic_slice_in_dim(carried_low, start, width, 2)
            carried_low = from_behind(piece, CURVE_LEVEL, 1)
            carried_high = from_behind(carried_high[:, :, :width], CURVE_LEVEL, -1)
            lower.append(carried_low)
            upper.append(carried_high)
        ghosts = []
        for face_id in range(6):
            windows = lower if face_id % 2 == 0 else upper
            lookup = jnp.concatenate(
                [surface[OPPOSITE[face_id]]] + [window[face_id // 2] for window in windows], axis=1
            )
            picked = jnp.take(lookup, position[face_id], axis=1)
            ghosts.append(jnp.where(present[face_id][None, :], picked, jnp.zeros_like(picked)))
        return ghosts

    preconditioned = precondition(residual_in, exchange)
    image = apply_operator(preconditioned, exchange(brick_faces(preconditioned, 8)), 8, 1.0)
    local_along = jnp.sum(residual_in * preconditioned)
    local_curvature = jnp.sum(preconditioned * image)
    along, curvature, old_square, cross_term, image_square = (
        one_axis_at_a_time(local_along, CURVE_LEVEL),
        one_axis_at_a_time(local_curvature, CURVE_LEVEL),
        one_axis_at_a_time(jnp.sum(residual_in * residual_in), CURVE_LEVEL),
        one_axis_at_a_time(jnp.sum(residual_in * image), CURVE_LEVEL),
        one_axis_at_a_time(jnp.sum(image * image), CURVE_LEVEL),
    )
    step_size = along / curvature
    solution = step_size * preconditioned
    residual = residual_in - step_size * image
    norm_square = old_square - 2.0 * step_size * cross_term + step_size * step_size * image_square
    return (solution, residual, jnp.sqrt(norm_square))


def solution(mesh):
    split = Mesh(
        mesh.devices.reshape(12, 4, 2, mesh.shape["level"]),
        ("curve_0", "curve_1", "curve_2", "level"),
    )
    return jax.shard_map(
        local,
        mesh=split,
        in_specs=(P(None, CURVE_LEVEL), P(), P(None, CURVE_LEVEL)),
        out_specs=(P(None, CURVE_LEVEL), P(None, CURVE_LEVEL), P()),
        check_vma=False,
    )
```

profile of v0, /device:TPU:1, one launch (start us, length us, event | category | flops | bytes accessed | tf_op | source)
XLA Modules:
  0.0 302.5 jit_solution(7051350016861100586)
XLA Ops:
  4.6 6.5 %collective-permute-start.3 = (f32[3,64,128]{1,2,0:T(8,128)S(1)}, f32[3,64,128]{1,2,0:T(8,128)S(1)}, u32[]{:S(2)}, u32[]{:S(2)}) collective-permute-start(f32[3,64,128]{1,2,0:T(8,128)S(1)} %get-tuple-element.418), channel_id=1, source_target_pairs={{1,0},{2,1},{3,2},{4,3},{5,4},{6,5},{7,6},{8,7},{9,8},{10,9},{11,1... | collective-permute-start | bytes 294920 | tf_op jit(solution)/shard_map/ppermute | solution.py:22
  15.2 3.2 %gather_fusion.1 = s32[768]{0:T(1024)S(1)} fusion(s32[768]{0:T(1024)S(1)} %copy-done.2, s32[1024]{0:T(1024)S(1)} %get-tuple-element.572), kind=kCustom, calls=%fused_computation.31 | custom fusion | bytes 9216 | tf_op jit(solution)/shard_map/gather | solution.py:112
  19.0 4.8 %gather_fusion.2 = s32[768]{0:T(1024)S(1)} fusion(s32[3]{0:T(128)S(1)} %copy-done.1, s32[1024]{0:T(1024)S(1)} %get-tuple-element.573), kind=kCustom, calls=%fused_computation.32 | custom fusion | bytes 9216 | tf_op jit(solution)/shard_map/gather | solution.py:112
  23.8 4.8 %gather_fusion = s32[768]{0:T(1024)S(1)} fusion(s32[3]{0:T(128)S(1)} %copy-done, s32[1024]{0:T(1024)S(1)} %get-tuple-element.573), kind=kCustom, calls=%fused_computation.30 | custom fusion | bytes 9216 | tf_op jit(solution)/shard_map/gather | solution.py:113
  29.3 4.9 %collective-permute-start.4 = (f32[3,64,128]{1,2,0:T(8,128)S(1)}, f32[3,64,128]{1,2,0:T(8,128)S(1)}, u32[]{:S(2)}, u32[]{:S(2)}) collective-permute-start(f32[3,64,128]{1,2,0:T(8,128)S(1)} %collective-permute-done.3), channel_id=1, source_target_pairs={{1,0},{2,1},{3,2},{4,3},{5,4},{6,5},{7,6},{8,7},{9,8},{10,9},{11,1... | collective-permute-start | bytes 294920 | tf_op jit(solution)/shard_map/ppermute | solution.py:22
  36.8 5.6 %collective-permute-start.5 = (f32[3,64,64]{1,2,0:T(8,128)S(1)}, f32[3,64,64]{1,2,0:T(8,128)S(1)}, u32[]{:S(2)}, u32[]{:S(2)}) collective-permute-start(f32[3,64,64]{1,2,0:T(8,128)S(1)} %slice.1835), channel_id=1, source_target_pairs={{1,0},{2,1},{3,2},{4,3},{5,4},{6,5},{7,6},{8,7},{9,8},{10,9},{11,1... | collective-permute-start | bytes 147464 | tf_op jit(solution)/shard_map/ppermute | solution.py:22
  58.3 2.9 collective-permute-start.6
  61.8 4.1 %collective-permute-start.10 = (f32[3,64,128]{1,2,0:T(8,128)S(1)}, f32[3,64,128]{1,2,0:T(8,128)S(1)}, u32[]{:S(2)}, u32[]{:S(2)}) collective-permute-start(f32[3,64,128]{1,2,0:T(8,128)S(1)} %collective-permute-done.9), channel_id=1, source_target_pairs={{1,0},{2,1},{3,2},{4,3},{5,4},{6,5},{7,6},{8,7},{9,8},{10,9},{11,1... | collective-permute-start | bytes 294920 | tf_op jit(solution)/shard_map/ppermute | solution.py:22
  68.5 5.6 %collective-permute-start.11 = (f32[3,64,64]{1,2,0:T(8,128)S(1)}, f32[3,64,64]{1,2,0:T(8,128)S(1)}, u32[]{:S(2)}, u32[]{:S(2)}) collective-permute-start(f32[3,64,64]{1,2,0:T(8,128)S(1)} %slice.1866), channel_id=1, source_target_pairs={{1,0},{2,1},{3,2},{4,3},{5,4},{6,5},{7,6},{8,7},{9,8},{10,9},{11,1... | collective-permute-start | bytes 147464 | tf_op jit(solution)/shard_map/ppermute | solution.py:22
  88.4 3.0 collective-permute-start.12
  91.4 4.9 %collective-permute-start.16 = (f32[3,16,128]{2,1,0:T(8,128)S(1)}, f32[3,16,128]{2,1,0:T(8,128)S(1)}, u32[]{:S(2)}, u32[]{:S(2)}) collective-permute-start(f32[3,16,128]{2,1,0:T(8,128)S(1)} %collective-permute-done.15), channel_id=1, source_target_pairs={{1,0},{2,1},{3,2},{4,3},{5,4},{6,5},{7,6},{8,7},{9,8},{10,9},{11,1... | collective-permute-start | bytes 73736 | tf_op jit(solution)/shard_map/ppermute | solution.py:22
  98.3 5.2 %collective-permute-start.17 = (f32[3,16,64]{2,1,0:T(8,128)S(1)}, f32[3,16,64]{2,1,0:T(8,128)S(1)}, u32[]{:S(2)}, u32[]{:S(2)}) collective-permute-start(f32[3,16,64]{2,1,0:T(8,128)S(1)} %bitcast.527), channel_id=1, source_target_pairs={{1,0},{2,1},{3,2},{4,3},{5,4},{6,5},{7,6},{8,7},{9,8},{10,9},{11,1... | collective-permute-start | bytes 36872 | tf_op jit(solution)/shard_map/ppermute | solution.py:22
  105.6 4.7 %collective-permute-done.14 = f32[3,16,64]{2,1,0:T(8,128)S(1)} collective-permute-done((f32[3,16,64]{2,1,0:T(8,128)S(1)}, f32[3,16,64]{2,1,0:T(8,128)S(1)}, u32[]{:S(2)}, u32[]{:S(2)}) %collective-permute-start.14) | collective-permute-done | bytes 12320 | tf_op jit(solution)/shard_map/ppermute | solution.py:22
  117.8 4.2 %collective-permute-start.21 = (f32[3,64,128]{1,2,0:T(8,128)S(1)}, f32[3,64,128]{1,2,0:T(8,128)S(1)}, u32[]{:S(2)}, u32[]{:S(2)}) collective-permute-start(f32[3,64,128]{1,2,0:T(8,128)S(1)} %get-tuple-element.414), channel_id=1, source_target_pairs={{1,0},{2,1},{3,2},{4,3},{5,4},{6,5},{7,6},{8,7},{9,8},{10,9},{11,1... | collective-permute-start | bytes 294920 | tf_op jit(solution)/shard_map/ppermute | solution.py:22
  125.3 5.0 %collective-permute-start.22 = (f32[3,64,128]{1,2,0:T(8,128)S(1)}, f32[3,64,128]{1,2,0:T(8,128)S(1)}, u32[]{:S(2)}, u32[]{:S(2)}) collective-permute-start(f32[3,64,128]{1,2,0:T(8,128)S(1)} %collective-permute-done.21), channel_id=1, source_target_pairs={{1,0},{2,1},{3,2},{4,3},{5,4},{6,5},{7,6},{8,7},{9,8},{10,9},{11,1... | collective-permute-start | bytes 294920 | tf_op jit(solution)/shard_map/ppermute | solution.py:22
  133.9 4.7 %collective-permute-start.23 = (f32[3,64,64]{1,2,0:T(8,128)S(1)}, f32[3,64,64]{1,2,0:T(8,128)S(1)}, u32[]{:S(2)}, u32[]{:S(2)}) collective-permute-start(f32[3,64,64]{1,2,0:T(8,128)S(1)} %slice.1928), channel_id=1, source_target_pairs={{1,0},{2,1},{3,2},{4,3},{5,4},{6,5},{7,6},{8,7},{9,8},{10,9},{11,1... | collective-permute-start | bytes 147464 | tf_op jit(solution)/shard_map/ppermute | solution.py:22
  151.8 4.7 %collective-permute-start.27 = (f32[3,64,128]{1,2,0:T(8,128)S(1)}, f32[3,64,128]{1,2,0:T(8,128)S(1)}, u32[]{:S(2)}, u32[]{:S(2)}) collective-permute-start(f32[3,64,128]{1,2,0:T(8,128)S(1)} %get-tuple-element.412), channel_id=1, source_target_pairs={{1,0},{2,1},{3,2},{4,3},{5,4},{6,5},{7,6},{8,7},{9,8},{10,9},{11,1... | collective-permute-start | bytes 294920 | tf_op jit(solution)/shard_map/ppermute | solution.py:22
  159.1 5.6 %collective-permute-start.28 = (f32[3,64,128]{1,2,0:T(8,128)S(1)}, f32[3,64,128]{1,2,0:T(8,128)S(1)}, u32[]{:S(2)}, u32[]{:S(2)}) collective-permute-start(f32[3,64,128]{1,2,0:T(8,128)S(1)} %collective-permute-done.27), channel_id=1, source_target_pairs={{1,0},{2,1},{3,2},{4,3},{5,4},{6,5},{7,6},{8,7},{9,8},{10,9},{11,1... | collective-permute-start | bytes 294920 | tf_op jit(solution)/shard_map/ppermute | solution.py:22
  167.7 5.2 %collective-permute-start.29 = (f32[3,64,64]{1,2,0:T(8,128)S(1)}, f32[3,64,64]{1,2,0:T(8,128)S(1)}, u32[]{:S(2)}, u32[]{:S(2)}) collective-permute-start(f32[3,64,64]{1,2,0:T(8,128)S(1)} %slice.1959), channel_id=1, source_target_pairs={{1,0},{2,1},{3,2},{4,3},{5,4},{6,5},{7,6},{8,7},{9,8},{10,9},{11,1... | collective-permute-start | bytes 147464 | tf_op jit(solution)/shard_map/ppermute | solution.py:22
  178.1 3.5 %collective-permute-done.26 = f32[3,64,64]{1,2,0:T(8,128)S(1)} collective-permute-done((f32[3,64,64]{1,2,0:T(8,128)S(1)}, f32[3,64,64]{1,2,0:T(8,128)S(1)}, u32[]{:S(2)}, u32[]{:S(2)}) %collective-permute-start.26) | collective-permute-done | bytes 49184 | tf_op jit(solution)/shard_map/ppermute | solution.py:22
  186.7 48.6 %all-reduce.5 = (f32[]{:T(128)}, f32[]{:T(128)}, f32[]{:T(128)}, f32[]{:T(128)}, f32[]{:T(128)}) all-reduce(f32[]{:T(128)} %get-tuple-element.375, f32[]{:T(128)} %get-tuple-element.376, f32[]{:T(128)} %get-tuple-element.377, f32[]{:T(128)} %get-tuple-element.374, ...), channel_id=1, replica_groups=mesh['curve_0'=12,'curve_1'=4,'curve_2'=2,'level'=8] {'curve_0'}, use_global_device_ids=true, to_apply=%region_2.5 | all-reduce | flops 5 | bytes 40 | tf_op jit(solution)/shard_map/psum | solution.py:26
  235.4 6.7 %all-reduce.7 = (f32[]{:T(128)}, f32[]{:T(128)}, f32[]{:T(128)}, f32[]{:T(128)}, f32[]{:T(128)}) all-reduce(f32[]{:T(128)} %get-tuple-element.378, f32[]{:T(128)} %get-tuple-element.379, f32[]{:T(128)} %get-tuple-element.380, f32[]{:T(128)} %get-tuple-element.381, ...), channel_id=1, replica_groups=mesh['curve_0'=12,'curve_1'=4,'curve_2'=2,'level'=8] {'curve_1'}, use_global_device_ids=true, to_apply=%region_3.6 | all-reduce | flops 5 | bytes 40 | tf_op jit(solution)/shard_map/psum | solution.py:26
  242.1 42.8 %all-reduce.8 = (f32[]{:T(128)}, f32[]{:T(128)}, f32[]{:T(128)}, f32[]{:T(128)}, f32[]{:T(128)}) all-reduce(f32[]{:T(128)} %get-tuple-element.388, f32[]{:T(128)} %get-tuple-element.389, f32[]{:T(128)} %get-tuple-element.390, f32[]{:T(128)} %get-tuple-element.391, ...), channel_id=1, replica_groups=mesh['curve_0'=12,'curve_1'=4,'curve_2'=2,'level'=8] {'curve_2'}, use_global_device_ids=true, to_apply=%region_4.7 | all-reduce | flops 5 | bytes 40 | tf_op jit(solution)/shard_map/psum | solution.py:26
  284.8 11.5 %all-reduce.6 = (f32[]{:T(128)}, f32[]{:T(128)}, f32[]{:T(128)}, f32[]{:T(128)}, f32[]{:T(128)}) all-reduce(f32[]{:T(128)} %get-tuple-element.393, f32[]{:T(128)} %get-tuple-element.394, f32[]{:T(128)} %get-tuple-element.395, f32[]{:T(128)} %get-tuple-element.396, ...), channel_id=1, replica_groups=mesh['curve_0'=12,'curve_1'=4,'curve_2'=2,'level'=8] {'level'}, use_global_device_ids=true, to_apply=%region_5.8 | all-reduce | flops 5 | bytes 40 | tf_op jit(solution)/shard_map/psum | solution.py:26
  (375 shorter events, 91.3 us)
Async XLA Ops:
  4.6 24.7 %collective-permute-start.3 = (f32[3,64,128]{1,2,0:T(8,128)S(1)}, f32[3,64,128]{1,2,0:T(8,128)S(1)}, u32[]{:S(2)}, u32[]{:S(2)}) collective-permute-start(f32[3,64,128]{1,2,0:T(8,128)S(1)} %get-tuple-element.418), channel_id=1, source_target_pairs={{1,0},{2,1},{3,2},{4,3},{5,4},{6,5},{7,6},{8,7},{9,8},{10,9},{11,1... | collective-permute-start | bytes 294920 | tf_op jit(solution)/shard_map/ppermute | solution.py:22
  11.0 23.1 %collective-permute-start = (f32[3,64,128]{1,2,0:T(8,128)S(1)}, f32[3,64,128]{1,2,0:T(8,128)S(1)}, u32[]{:S(2)}, u32[]{:S(2)}) collective-permute-start(f32[3,64,128]{1,2,0:T(8,128)S(1)} %get-tuple-element.419), channel_id=1, source_target_pairs={{0,1},{1,2},{2,3},{3,4},{4,5},{5,6},{6,7},{7,8},{8,9},{9,10},{10,1... | collective-permute-start | bytes 294920 | tf_op jit(solution)/shard_map/ppermute | solution.py:22
  29.3 7.5 %collective-permute-start.4 = (f32[3,64,128]{1,2,0:T(8,128)S(1)}, f32[3,64,128]{1,2,0:T(8,128)S(1)}, u32[]{:S(2)}, u32[]{:S(2)}) collective-permute-start(f32[3,64,128]{1,2,0:T(8,128)S(1)} %collective-permute-done.3), channel_id=1, source_target_pairs={{1,0},{2,1},{3,2},{4,3},{5,4},{6,5},{7,6},{8,7},{9,8},{10,9},{11,1... | collective-permute-start | bytes 294920 | tf_op jit(solution)/shard_map/ppermute | solution.py:22
  34.2 9.4 %collective-permute-start.1 = (f32[3,64,128]{1,2,0:T(8,128)S(1)}, f32[3,64,128]{1,2,0:T(8,128)S(1)}, u32[]{:S(2)}, u32[]{:S(2)}) collective-permute-start(f32[3,64,128]{1,2,0:T(8,128)S(1)} %collective-permute-done), channel_id=1, source_target_pairs={{0,1},{1,2},{2,3},{3,4},{4,5},{5,6},{6,7},{7,8},{8,9},{9,10},{10,1... | collective-permute-start | bytes 294920 | tf_op jit(solution)/shard_map/ppermute | solution.py:22
  36.8 8.8 %collective-permute-start.5 = (f32[3,64,64]{1,2,0:T(8,128)S(1)}, f32[3,64,64]{1,2,0:T(8,128)S(1)}, u32[]{:S(2)}, u32[]{:S(2)}) collective-permute-start(f32[3,64,64]{1,2,0:T(8,128)S(1)} %slice.1835), channel_id=1, source_target_pairs={{1,0},{2,1},{3,2},{4,3},{5,4},{6,5},{7,6},{8,7},{9,8},{10,9},{11,1... | collective-permute-start | bytes 147464 | tf_op jit(solution)/shard_map/ppermute | solution.py:22
  43.6 7.1 %collective-permute-start.2 = (f32[3,64,64]{1,2,0:T(8,128)S(1)}, f32[3,64,64]{1,2,0:T(8,128)S(1)}, u32[]{:S(2)}, u32[]{:S(2)}) collective-permute-start(f32[3,64,64]{1,2,0:T(8,128)S(1)} %constant_dynamic-slice_fusion.4), channel_id=1, source_target_pairs={{0,1},{1,2},{2,3},{3,4},{4,5},{5,6},{6,7},{7,8},{8,9},{9,10},{10,1... | collective-permute-start | bytes 147464 | tf_op jit(solution)/shard_map/ppermute | solution.py:22
  58.3 8.2 %collective-permute-start.6 = (f32[3,64,128]{1,2,0:T(8,128)S(1)}, f32[3,64,128]{1,2,0:T(8,128)S(1)}, u32[]{:S(2)}, u32[]{:S(2)}) collective-permute-start(f32[3,64,128]{1,2,0:T(8,128)S(1)} %get-tuple-element.417), channel_id=1, source_target_pairs={{0,1},{1,2},{2,3},{3,4},{4,5},{5,6},{6,7},{7,8},{8,9},{9,10},{10,1... | collective-permute-start | bytes 294920 | tf_op jit(solution)/shard_map/ppermute | solution.py:22
  66.5 8.2 %collective-permute-start.7 = (f32[3,64,128]{1,2,0:T(8,128)S(1)}, f32[3,64,128]{1,2,0:T(8,128)S(1)}, u32[]{:S(2)}, u32[]{:S(2)}) collective-permute-start(f32[3,64,128]{1,2,0:T(8,128)S(1)} %collective-permute-done.6), channel_id=1, source_target_pairs={{0,1},{1,2},{2,3},{3,4},{4,5},{5,6},{6,7},{7,8},{8,9},{9,10},{10,1... | collective-permute-start | bytes 294920 | tf_op jit(solution)/shard_map/ppermute | solution.py:22
  68.5 8.1 %collective-permute-start.11 = (f32[3,64,64]{1,2,0:T(8,128)S(1)}, f32[3,64,64]{1,2,0:T(8,128)S(1)}, u32[]{:S(2)}, u32[]{:S(2)}) collective-permute-start(f32[3,64,64]{1,2,0:T(8,128)S(1)} %slice.1866), channel_id=1, source_target_pairs={{1,0},{2,1},{3,2},{4,3},{5,4},{6,5},{7,6},{8,7},{9,8},{10,9},{11,1... | collective-permute-start | bytes 147464 | tf_op jit(solution)/shard_map/ppermute | solution.py:22
  88.4 7.9 %collective-permute-start.12 = (f32[3,16,128]{2,1,0:T(8,128)S(1)}, f32[3,16,128]{2,1,0:T(8,128)S(1)}, u32[]{:S(2)}, u32[]{:S(2)}) collective-permute-start(f32[3,16,128]{2,1,0:T(8,128)S(1)} %get-tuple-element.525), channel_id=1, source_target_pairs={{0,1},{1,2},{2,3},{3,4},{4,5},{5,6},{6,7},{7,8},{8,9},{9,10},{10,1... | collective-permute-start | bytes 73736 | tf_op jit(solution)/shard_map/ppermute | solution.py:22
  96.4 7.2 %collective-permute-start.13 = (f32[3,16,128]{2,1,0:T(8,128)S(1)}, f32[3,16,128]{2,1,0:T(8,128)S(1)}, u32[]{:S(2)}, u32[]{:S(2)}) collective-permute-start(f32[3,16,128]{2,1,0:T(8,128)S(1)} %collective-permute-done.12), channel_id=1, source_target_pairs={{0,1},{1,2},{2,3},{3,4},{4,5},{5,6},{6,7},{7,8},{8,9},{9,10},{10,1... | collective-permute-start | bytes 73736 | tf_op jit(solution)/shard_map/ppermute | solution.py:22
  98.3 14.8 %collective-permute-start.17 = (f32[3,16,64]{2,1,0:T(8,128)S(1)}, f32[3,16,64]{2,1,0:T(8,128)S(1)}, u32[]{:S(2)}, u32[]{:S(2)}) collective-permute-start(f32[3,16,64]{2,1,0:T(8,128)S(1)} %bitcast.527), channel_id=1, source_target_pairs={{1,0},{2,1},{3,2},{4,3},{5,4},{6,5},{7,6},{8,7},{9,8},{10,9},{11,1... | collective-permute-start | bytes 36872 | tf_op jit(solution)/shard_map/ppermute | solution.py:22
  117.8 7.5 %collective-permute-start.21 = (f32[3,64,128]{1,2,0:T(8,128)S(1)}, f32[3,64,128]{1,2,0:T(8,128)S(1)}, u32[]{:S(2)}, u32[]{:S(2)}) collective-permute-start(f32[3,64,128]{1,2,0:T(8,128)S(1)} %get-tuple-element.414), channel_id=1, source_target_pairs={{1,0},{2,1},{3,2},{4,3},{5,4},{6,5},{7,6},{8,7},{9,8},{10,9},{11,1... | collective-permute-start | bytes 294920 | tf_op jit(solution)/shard_map/ppermute | solution.py:22
  122.6 8.2 %collective-permute-start.18 = (f32[3,64,128]{1,2,0:T(8,128)S(1)}, f32[3,64,128]{1,2,0:T(8,128)S(1)}, u32[]{:S(2)}, u32[]{:S(2)}) collective-permute-start(f32[3,64,128]{1,2,0:T(8,128)S(1)} %get-tuple-element.415), channel_id=1, source_target_pairs={{0,1},{1,2},{2,3},{3,4},{4,5},{5,6},{6,7},{7,8},{8,9},{9,10},{10,1... | collective-permute-start | bytes 294920 | tf_op jit(solution)/shard_map/ppermute | solution.py:22
  125.3 8.6 %collective-permute-start.22 = (f32[3,64,128]{1,2,0:T(8,128)S(1)}, f32[3,64,128]{1,2,0:T(8,128)S(1)}, u32[]{:S(2)}, u32[]{:S(2)}) collective-permute-start(f32[3,64,128]{1,2,0:T(8,128)S(1)} %collective-permute-done.21), channel_id=1, source_target_pairs={{1,0},{2,1},{3,2},{4,3},{5,4},{6,5},{7,6},{8,7},{9,8},{10,9},{11,1... | collective-permute-start | bytes 294920 | tf_op jit(solution)/shard_map/ppermute | solution.py:22
  130.8 9.1 %collective-permute-start.19 = (f32[3,64,128]{1,2,0:T(8,128)S(1)}, f32[3,64,128]{1,2,0:T(8,128)S(1)}, u32[]{:S(2)}, u32[]{:S(2)}) collective-permute-start(f32[3,64,128]{1,2,0:T(8,128)S(1)} %collective-permute-done.18), channel_id=1, source_target_pairs={{0,1},{1,2},{2,3},{3,4},{4,5},{5,6},{6,7},{7,8},{8,9},{9,10},{10,1... | collective-permute-start | bytes 294920 | tf_op jit(solution)/shard_map/ppermute | solution.py:22
  133.9 8.2 %collective-permute-start.23 = (f32[3,64,64]{1,2,0:T(8,128)S(1)}, f32[3,64,64]{1,2,0:T(8,128)S(1)}, u32[]{:S(2)}, u32[]{:S(2)}) collective-permute-start(f32[3,64,64]{1,2,0:T(8,128)S(1)} %slice.1928), channel_id=1, source_target_pairs={{1,0},{2,1},{3,2},{4,3},{5,4},{6,5},{7,6},{8,7},{9,8},{10,9},{11,1... | collective-permute-start | bytes 147464 | tf_op jit(solution)/shard_map/ppermute | solution.py:22
  140.0 7.2 %collective-permute-start.20 = (f32[3,64,64]{1,2,0:T(8,128)S(1)}, f32[3,64,64]{1,2,0:T(8,128)S(1)}, u32[]{:S(2)}, u32[]{:S(2)}) collective-permute-start(f32[3,64,64]{1,2,0:T(8,128)S(1)} %constant_dynamic-slice_fusion.1), channel_id=1, source_target_pairs={{0,1},{1,2},{2,3},{3,4},{4,5},{5,6},{6,7},{7,8},{8,9},{9,10},{10,1... | collective-permute-start | bytes 147464 | tf_op jit(solution)/shard_map/ppermute | solution.py:22
  151.8 7.3 %collective-permute-start.27 = (f32[3,64,128]{1,2,0:T(8,128)S(1)}, f32[3,64,128]{1,2,0:T(8,128)S(1)}, u32[]{:S(2)}, u32[]{:S(2)}) collective-permute-start(f32[3,64,128]{1,2,0:T(8,128)S(1)} %get-tuple-element.412), channel_id=1, source_target_pairs={{1,0},{2,1},{3,2},{4,3},{5,4},{6,5},{7,6},{8,7},{9,8},{10,9},{11,1... | collective-permute-start | bytes 294920 | tf_op jit(solution)/shard_map/ppermute | solution.py:22
  157.1 8.2 %collective-permute-start.24 = (f32[3,64,128]{1,2,0:T(8,128)S(1)}, f32[3,64,128]{1,2,0:T(8,128)S(1)}, u32[]{:S(2)}, u32[]{:S(2)}) collective-permute-start(f32[3,64,128]{1,2,0:T(8,128)S(1)} %get-tuple-element.413), channel_id=1, source_target_pairs={{0,1},{1,2},{2,3},{3,4},{4,5},{5,6},{6,7},{7,8},{8,9},{9,10},{10,1... | collective-permute-start | bytes 294920 | tf_op jit(solution)/shard_map/ppermute | solution.py:22
  159.1 8.6 %collective-permute-start.28 = (f32[3,64,128]{1,2,0:T(8,128)S(1)}, f32[3,64,128]{1,2,0:T(8,128)S(1)}, u32[]{:S(2)}, u32[]{:S(2)}) collective-permute-start(f32[3,64,128]{1,2,0:T(8,128)S(1)} %collective-permute-done.27), channel_id=1, source_target_pairs={{1,0},{2,1},{3,2},{4,3},{5,4},{6,5},{7,6},{8,7},{9,8},{10,9},{11,1... | collective-permute-start | bytes 294920 | tf_op jit(solution)/shard_map/ppermute | solution.py:22
  165.3 8.2 %collective-permute-start.25 = (f32[3,64,128]{1,2,0:T(8,128)S(1)}, f32[3,64,128]{1,2,0:T(8,128)S(1)}, u32[]{:S(2)}, u32[]{:S(2)}) collective-permute-start(f32[3,64,128]{1,2,0:T(8,128)S(1)} %collective-permute-done.24), channel_id=1, source_target_pairs={{0,1},{1,2},{2,3},{3,4},{4,5},{5,6},{6,7},{7,8},{8,9},{9,10},{10,1... | collective-permute-start | bytes 294920 | tf_op jit(solution)/shard_map/ppermute | solution.py:22
  167.7 7.7 %collective-permute-start.29 = (f32[3,64,64]{1,2,0:T(8,128)S(1)}, f32[3,64,64]{1,2,0:T(8,128)S(1)}, u32[]{:S(2)}, u32[]{:S(2)}) collective-permute-start(f32[3,64,64]{1,2,0:T(8,128)S(1)} %slice.1959), channel_id=1, source_target_pairs={{1,0},{2,1},{3,2},{4,3},{5,4},{6,5},{7,6},{8,7},{9,8},{10,9},{11,1... | collective-permute-start | bytes 147464 | tf_op jit(solution)/shard_map/ppermute | solution.py:22
  173.5 8.0 %collective-permute-start.26 = (f32[3,64,64]{1,2,0:T(8,128)S(1)}, f32[3,64,64]{1,2,0:T(8,128)S(1)}, u32[]{:S(2)}, u32[]{:S(2)}) collective-permute-start(f32[3,64,64]{1,2,0:T(8,128)S(1)} %constant_dynamic-slice_fusion), channel_id=1, source_target_pairs={{0,1},{1,2},{2,3},{3,4},{4,5},{5,6},{6,7},{7,8},{8,9},{9,10},{10,1... | collective-permute-start | bytes 147464 | tf_op jit(solution)/shard_map/ppermute | solution.py:22
  (10 other events, 45.9 us)
where the time goes:
time: 307 us; the launch traced here: 302 us
  blocking collectives  110 us (36%)
  starting transfers between devices  102 us (33%)
  local copies, waits for them, and re-layouts  50.7 us (17%)
  waiting for transfers between devices  24.6 us (8%)
  between operations  8.55 us (3%)
  other arithmetic  7.15 us (2%)
    psum x4, blocking collectives, one_axis_at_a_time(): return functools.reduce(lax.psum, axes, x)  110 us
    ppermute x30, starting transfers between devices, from_behind(): return lax.ppermute(block, axis, route)  102 us
    ppermute x30, waiting for transfers between devices, from_behind(): return lax.ppermute(block, axis, route)  24.6 us
    gather x30, local copies, waits for them, and re-layouts, exchange(): picked = jnp.take(lookup, position[face_id], axis=1)  19.5 us
  transfers between devices with their start and end apart: 30, of which 19 were waited for; matrix products, arithmetic and copies ran while one was open for 9% of the time, Pallas kernels for 0%

commit v1 on v0

v1 whole, which is shorter than its diff:
```python
import functools

import jax
import jax.numpy as jnp
from jax import lax
from jax.experimental import pallas as pl
from jax.experimental.pallas import tpu as pltpu
from jax.sharding import Mesh
from jax.sharding import PartitionSpec as P

LANES = 128
TAIL = 64
FINE = 192
COARSE = 48
GROUP = 16
AXES = ("outer", "inner")
RELAX_FINE = (2.0 / 3.0) / 6.0
RELAX_COARSE = (2.0 / 3.0) / 1.5

VMEM = pl.BlockSpec(memory_space=pltpu.VMEM)
SMEM = pl.BlockSpec(memory_space=pltpu.SMEM)

LANE_ROW = 0
WINDOW_ROW = 8
FORWARD_UP = 16
FORWARD_DOWN = 24
TABLE_ROWS = 32


def f32(*shape):
    return jax.ShapeDtypeStruct(shape, jnp.float32)


def i32(*shape):
    return jax.ShapeDtypeStruct(shape, jnp.int32)


def call(kernel, name, outs, *args, in_specs=None, out_specs=None, scratch=()):
    return pl.pallas_call(
        kernel,
        out_shape=outs,
        in_specs=in_specs or [VMEM] * len(args),
        out_specs=out_specs or [VMEM] * len(outs),
        scratch_shapes=list(scratch),
        name=name,
    )(*args)


def take(block, lanes):
    return jnp.take_along_axis(block, lanes, axis=1, mode="promise_in_bounds")


def write_faces(values, up, down):
    up[0:64, :] = values[448:512, :]
    down[0:64, :] = values[0:64, :]
    for x in range(8):
        up[64 + 8 * x : 72 + 8 * x, :] = values[64 * x + 56 : 64 * x + 64, :]
        down[64 + 8 * x : 72 + 8 * x, :] = values[64 * x : 64 * x + 8, :]
    up[128:192, :] = values[pl.ds(7, 64, stride=8), :]
    down[128:192, :] = values[pl.ds(0, 64, stride=8), :]


def write_coarse_faces(values, up, down):
    up[0:16, :] = values[48:64, :]
    down[0:16, :] = values[0:16, :]
    for x in range(4):
        up[16 + 4 * x : 20 + 4 * x, :] = values[16 * x + 12 : 16 * x + 16, :]
        down[16 + 4 * x : 20 + 4 * x, :] = values[16 * x : 16 * x + 4, :]
    up[32:48, :] = values[pl.ds(3, 16, stride=4), :]
    down[32:48, :] = values[pl.ds(0, 16, stride=4), :]


def read_ghosts(table, windows, ghosts, rows):
    per_face = rows // 3
    packed = rows // 2
    for face in range(6):
        own, near, far = windows[face % 2]
        lane = jnp.broadcast_to(table[LANE_ROW + face : LANE_ROW + face + 1, :], (8, LANES))
        window = jnp.broadcast_to(table[WINDOW_ROW + face : WINDOW_ROW + face + 1, :], (8, LANES))
        is_own, is_near, is_far, is_last = [window == which for which in range(4)]
        first_half = jnp.minimum(lane, TAIL - 1)
        second_half = first_half + TAIL
        for step in range(0, per_face, 8):
            row = (face // 2) * per_face + step
            last_row = rows + row % packed
            last_lane = first_half if row < packed else second_half
            picked = jnp.where(is_last, take(far[last_row : last_row + 8, :], last_lane), 0.0)
            picked = jnp.where(is_far, take(far[row : row + 8, :], lane), picked)
            picked = jnp.where(is_near, take(near[row : row + 8, :], lane), picked)
            picked = jnp.where(is_own, take(own[row : row + 8, :], lane), picked)
            ghosts[face * per_face + step : face * per_face + step + 8, :] = picked


def beside(values, ghosts, x, y):
    sub = lax.broadcasted_iota(jnp.int32, (8, LANES), 0)
    at = 64 * x + 8 * y
    line = 8 * x + y
    centre = values[at : at + 8, :]
    below_x = values[at - 64 : at - 56, :] if x > 0 else ghosts[8 * y : 8 * y + 8, :]
    above_x = values[at + 64 : at + 72, :] if x < 7 else ghosts[64 + 8 * y : 72 + 8 * y, :]
    below_y = values[at - 8 : at, :] if y > 0 else ghosts[128 + 8 * x : 136 + 8 * x, :]
    above_y = values[at + 8 : at + 16, :] if y < 7 else ghosts[192 + 8 * x : 200 + 8 * x, :]
    below_z = jnp.where(sub == 0, ghosts[256 + line : 257 + line, :], pltpu.roll(centre, 1, 0))
    above_z = jnp.where(sub == 7, ghosts[320 + line : 321 + line, :], pltpu.roll(centre, 7, 0))
    return centre, ((above_x + below_x) + (above_y + below_y)) + (above_z + below_z)


def start_kernel(device_ref, counts_ref, right_ref, neighbours_ref, residual, up, down, table):
    device = device_ref[0]
    own_count = counts_ref[device]
    lane = lax.broadcasted_iota(jnp.int32, (8, LANES), 1)
    live = lane < own_count
    for row in range(0, 512, 8):
        residual[row : row + 8, :] = jnp.where(live, right_ref[row : row + 8, :], 0.0)
    write_faces(residual, up, down)
    slot = neighbours_ref[...]
    present = slot >= 0
    slot = jnp.where(present, slot, 0)
    distance = jnp.abs(lax.shift_right_logical(slot, 7) - device)
    offset = slot & (LANES - 1)
    face = lax.broadcasted_iota(jnp.int32, (6, LANES), 0)
    skipped = jnp.maximum(counts_ref[jnp.maximum(device - 3, 0)] - TAIL, 0)
    shifted = jnp.where((distance == 3) & (face % 2 == 0), offset - skipped, offset)
    table[LANE_ROW : LANE_ROW + 6, :] = jnp.clip(shifted, 0, LANES - 1)
    table[WINDOW_ROW : WINDOW_ROW + 6, :] = jnp.where(present, distance, -1)
    forward = jnp.maximum(counts_ref[jnp.maximum(device - 1, 0)] - TAIL, 0)
    table[FORWARD_UP : FORWARD_UP + 8, :] = (lane & (TAIL - 1)) + forward
    table[FORWARD_DOWN : FORWARD_DOWN + 8, :] = lane & (TAIL - 1)


def pack_kernel(rows, forward_row, own, received, table, message):
    half = rows // 2
    lane = lax.broadcasted_iota(jnp.int32, (8, LANES), 1)
    forward = table[forward_row : forward_row + 8, :]
    message[0:rows, :] = own[...]
    for row in range(0, half, 8):
        first = take(received[row : row + 8, :], forward)
        second = take(received[half + row : half + row + 8, :], forward)
        message[rows + row : rows + row + 8, :] = jnp.where(lane < TAIL, first, second)


def smooth_kernel(residual, up, down, near_up, far_up, near_down, far_down, table, out, out_up, out_down, ghosts):
    read_ghosts(table, ((up, near_up, far_up), (down, near_down, far_down)), ghosts, FINE)
    for x in range(8):
        for y in range(8):
            centre, around = beside(residual, ghosts, x, y)
            first = RELAX_FINE * centre
            applied = 6.0 * first - RELAX_FINE * around
            at = 64 * x + 8 * y
            out[at : at + 8, :] = first + RELAX_FINE * (centre - applied)
    write_faces(out, out_up, out_down)


def defect_kernel(
    residual, second, up, down, near_up, far_up, near_down, far_down, table,
    defect, coarse, out_up, out_down, ghosts, sums, scaled,
):
    read_ghosts(table, ((up, near_up, far_up), (down, near_down, far_down)), ghosts, FINE)
    for big_x in range(4):
        for big_y in range(4):
            total = None
            for x in (2 * big_x, 2 * big_x + 1):
                for y in (2 * big_y, 2 * big_y + 1):
                    centre, around = beside(second, ghosts, x, y)
                    at = 64 * x + 8 * y
                    part = residual[at : at + 8, :] - (6.0 * centre - around)
                    defect[at : at + 8, :] = part
                    total = part if total is None else total + part
            at = 32 * big_x + 8 * big_y
            sums[at : at + 8, :] = total
    restricted = (sums[pl.ds(0, 64, stride=2), :] + sums[pl.ds(1, 64, stride=2), :]) * 0.125
    coarse[...] = restricted
    scaled[...] = RELAX_COARSE * restricted
    write_coarse_faces(scaled, out_up, out_down)


def coarse_kernel(
    coarse, up, down, near_up, far_up, near_down, far_down, table,
    out, out_up, out_down, ghosts, low_y, high_y, low_z, high_z,
):
    read_ghosts(table, ((up, near_up, far_up), (down, near_down, far_down)), ghosts, COARSE)
    for x in range(4):
        low_y[16 * x : 16 * x + 4, :] = ghosts[32 + 4 * x : 36 + 4 * x, :]
        high_y[16 * x + 12 : 16 * x + 16, :] = ghosts[48 + 4 * x : 52 + 4 * x, :]
    low_z[pl.ds(0, 16, stride=4), :] = ghosts[64:80, :]
    high_z[pl.ds(3, 16, stride=4), :] = ghosts[80:96, :]
    rhs = coarse[...]
    first = RELAX_COARSE * rhs
    row = lax.broadcasted_iota(jnp.int32, (64, LANES), 0)
    below_x = jnp.concatenate([ghosts[0:16, :], first[0:48, :]], axis=0)
    above_x = jnp.concatenate([first[16:64, :], ghosts[16:32, :]], axis=0)
    below_y = jnp.where((row & 15) < 4, low_y[...], pltpu.roll(first, 4, 0))
    above_y = jnp.where((row & 15) >= 12, high_y[...], pltpu.roll(first, 60, 0))
    below_z = jnp.where((row & 3) == 0, low_z[...], pltpu.roll(first, 1, 0))
    above_z = jnp.where((row & 3) == 3, high_z[...], pltpu.roll(first, 63, 0))
    around = ((above_x + below_x) + (above_y + below_y)) + (above_z + below_z)
    out[...] = first + RELAX_COARSE * (rhs - (6.0 * first - around) * 0.25)
    write_coarse_faces(out, out_up, out_down)


def correct_kernel(
    second, defect, coarse, up, down, near_up, far_up, near_down, far_down, table,
    out, out_up, out_down, ghosts, wide, wide_ghosts, spread,
):
    read_ghosts(table, ((up, near_up, far_up), (down, near_down, far_down)), ghosts, COARSE)
    wide[pl.ds(0, 64, stride=2), :] = coarse[...]
    wide[pl.ds(1, 64, stride=2), :] = coarse[...]
    wide_ghosts[pl.ds(0, 64, stride=2), :] = ghosts[0:64, :]
    wide_ghosts[pl.ds(1, 64, stride=2), :] = ghosts[0:64, :]
    for x in range(8):
        for y in range(8):
            at = 64 * x + 8 * y
            source = 32 * (x // 2) + 8 * (y // 2)
            spread[at : at + 8, :] = wide[source : source + 8, :]
    sub = lax.broadcasted_iota(jnp.int32, (8, LANES), 0)
    for x in range(8):
        for y in range(8):
            at = 64 * x + 8 * y
            cell = 4 * (x // 2) + y // 2
            centre = spread[at : at + 8, :]
            side_x = 8 * (y // 2)
            side_y = 8 * (x // 2)
            below_x = spread[at - 64 : at - 56, :] if x > 0 else wide_ghosts[side_x : side_x + 8, :]
            above_x = spread[at + 64 : at + 72, :] if x < 7 else wide_ghosts[32 + side_x : 40 + side_x, :]
            below_y = spread[at - 8 : at, :] if y > 0 else wide_ghosts[64 + side_y : 72 + side_y, :]
            above_y = spread[at + 8 : at + 16, :] if y < 7 else wide_ghosts[96 + side_y : 104 + side_y, :]
            below_z = jnp.where(sub == 0, ghosts[64 + cell : 65 + cell, :], pltpu.roll(centre, 1, 0))
            above_z = jnp.where(sub == 7, ghosts[80 + cell : 81 + cell, :], pltpu.roll(centre, 7, 0))
            around = ((above_x + below_x) + (above_y + below_y)) + (above_z + below_z)
            left = defect[at : at + 8, :] - (6.0 * centre - around)
            out[at : at + 8, :] = (second[at : at + 8, :] + centre) + RELAX_FINE * left
    write_faces(out, out_up, out_down)


def image_kernel(residual, direction, up, down, near_up, far_up, near_down, far_down, table, image, sums, ghosts):
    read_ghosts(table, ((up, near_up, far_up), (down, near_down, far_down)), ghosts, FINE)
    zero = jnp.zeros((8, LANES), jnp.float32)
    parts = [zero] * 5
    for x in range(8):
        for y in range(8):
            centre, around = beside(direction, ghosts, x, y)
            at = 64 * x + 8 * y
            applied = 6.0 * centre - around
            image[at : at + 8, :] = applied
            start = residual[at : at + 8, :]
            terms = (start * centre, centre * applied, start * start, start * applied, applied * applied)
            parts = [part + term for part, term in zip(parts, terms)]
    lane = lax.broadcasted_iota(jnp.int32, (1, LANES), 1)
    row = jnp.zeros((1, LANES), jnp.float32)
    for index, part in enumerate(parts):
        row = jnp.where(lane == index, jnp.sum(part), row)
    for copy in range(sums.shape[0]):
        sums[copy] = row


def add_kernel(received, out):
    total = received[0]
    for index in range(1, received.shape[0]):
        total = total + received[index]
    for copy in range(out.shape[0]):
        out[copy] = total


def finish_kernel(received, residual, direction, image, solution, left, norm):
    total = received[0]
    for index in range(1, received.shape[0]):
        total = total + received[index]
    lane = lax.broadcasted_iota(jnp.int32, (1, LANES), 1)
    along, curvature, old_square, cross_term, image_square = [
        jnp.full((8, LANES), jnp.sum(jnp.where(lane == index, total, 0.0)), jnp.float32) for index in range(5)
    ]
    step_size = along / curvature
    for row in range(0, 512, 8):
        solution[row : row + 8, :] = step_size * direction[row : row + 8, :]
        left[row : row + 8, :] = residual[row : row + 8, :] - step_size * image[row : row + 8, :]
    norm[...] = jnp.sqrt(old_square - 2.0 * step_size * cross_term + step_size * step_size * image_square)


def shift(block, distance):
    count = lax.axis_size(AXES)
    route = [(i, i + distance) for i in range(count) if 0 <= i + distance < count]
    return lax.ppermute(block, AXES, route)


def exchange(up, down, table, rows):
    near_up = shift(up, 1)
    near_down = shift(down, -1)
    message = [f32(rows + rows // 2, LANES)]
    (message_up,) = call(functools.partial(pack_kernel, rows, FORWARD_UP), "pack_up", message, up, near_up, table)
    far_up = shift(message_up, 2)
    (message_down,) = call(
        functools.partial(pack_kernel, rows, FORWARD_DOWN), "pack_down", message, down, near_down, table
    )
    far_down = shift(message_down, -2)
    return up, down, near_up, far_up, near_down, far_down, table


def local(right_side, counts, neighbours):
    device = lax.axis_index(AXES).astype(jnp.int32).reshape(1)
    fine = f32(512, LANES)
    faces = [f32(FINE, LANES)] * 2
    coarse = f32(64, LANES)
    coarse_faces = [f32(COARSE, LANES)] * 2
    fine_ghosts = pltpu.VMEM((2 * FINE, LANES), jnp.float32)
    coarse_ghosts = pltpu.VMEM((2 * COARSE, LANES), jnp.float32)
    scratch = lambda rows: pltpu.VMEM((rows, LANES), jnp.float32)

    residual_in, up, down, table = call(
        start_kernel, "start", [fine, *faces, i32(TABLE_ROWS, LANES)], device, counts, right_side, neighbours,
        in_specs=[SMEM, SMEM, VMEM, VMEM],
    )
    second, up, down = call(
        smooth_kernel, "smooth", [fine, *faces], residual_in, *exchange(up, down, table, FINE), scratch=[fine_ghosts]
    )
    defect, rhs, up, down = call(
        defect_kernel, "defect", [fine, coarse, *coarse_faces],
        residual_in, second, *exchange(up, down, table, FINE), scratch=[fine_ghosts, scratch(128), scratch(64)],
    )
    correction, up, down = call(
        coarse_kernel, "coarse", [coarse, *coarse_faces],
        rhs, *exchange(up, down, table, COARSE), scratch=[coarse_ghosts] + [scratch(64)] * 4,
    )
    direction, up, down = call(
        correct_kernel, "correct", [fine, *faces],
        second, defect, correction, *exchange(up, down, table, COARSE),
        scratch=[coarse_ghosts, scratch(128), scratch(128), scratch(512)],
    )
    image, sums = call(
        image_kernel, "image", [fine, f32(lax.axis_size("inner"), 1, LANES)],
        residual_in, direction, *exchange(up, down, table, FINE), scratch=[fine_ghosts],
    )
    received = lax.all_to_all(sums, "inner", 0, 0, tiled=True)
    (sums,) = call(add_kernel, "add", [f32(lax.axis_size("outer"), 1, LANES)], received)
    received = lax.all_to_all(sums, "outer", 0, 0, tiled=True)
    solved, left, norm = call(
        finish_kernel, "finish", [fine, fine, f32(8, LANES)], received, residual_in, direction, image
    )
    return solved, left, norm[0, 0]


def solution(mesh):
    devices = mesh.devices.reshape(-1, GROUP)
    split = Mesh(devices, AXES)
    return jax.shard_map(
        local,
        mesh=split,
        in_specs=(P(None, AXES), P(), P(None, AXES)),
        out_specs=(P(None, AXES), P(None, AXES), P()),
        check_vma=False,
    )
```

time: 307 us -> 217 us (0.71); the launches traced: 302 us -> 216 us
  blocking collectives: 110 us -> 69.4 us
  local copies, waits for them, and re-layouts: 50.7 us -> 10.6 us
  Pallas kernels: 0 us -> 32.6 us
  starting transfers between devices: 102 us -> 74.5 us
  between operations: 8.55 us -> 0.97 us
  other arithmetic: 7.15 us -> 0 us
  waiting for transfers between devices: 24.6 us -> 27.9 us
    psum x4 -> x0, blocking collectives: 110 us -> none  [one_axis_at_a_time(): return functools.reduce(lax.psum, axes, x)]
    all_to_all x0 -> x2, blocking collectives: none -> 69.4 us  [the longest x1 55.6 us: local(): received = lax.all_to_all(sums, 'outer', 0, 0, tiled=True)]
    pallas_call x0 -> x18, Pallas kernels: none -> 32.6 us  [call(): pl.pallas_call(kernel, out_shape=outs, in_specs=in_specs or [VMEM] * len(...]
    gather x33 -> x0, local copies, waits for them, and re-layouts: 32.2 us -> none  [the longest x30 19.5 us: exchange(): picked = jnp.take(lookup, position[face_id], axis=1)]
    ppermute x30 -> x20, starting transfers between devices: 102 us -> 74.5 us  [shift(): return lax.ppermute(block, AXES, route)]
    unnamed x36 -> x40, local copies, waits for them, and re-layouts: 5.24 us -> 9.43 us
    scatter x30 -> x0, local copies, waits for them, and re-layouts: 4.06 us -> none  [the longest x5 0.7 us: apply_operator(): padded = padded.at[1:-1, 0, 1:-1].set(shaped[2])]
    ppermute x30 -> x20, waiting for transfers between devices: 24.6 us -> 27.9 us  [shift(): return lax.ppermute(block, AXES, route)]
  transfers between devices with their start and end apart: 30 -> 20, of which waited for: 19 -> 11; matrix products, arithmetic and copies ran while one was open for 9% -> 0% of each run, Pallas kernels for 0% -> 7%
where the time goes in v1:
time: 217 us; the launch traced here: 216 us
  starting transfers between devices  74.5 us (34%)
  blocking collectives  69.4 us (32%)
  Pallas kernels  32.6 us (15%)
  waiting for transfers between devices  27.9 us (13%)
  local copies, waits for them, and re-layouts  10.6 us (5%)
    ppermute x20, starting transfers between devices, shift(): return lax.ppermute(block, AXES, route)  74.5 us
    all_to_all x1, blocking collectives, local(): received = lax.all_to_all(sums, 'outer', 0, 0, tiled=True)  55.6 us
    pallas_call x18, Pallas kernels, call(): pl.pallas_call(kernel, out_shape=outs, in_specs=in_specs or [VMEM] * len(...  32.6 us
    ppermute x20, waiting for transfers between devices, shift(): return lax.ppermute(block, AXES, route)  27.9 us
    all_to_all x1, blocking collectives, local(): received = lax.all_to_all(sums, 'inner', 0, 0, tiled=True)  13.8 us
    unnamed x40, local copies, waits for them, and re-layouts  9.43 us
  transfers between devices with their start and end apart: 20, of which 11 were waited for; matrix products, arithmetic and copies ran while one was open for 0% of the time, Pallas kernels for 7%

profile of v1, /device:TPU:1, one launch (start us, length us, event | category | flops | bytes accessed | tf_op | source)
XLA Modules:
  0.0 216.1 jit_solution(5694572177580322983)
XLA Ops:
  2.4 4.0 %collective-permute-start = (f32[192,128]{1,0:T(8,128)}, f32[192,128]{1,0:T(8,128)S(1)}, u32[]{:S(2)}, u32[]{:S(2)}) collective-permute-start(f32[192,128]{1,0:T(8,128)} %get-tuple-element.26.own.up), channel_id=1, source_target_pairs={{0,1},{1,2},{2,3},{3,4},{4,5},{5,6},{6,7},{7,8},{8,9},{9,10},{10,1... | collective-permute-start | bytes 294920 | tf_op jit(solution)/shard_map/ppermute | solution.py:282
  6.5 4.4 %collective-permute-start.2 = (f32[192,128]{1,0:T(8,128)}, f32[192,128]{1,0:T(8,128)S(1)}, u32[]{:S(2)}, u32[]{:S(2)}) collective-permute-start(f32[192,128]{1,0:T(8,128)} %get-tuple-element.27.own.down), channel_id=1, source_target_pairs={{1,0},{2,1},{3,2},{4,3},{5,4},{6,5},{7,6},{8,7},{9,8},{10,9},{11,1... | collective-permute-start | bytes 294920 | tf_op jit(solution)/shard_map/ppermute | solution.py:282
  18.9 5.7 %collective-permute-start.3 = (f32[288,128]{1,0:T(8,128)}, f32[288,128]{1,0:T(8,128)S(1)}, u32[]{:S(2)}, u32[]{:S(2)}) collective-permute-start(f32[288,128]{1,0:T(8,128)} %pack_down.5), channel_id=1, source_target_pairs={{2,0},{3,1},{4,2},{5,3},{6,4},{7,5},{8,6},{9,7},{10,8},{11,9},{12,... | collective-permute-start | bytes 442376 | tf_op jit(solution)/shard_map/ppermute | solution.py:282
  28.7 2.5 %smooth.1 = (f32[512,128]{1,0:T(8,128)}, f32[192,128]{1,0:T(8,128)}, f32[192,128]{1,0:T(8,128)}) custom-call(f32[512,128]{1,0:T(8,128)} %get-tuple-element.25.residual, f32[192,128]{1,0:T(8,128)} %get-tuple-element.26.own.up, f32[192,128]{1,0:T(8,128)} %get-tuple-element.27.own.down, f32[192,128]{1,0:T(8,128)} %copy-done.1, f32[288,128]{1,0:T(8,128)} %copy-done.10, ...), custom_call_target="tpu_custom_call" | custom-call | tf_op jit(solution)/shard_map/smooth/pallas_call | solution.py:39
  33.2 4.9 %collective-permute-start.6 = (f32[192,128]{1,0:T(8,128)}, f32[192,128]{1,0:T(8,128)S(1)}, u32[]{:S(2)}, u32[]{:S(2)}) collective-permute-start(f32[192,128]{1,0:T(8,128)} %get-tuple-element.31.own.down), channel_id=1, source_target_pairs={{1,0},{2,1},{3,2},{4,3},{5,4},{6,5},{7,6},{8,7},{9,8},{10,9},{11,1... | collective-permute-start | bytes 294920 | tf_op jit(solution)/shard_map/ppermute | solution.py:282
  40.9 4.3 %collective-permute-start.5 = (f32[288,128]{1,0:T(8,128)}, f32[288,128]{1,0:T(8,128)S(1)}, u32[]{:S(2)}, u32[]{:S(2)}) collective-permute-start(f32[288,128]{1,0:T(8,128)} %pack_up.6), channel_id=1, source_target_pairs={{0,2},{1,3},{2,4},{3,5},{4,6},{5,7},{6,8},{7,9},{8,10},{9,11},{10,... | collective-permute-start | bytes 442376 | tf_op jit(solution)/shard_map/ppermute | solution.py:282
  47.6 3.3 %collective-permute-start.7 = (f32[288,128]{1,0:T(8,128)}, f32[288,128]{1,0:T(8,128)S(1)}, u32[]{:S(2)}, u32[]{:S(2)}) collective-permute-start(f32[288,128]{1,0:T(8,128)} %pack_down.6), channel_id=1, source_target_pairs={{2,0},{3,1},{4,2},{5,3},{6,4},{7,5},{8,6},{9,7},{10,8},{11,9},{12,... | collective-permute-start | bytes 442376 | tf_op jit(solution)/shard_map/ppermute | solution.py:282
  52.1 5.6 %collective-permute-done.7.far_down = f32[288,128]{1,0:T(8,128)S(1)} collective-permute-done((f32[288,128]{1,0:T(8,128)}, f32[288,128]{1,0:T(8,128)S(1)}, u32[]{:S(2)}, u32[]{:S(2)}) %collective-permute-start.7) | collective-permute-done | bytes 147488 | tf_op jit(solution)/shard_map/ppermute | solution.py:282
  58.4 2.5 %defect.1 = (f32[512,128]{1,0:T(8,128)}, f32[64,128]{1,0:T(8,128)}, f32[48,128]{1,0:T(8,128)}, f32[48,128]{1,0:T(8,128)}) custom-call(f32[512,128]{1,0:T(8,128)} %get-tuple-element.25.residual, f32[512,128]{1,0:T(8,128)} %get-tuple-element.29.second, f32[192,128]{1,0:T(8,128)} %get-tuple-element.30.own.up, f32[192,128]{1,0:T(8,128)} %get-tuple-element.31.own.down, ...), custom_call_target="tpu_custom_call" | custom-call | tf_op jit(solution)/shard_map/defect/pallas_call | solution.py:39
  62.8 4.9 %collective-permute-start.10 = (f32[48,128]{1,0:T(8,128)}, f32[48,128]{1,0:T(8,128)S(1)}, u32[]{:S(2)}, u32[]{:S(2)}) collective-permute-start(f32[48,128]{1,0:T(8,128)} %get-tuple-element.35.own.down), channel_id=1, source_target_pairs={{1,0},{2,1},{3,2},{4,3},{5,4},{6,5},{7,6},{8,7},{9,8},{10,9},{11,1... | collective-permute-start | bytes 73736 | tf_op jit(solution)/shard_map/ppermute | solution.py:282
  69.7 6.0 %collective-permute-start.9 = (f32[72,128]{1,0:T(8,128)}, f32[72,128]{1,0:T(8,128)S(1)}, u32[]{:S(2)}, u32[]{:S(2)}) collective-permute-start(f32[72,128]{1,0:T(8,128)} %pack_up.7), channel_id=1, source_target_pairs={{0,2},{1,3},{2,4},{3,5},{4,6},{5,7},{6,8},{7,9},{8,10},{9,11},{10,... | collective-permute-start | bytes 110600 | tf_op jit(solution)/shard_map/ppermute | solution.py:282
  79.7 4.4 %collective-permute-done.11.far_down = f32[72,128]{1,0:T(8,128)S(1)} collective-permute-done((f32[72,128]{1,0:T(8,128)}, f32[72,128]{1,0:T(8,128)S(1)}, u32[]{:S(2)}, u32[]{:S(2)}) %collective-permute-start.11) | collective-permute-done | bytes 36896 | tf_op jit(solution)/shard_map/ppermute | solution.py:282
  86.4 2.5 %collective-permute-start.12 = (f32[48,128]{1,0:T(8,128)}, f32[48,128]{1,0:T(8,128)S(1)}, u32[]{:S(2)}, u32[]{:S(2)}) collective-permute-start(f32[48,128]{1,0:T(8,128)} %get-tuple-element.37.own.up), channel_id=1, source_target_pairs={{0,1},{1,2},{2,3},{3,4},{4,5},{5,6},{6,7},{7,8},{8,9},{9,10},{10,1... | collective-permute-start | bytes 73736 | tf_op jit(solution)/shard_map/ppermute | solution.py:282
  88.9 4.5 %collective-permute-start.14 = (f32[48,128]{1,0:T(8,128)}, f32[48,128]{1,0:T(8,128)S(1)}, u32[]{:S(2)}, u32[]{:S(2)}) collective-permute-start(f32[48,128]{1,0:T(8,128)} %get-tuple-element.38.own.down), channel_id=1, source_target_pairs={{1,0},{2,1},{3,2},{4,3},{5,4},{6,5},{7,6},{8,7},{9,8},{10,9},{11,1... | collective-permute-start | bytes 73736 | tf_op jit(solution)/shard_map/ppermute | solution.py:282
  95.5 4.0 %collective-permute-start.13 = (f32[72,128]{1,0:T(8,128)}, f32[72,128]{1,0:T(8,128)S(1)}, u32[]{:S(2)}, u32[]{:S(2)}) collective-permute-start(f32[72,128]{1,0:T(8,128)} %pack_up.8), channel_id=1, source_target_pairs={{0,2},{1,3},{2,4},{3,5},{4,6},{5,7},{6,8},{7,9},{8,10},{9,11},{10,... | collective-permute-start | bytes 110600 | tf_op jit(solution)/shard_map/ppermute | solution.py:282
  101.6 3.6 %collective-permute-start.15 = (f32[72,128]{1,0:T(8,128)}, f32[72,128]{1,0:T(8,128)S(1)}, u32[]{:S(2)}, u32[]{:S(2)}) collective-permute-start(f32[72,128]{1,0:T(8,128)} %pack_down.8), channel_id=1, source_target_pairs={{2,0},{3,1},{4,2},{5,3},{6,4},{7,5},{8,6},{9,7},{10,8},{11,9},{12,... | collective-permute-start | bytes 110600 | tf_op jit(solution)/shard_map/ppermute | solution.py:282
  110.1 3.9 %collective-permute-start.16 = (f32[192,128]{1,0:T(8,128)}, f32[192,128]{1,0:T(8,128)S(1)}, u32[]{:S(2)}, u32[]{:S(2)}) collective-permute-start(f32[192,128]{1,0:T(8,128)} %get-tuple-element.40.own.up), channel_id=1, source_target_pairs={{0,1},{1,2},{2,3},{3,4},{4,5},{5,6},{6,7},{7,8},{8,9},{9,10},{10,1... | collective-permute-start | bytes 294920 | tf_op jit(solution)/shard_map/ppermute | solution.py:282
  114.1 3.3 %collective-permute-start.18 = (f32[192,128]{1,0:T(8,128)}, f32[192,128]{1,0:T(8,128)S(1)}, u32[]{:S(2)}, u32[]{:S(2)}) collective-permute-start(f32[192,128]{1,0:T(8,128)} %get-tuple-element.41.own.down), channel_id=1, source_target_pairs={{1,0},{2,1},{3,2},{4,3},{5,4},{6,5},{7,6},{8,7},{9,8},{10,9},{11,1... | collective-permute-start | bytes 294920 | tf_op jit(solution)/shard_map/ppermute | solution.py:282
  120.2 3.6 %collective-permute-start.17 = (f32[288,128]{1,0:T(8,128)}, f32[288,128]{1,0:T(8,128)S(1)}, u32[]{:S(2)}, u32[]{:S(2)}) collective-permute-start(f32[288,128]{1,0:T(8,128)} %pack_up.9), channel_id=1, source_target_pairs={{0,2},{1,3},{2,4},{3,5},{4,6},{5,7},{6,8},{7,9},{8,10},{9,11},{10,... | collective-permute-start | bytes 442376 | tf_op jit(solution)/shard_map/ppermute | solution.py:282
  126.2 4.0 %collective-permute-start.19 = (f32[288,128]{1,0:T(8,128)}, f32[288,128]{1,0:T(8,128)S(1)}, u32[]{:S(2)}, u32[]{:S(2)}) collective-permute-start(f32[288,128]{1,0:T(8,128)} %pack_down.9), channel_id=1, source_target_pairs={{2,0},{3,1},{4,2},{5,3},{6,4},{7,5},{8,6},{9,7},{10,8},{11,9},{12,... | collective-permute-start | bytes 442376 | tf_op jit(solution)/shard_map/ppermute | solution.py:282
  130.7 8.1 %collective-permute-done.19.far_down = f32[288,128]{1,0:T(8,128)S(1)} collective-permute-done((f32[288,128]{1,0:T(8,128)}, f32[288,128]{1,0:T(8,128)S(1)}, u32[]{:S(2)}, u32[]{:S(2)}) %collective-permute-start.19) | collective-permute-done | bytes 147488 | tf_op jit(solution)/shard_map/ppermute | solution.py:282
  139.4 2.5 %image.1 = (f32[512,128]{1,0:T(8,128)}, f32[16,1,128]{2,1,0:T(1,128)}) custom-call(f32[512,128]{1,0:T(8,128)} %get-tuple-element.25.residual, f32[512,128]{1,0:T(8,128)} %get-tuple-element.39.direction, f32[192,128]{1,0:T(8,128)} %get-tuple-element.40.own.up, f32[192,128]{1,0:T(8,128)} %get-tuple-element.41.own.down, f32[192,128]{1,0:T(8,128)} %copy-done.2, ...), custom_call_target="tpu_custom_call" | custom-call | tf_op jit(solution)/shard_map/image/pallas_call | solution.py:39
  142.0 13.8 %all_to_all.10.received = f32[16,1,128]{2,1,0:T(1,128)} all-to-all(f32[16,1,128]{2,1,0:T(1,128)} %get-tuple-element.42), channel_id=1, replica_groups=mesh['curve'=96,'level'=8] {'curve':(48)2,'level'}, dimensions={0} | all-to-all | bytes 16384 | tf_op jit(solution)/shard_map/all_to_all | solution.py:332
  157.1 55.6 %all_to_all.11.received = f32[48,1,128]{2,1,0:T(1,128)} all-to-all(f32[48,1,128]{2,1,0:T(1,128)} %add.5), channel_id=1, replica_groups=mesh['curve'=96,'level'=8] {'curve':(1)48}, dimensions={0} | all-to-all | bytes 49152 | tf_op jit(solution)/shard_map/all_to_all | solution.py:334
  (77 shorter events, 53.0 us)
Async XLA Ops:
  2.4 9.9 %collective-permute-start = (f32[192,128]{1,0:T(8,128)}, f32[192,128]{1,0:T(8,128)S(1)}, u32[]{:S(2)}, u32[]{:S(2)}) collective-permute-start(f32[192,128]{1,0:T(8,128)} %get-tuple-element.26.own.up), channel_id=1, source_target_pairs={{0,1},{1,2},{2,3},{3,4},{4,5},{5,6},{6,7},{7,8},{8,9},{9,10},{10,1... | collective-permute-start | bytes 294920 | tf_op jit(solution)/shard_map/ppermute | solution.py:282
  6.5 10.1 %collective-permute-start.2 = (f32[192,128]{1,0:T(8,128)}, f32[192,128]{1,0:T(8,128)S(1)}, u32[]{:S(2)}, u32[]{:S(2)}) collective-permute-start(f32[192,128]{1,0:T(8,128)} %get-tuple-element.27.own.down), channel_id=1, source_target_pairs={{1,0},{2,1},{3,2},{4,3},{5,4},{6,5},{7,6},{8,7},{9,8},{10,9},{11,1... | collective-permute-start | bytes 294920 | tf_op jit(solution)/shard_map/ppermute | solution.py:282
  14.7 11.4 %collective-permute-start.1 = (f32[288,128]{1,0:T(8,128)}, f32[288,128]{1,0:T(8,128)S(1)}, u32[]{:S(2)}, u32[]{:S(2)}) collective-permute-start(f32[288,128]{1,0:T(8,128)} %pack_up.5), channel_id=1, source_target_pairs={{0,2},{1,3},{2,4},{3,5},{4,6},{5,7},{6,8},{7,9},{8,10},{9,11},{10,... | collective-permute-start | bytes 442376 | tf_op jit(solution)/shard_map/ppermute | solution.py:282
  18.9 9.1 %collective-permute-start.3 = (f32[288,128]{1,0:T(8,128)}, f32[288,128]{1,0:T(8,128)S(1)}, u32[]{:S(2)}, u32[]{:S(2)}) collective-permute-start(f32[288,128]{1,0:T(8,128)} %pack_down.5), channel_id=1, source_target_pairs={{2,0},{3,1},{4,2},{5,3},{6,4},{7,5},{8,6},{9,7},{10,8},{11,9},{12,... | collective-permute-start | bytes 442376 | tf_op jit(solution)/shard_map/ppermute | solution.py:282
  31.2 7.3 %collective-permute-start.4 = (f32[192,128]{1,0:T(8,128)}, f32[192,128]{1,0:T(8,128)S(1)}, u32[]{:S(2)}, u32[]{:S(2)}) collective-permute-start(f32[192,128]{1,0:T(8,128)} %get-tuple-element.30.own.up), channel_id=1, source_target_pairs={{0,1},{1,2},{2,3},{3,4},{4,5},{5,6},{6,7},{7,8},{8,9},{9,10},{10,1... | collective-permute-start | bytes 294920 | tf_op jit(solution)/shard_map/ppermute | solution.py:282
  33.2 12.1 %collective-permute-start.6 = (f32[192,128]{1,0:T(8,128)}, f32[192,128]{1,0:T(8,128)S(1)}, u32[]{:S(2)}, u32[]{:S(2)}) collective-permute-start(f32[192,128]{1,0:T(8,128)} %get-tuple-element.31.own.down), channel_id=1, source_target_pairs={{1,0},{2,1},{3,2},{4,3},{5,4},{6,5},{7,6},{8,7},{9,8},{10,9},{11,1... | collective-permute-start | bytes 294920 | tf_op jit(solution)/shard_map/ppermute | solution.py:282
  40.9 11.1 %collective-permute-start.5 = (f32[288,128]{1,0:T(8,128)}, f32[288,128]{1,0:T(8,128)S(1)}, u32[]{:S(2)}, u32[]{:S(2)}) collective-permute-start(f32[288,128]{1,0:T(8,128)} %pack_up.6), channel_id=1, source_target_pairs={{0,2},{1,3},{2,4},{3,5},{4,6},{5,7},{6,8},{7,9},{8,10},{9,11},{10,... | collective-permute-start | bytes 442376 | tf_op jit(solution)/shard_map/ppermute | solution.py:282
  47.6 10.1 %collective-permute-start.7 = (f32[288,128]{1,0:T(8,128)}, f32[288,128]{1,0:T(8,128)S(1)}, u32[]{:S(2)}, u32[]{:S(2)}) collective-permute-start(f32[288,128]{1,0:T(8,128)} %pack_down.6), channel_id=1, source_target_pairs={{2,0},{3,1},{4,2},{5,3},{6,4},{7,5},{8,6},{9,7},{10,8},{11,9},{12,... | collective-permute-start | bytes 442376 | tf_op jit(solution)/shard_map/ppermute | solution.py:282
  52.1 5.6 %copy-start.6 = (f32[288,128]{1,0:T(8,128)}, f32[288,128]{1,0:T(8,128)S(1)}, u32[]{:S(2)}) copy-start(f32[288,128]{1,0:T(8,128)S(1)} %collective-permute-done.5.far_up) | copy-start | bytes 442372
  60.9 6.8 %collective-permute-start.8 = (f32[48,128]{1,0:T(8,128)}, f32[48,128]{1,0:T(8,128)S(1)}, u32[]{:S(2)}, u32[]{:S(2)}) collective-permute-start(f32[48,128]{1,0:T(8,128)} %get-tuple-element.34.own.up), channel_id=1, source_target_pairs={{0,1},{1,2},{2,3},{3,4},{4,5},{5,6},{6,7},{7,8},{8,9},{9,10},{10,1... | collective-permute-start | bytes 73736 | tf_op jit(solution)/shard_map/ppermute | solution.py:282
  62.8 12.9 %collective-permute-start.10 = (f32[48,128]{1,0:T(8,128)}, f32[48,128]{1,0:T(8,128)S(1)}, u32[]{:S(2)}, u32[]{:S(2)}) collective-permute-start(f32[48,128]{1,0:T(8,128)} %get-tuple-element.35.own.down), channel_id=1, source_target_pairs={{1,0},{2,1},{3,2},{4,3},{5,4},{6,5},{7,6},{8,7},{9,8},{10,9},{11,1... | collective-permute-start | bytes 73736 | tf_op jit(solution)/shard_map/ppermute | solution.py:282
  69.7 10.0 %collective-permute-start.9 = (f32[72,128]{1,0:T(8,128)}, f32[72,128]{1,0:T(8,128)S(1)}, u32[]{:S(2)}, u32[]{:S(2)}) collective-permute-start(f32[72,128]{1,0:T(8,128)} %pack_up.7), channel_id=1, source_target_pairs={{0,2},{1,3},{2,4},{3,5},{4,6},{5,7},{6,8},{7,9},{8,10},{9,11},{10,... | collective-permute-start | bytes 110600 | tf_op jit(solution)/shard_map/ppermute | solution.py:282
  77.8 6.3 %collective-permute-start.11 = (f32[72,128]{1,0:T(8,128)}, f32[72,128]{1,0:T(8,128)S(1)}, u32[]{:S(2)}, u32[]{:S(2)}) collective-permute-start(f32[72,128]{1,0:T(8,128)} %pack_down.7), channel_id=1, source_target_pairs={{2,0},{3,1},{4,2},{5,3},{6,4},{7,5},{8,6},{9,7},{10,8},{11,9},{12,... | collective-permute-start | bytes 110600 | tf_op jit(solution)/shard_map/ppermute | solution.py:282
  79.7 4.4 %copy-start.18 = (f32[72,128]{1,0:T(8,128)}, f32[72,128]{1,0:T(8,128)S(1)}, u32[]{:S(2)}) copy-start(f32[72,128]{1,0:T(8,128)S(1)} %collective-permute-done.9.far_up) | copy-start | bytes 110596
  86.4 7.0 %collective-permute-start.12 = (f32[48,128]{1,0:T(8,128)}, f32[48,128]{1,0:T(8,128)S(1)}, u32[]{:S(2)}, u32[]{:S(2)}) collective-permute-start(f32[48,128]{1,0:T(8,128)} %get-tuple-element.37.own.up), channel_id=1, source_target_pairs={{0,1},{1,2},{2,3},{3,4},{4,5},{5,6},{6,7},{7,8},{8,9},{9,10},{10,1... | collective-permute-start | bytes 73736 | tf_op jit(solution)/shard_map/ppermute | solution.py:282
  88.9 10.6 %collective-permute-start.14 = (f32[48,128]{1,0:T(8,128)}, f32[48,128]{1,0:T(8,128)S(1)}, u32[]{:S(2)}, u32[]{:S(2)}) collective-permute-start(f32[48,128]{1,0:T(8,128)} %get-tuple-element.38.own.down), channel_id=1, source_target_pairs={{1,0},{2,1},{3,2},{4,3},{5,4},{6,5},{7,6},{8,7},{9,8},{10,9},{11,1... | collective-permute-start | bytes 73736 | tf_op jit(solution)/shard_map/ppermute | solution.py:282
  95.5 9.7 %collective-permute-start.13 = (f32[72,128]{1,0:T(8,128)}, f32[72,128]{1,0:T(8,128)S(1)}, u32[]{:S(2)}, u32[]{:S(2)}) collective-permute-start(f32[72,128]{1,0:T(8,128)} %pack_up.8), channel_id=1, source_target_pairs={{0,2},{1,3},{2,4},{3,5},{4,6},{5,7},{6,8},{7,9},{8,10},{9,11},{10,... | collective-permute-start | bytes 110600 | tf_op jit(solution)/shard_map/ppermute | solution.py:282
  101.6 5.8 %collective-permute-start.15 = (f32[72,128]{1,0:T(8,128)}, f32[72,128]{1,0:T(8,128)S(1)}, u32[]{:S(2)}, u32[]{:S(2)}) collective-permute-start(f32[72,128]{1,0:T(8,128)} %pack_down.8), channel_id=1, source_target_pairs={{2,0},{3,1},{4,2},{5,3},{6,4},{7,5},{8,6},{9,7},{10,8},{11,9},{12,... | collective-permute-start | bytes 110600 | tf_op jit(solution)/shard_map/ppermute | solution.py:282
  105.2 2.2 %copy-start.16 = (f32[72,128]{1,0:T(8,128)}, f32[72,128]{1,0:T(8,128)S(1)}, u32[]{:S(2)}) copy-start(f32[72,128]{1,0:T(8,128)S(1)} %collective-permute-done.13.far_up) | copy-start | bytes 110596
  110.1 7.8 %collective-permute-start.16 = (f32[192,128]{1,0:T(8,128)}, f32[192,128]{1,0:T(8,128)S(1)}, u32[]{:S(2)}, u32[]{:S(2)}) collective-permute-start(f32[192,128]{1,0:T(8,128)} %get-tuple-element.40.own.up), channel_id=1, source_target_pairs={{0,1},{1,2},{2,3},{3,4},{4,5},{5,6},{6,7},{7,8},{8,9},{9,10},{10,1... | collective-permute-start | bytes 294920 | tf_op jit(solution)/shard_map/ppermute | solution.py:282
  114.1 9.8 %collective-permute-start.18 = (f32[192,128]{1,0:T(8,128)}, f32[192,128]{1,0:T(8,128)S(1)}, u32[]{:S(2)}, u32[]{:S(2)}) collective-permute-start(f32[192,128]{1,0:T(8,128)} %get-tuple-element.41.own.down), channel_id=1, source_target_pairs={{1,0},{2,1},{3,2},{4,3},{5,4},{6,5},{7,6},{8,7},{9,8},{10,9},{11,1... | collective-permute-start | bytes 294920 | tf_op jit(solution)/shard_map/ppermute | solution.py:282
  120.2 10.4 %collective-permute-start.17 = (f32[288,128]{1,0:T(8,128)}, f32[288,128]{1,0:T(8,128)S(1)}, u32[]{:S(2)}, u32[]{:S(2)}) collective-permute-start(f32[288,128]{1,0:T(8,128)} %pack_up.9), channel_id=1, source_target_pairs={{0,2},{1,3},{2,4},{3,5},{4,6},{5,7},{6,8},{7,9},{8,10},{9,11},{10,... | collective-permute-start | bytes 442376 | tf_op jit(solution)/shard_map/ppermute | solution.py:282
  126.2 12.6 %collective-permute-start.19 = (f32[288,128]{1,0:T(8,128)}, f32[288,128]{1,0:T(8,128)S(1)}, u32[]{:S(2)}, u32[]{:S(2)}) collective-permute-start(f32[288,128]{1,0:T(8,128)} %pack_down.9), channel_id=1, source_target_pairs={{2,0},{3,1},{4,2},{5,3},{6,4},{7,5},{8,6},{9,7},{10,8},{11,9},{12,... | collective-permute-start | bytes 442376 | tf_op jit(solution)/shard_map/ppermute | solution.py:282
  130.7 8.1 %copy-start.7 = (f32[288,128]{1,0:T(8,128)}, f32[288,128]{1,0:T(8,128)S(1)}, u32[]{:S(2)}) copy-start(f32[288,128]{1,0:T(8,128)S(1)} %collective-permute-done.17.far_up) | copy-start | bytes 442372
  (16 other events, 11.5 us)

commit v2 on v1

--- a/solution.py
+++ b/solution.py
@@ -13,6 +13,7 @@
 FINE = 192
 COARSE = 48
 GROUP = 16
+GRANT = 8 * 1024 * 1024
 AXES = ("outer", "inner")
 RELAX_FINE = (2.0 / 3.0) / 6.0
 RELAX_COARSE = (2.0 / 3.0) / 1.5
@@ -24,7 +25,9 @@
 WINDOW_ROW = 8
 FORWARD_UP = 16
 FORWARD_DOWN = 24
-TABLE_ROWS = 32
+UPPER_NEAR = 32
+UPPER_FAR = 40
+TABLE_ROWS = 48
 
 
 def f32(*shape):
@@ -42,12 +45,30 @@
         in_specs=in_specs or [VMEM] * len(args),
         out_specs=out_specs or [VMEM] * len(outs),
         scratch_shapes=list(scratch),
+        compiler_params=pltpu.CompilerParams(vmem_limit_bytes=GRANT),
         name=name,
     )(*args)
 
 
 def take(block, lanes):
     return jnp.take_along_axis(block, lanes, axis=1, mode="promise_in_bounds")
+
+
+class Chosen:
+    def __init__(self, flag, if_set, if_clear):
+        self.flag, self.if_set, self.if_clear = flag, if_set, if_clear
+
+    def __getitem__(self, at):
+        return jnp.where(self.flag, self.if_set[at], self.if_clear[at])
+
+
+def write_pair(table, flag_row, up, down, inner, outer, rows):
+    upper = table[flag_row : flag_row + 8, :] > 0
+    for row in range(0, rows, 8):
+        high = up[row : row + 8, :]
+        low = down[row : row + 8, :]
+        inner[row : row + 8, :] = jnp.where(upper, low, high)
+        outer[row : row + 8, :] = jnp.where(upper, high, low)
 
 
 def write_faces(values, up, down):
@@ -70,7 +91,17 @@
     down[32:48, :] = values[pl.ds(0, 16, stride=4), :]
 
 
-def read_ghosts(table, windows, ghosts, rows):
+def windows_of(table, up, down, near_inner, near_outer, far_inner, far_outer):
+    near = table[UPPER_NEAR : UPPER_NEAR + 8, :] > 0
+    far = table[UPPER_FAR : UPPER_FAR + 8, :] > 0
+    return (
+        (up, Chosen(near, near_inner, near_outer), Chosen(far, far_inner, far_outer)),
+        (down, Chosen(near, near_outer, near_inner), Chosen(far, far_outer, far_inner)),
+    )
+
+
+def read_ghosts(table, faces, ghosts, rows):
+    windows = windows_of(table, *faces)
     per_face = rows // 3
     packed = rows // 2
     for face in range(6):
@@ -105,7 +136,7 @@
     return centre, ((above_x + below_x) + (above_y + below_y)) + (above_z + below_z)
 
 
-def start_kernel(device_ref, counts_ref, right_ref, neighbours_ref, residual, up, down, table):
+def start_kernel(device_ref, counts_ref, right_ref, neighbours_ref, residual, up, down, inner, outer, table):
     device = device_ref[0]
     own_count = counts_ref[device]
     lane = lax.broadcasted_iota(jnp.int32, (8, LANES), 1)
@@ -113,6 +144,9 @@
     for row in range(0, 512, 8):
         residual[row : row + 8, :] = jnp.where(live, right_ref[row : row + 8, :], 0.0)
     write_faces(residual, up, down)
+    table[UPPER_NEAR : UPPER_NEAR + 8, :] = jnp.full((8, LANES), device & 1, jnp.int32)
+    table[UPPER_FAR : UPPER_FAR + 8, :] = jnp.full((8, LANES), device & 2, jnp.int32)
+    write_pair(table, UPPER_NEAR, up, down, inner, outer, FINE)
     slot = neighbours_ref[...]
     present = slot >= 0
     slot = jnp.where(present, slot, 0)
@@ -128,19 +162,32 @@
     table[FORWARD_DOWN : FORWARD_DOWN + 8, :] = lane & (TAIL - 1)
 
 
-def pack_kernel(rows, forward_row, own, received, table, message):
+def pack_kernel(rows, up, down, near_inner, near_outer, table, inner, outer):
     half = rows // 2
     lane = lax.broadcasted_iota(jnp.int32, (8, LANES), 1)
-    forward = table[forward_row : forward_row + 8, :]
-    message[0:rows, :] = own[...]
+    write_pair(table, UPPER_FAR, up, down, inner, outer, rows)
+    near = table[UPPER_NEAR : UPPER_NEAR + 8, :] > 0
+    upper = table[UPPER_FAR : UPPER_FAR + 8, :] > 0
+    near_up = Chosen(near, near_inner, near_outer)
+    near_down = Chosen(near, near_outer, near_inner)
+
+    def packed(block, lanes, row):
+        first = take(block[row : row + 8, :], lanes)
+        second = take(block[half + row : half + row + 8, :], lanes)
+        return jnp.where(lane < TAIL, first, second)
+
+    lanes_up = table[FORWARD_UP : FORWARD_UP + 8, :]
+    lanes_down = table[FORWARD_DOWN : FORWARD_DOWN + 8, :]
     for row in range(0, half, 8):
-        first = take(received[row : row + 8, :], forward)
-        second = take(received[half + row : half + row + 8, :], forward)
-        message[rows + row : rows + row + 8, :] = jnp.where(lane < TAIL, first, second)
-
-
-def smooth_kernel(residual, up, down, near_up, far_up, near_down, far_down, table, out, out_up, out_down, ghosts):
-    read_ghosts(table, ((up, near_up, far_up), (down, near_down, far_down)), ghosts, FINE)
+        high = packed(near_up, lanes_up, row)
+        low = packed(near_down, lanes_down, row)
+        inner[rows + row : rows + row + 8, :] = jnp.where(upper, low, high)
+        outer[rows + row : rows + row + 8, :] = jnp.where(upper, high, low)
+
+
+def smooth_kernel(residual, *refs):
+    *faces, table, out, out_up, out_down, out_inner, out_outer, ghosts = refs
+    read_ghosts(table, faces, ghosts, FINE)
     for x in range(8):
         for y in range(8):
             centre, around = beside(residual, ghosts, x, y)
@@ -149,13 +196,12 @@
             at = 64 * x + 8 * y
             out[at : at + 8, :] = first + RELAX_FINE * (centre - applied)
     write_faces(out, out_up, out_down)
-
-
-def defect_kernel(
-    residual, second, up, down, near_up, far_up, near_down, far_down, table,
-    defect, coarse, out_up, out_down, ghosts, sums, scaled,
-):
-    read_ghosts(table, ((up, near_up, far_up), (down, near_down, far_down)), ghosts, FINE)
+    write_pair(table, UPPER_NEAR, out_up, out_down, out_inner, out_outer, FINE)
+
+
+def defect_kernel(residual, second, *refs):
+    *faces, table, defect, coarse, out_up, out_down, out_inner, out_outer, ghosts, sums, scaled = refs
+    read_ghosts(table, faces, ghosts, FINE)
     for big_x in range(4):
         for big_y in range(4):
             total = None
@@ -172,13 +218,12 @@
     coarse[...] = restricted
     scaled[...] = RELAX_COARSE * restricted
     write_coarse_faces(scaled, out_up, out_down)
-
-
-def coarse_kernel(
-    coarse, up, down, near_up, far_up, near_down, far_down, table,
-    out, out_up, out_down, ghosts, low_y, high_y, low_z, high_z,
-):
-    read_ghosts(table, ((up, near_up, far_up), (down, near_down, far_down)), ghosts, COARSE)
+    write_pair(table, UPPER_NEAR, out_up, out_down, out_inner, out_outer, COARSE)
+
+
+def coarse_kernel(coarse, *refs):
+    *faces, table, out, out_up, out_down, out_inner, out_outer, ghosts, low_y, high_y, low_z, high_z = refs
+    read_ghosts(table, faces, ghosts, COARSE)
     for x in range(4):
         low_y[16 * x : 16 * x + 4, :] = ghosts[32 + 4 * x : 36 + 4 * x, :]
         high_y[16 * x + 12 : 16 * x + 16, :] = ghosts[48 + 4 * x : 52 + 4 * x, :]
@@ -196,13 +241,12 @@
     around = ((above_x + below_x) + (above_y + below_y)) + (above_z + below_z)
     out[...] = first + RELAX_COARSE * (rhs - (6.0 * first - around) * 0.25)
     write_coarse_faces(out, out_up, out_down)
-
-
-def correct_kernel(
-    second, defect, coarse, up, down, near_up, far_up, near_down, far_down, table,
-    out, out_up, out_down, ghosts, wide, wide_ghosts, spread,
-):
-    read_ghosts(table, ((up, near_up, far_up), (down, near_down, far_down)), ghosts, COARSE)
+    write_pair(table, UPPER_NEAR, out_up, out_down, out_inner, out_outer, COARSE)
+
+
+def correct_kernel(second, defect, coarse, *refs):
+    *faces, table, out, out_up, out_down, out_inner, out_outer, ghosts, wide, wide_ghosts, spread = refs
+    read_ghosts(table, faces, ghosts, COARSE)
     wide[pl.ds(0, 64, stride=2), :] = coarse[...]
     wide[pl.ds(1, 64, stride=2), :] = coarse[...]
     wide_ghosts[pl.ds(0, 64, stride=2), :] = ghosts[0:64, :]
@@ -230,10 +274,12 @@
             left = defect[at : at + 8, :] - (6.0 * centre - around)
             out[at : at + 8, :] = (second[at : at + 8, :] + centre) + RELAX_FINE * left
     write_faces(out, out_up, out_down)
-
-
-def image_kernel(residual, direction, up, down, near_up, far_up, near_down, far_down, table, image, sums, ghosts):
-    read_ghosts(table, ((up, near_up, far_up), (down, near_down, far_down)), ghosts, FINE)
+    write_pair(table, UPPER_NEAR, out_up, out_down, out_inner, out_outer, FINE)
+
+
+def image_kernel(residual, direction, *refs):
+    *faces, table, image, sums, ghosts = refs
+    read_ghosts(table, faces, ghosts, FINE)
     zero = jnp.zeros((8, LANES), jnp.float32)
     parts = [zero] * 5
     for x in range(8):
@@ -276,58 +322,60 @@
     norm[...] = jnp.sqrt(old_square - 2.0 * step_size * cross_term + step_size * step_size * image_square)
 
 
-def shift(block, distance):
+def swap(block, distance, offset):
     count = lax.axis_size(AXES)
-    route = [(i, i + distance) for i in range(count) if 0 <= i + distance < count]
+    route = []
+    for low in range(offset - 2 * distance, count):
+        if low >= 0 and low + distance < count and (low - offset) % (2 * distance) < distance:
+            route += [(low, low + distance), (low + distance, low)]
     return lax.ppermute(block, AXES, route)
 
 
-def exchange(up, down, table, rows):
-    near_up = shift(up, 1)
-    near_down = shift(down, -1)
-    message = [f32(rows + rows // 2, LANES)]
-    (message_up,) = call(functools.partial(pack_kernel, rows, FORWARD_UP), "pack_up", message, up, near_up, table)
-    far_up = shift(message_up, 2)
-    (message_down,) = call(
-        functools.partial(pack_kernel, rows, FORWARD_DOWN), "pack_down", message, down, near_down, table
-    )
-    far_down = shift(message_down, -2)
-    return up, down, near_up, far_up, near_down, far_down, table
+def exchange(up, down, inner, outer, table, rows):
+    near_outer = swap(outer, 1, 1)
+    near_inner = swap(inner, 1, 0)
+    message = f32(rows + rows // 2, LANES)
+    inner, outer = call(
+        functools.partial(pack_kernel, rows), "pack", [message] * 2, up, down, near_inner, near_outer, table
+    )
+    far_outer = swap(outer, 2, 2)
+    far_inner = swap(inner, 2, 0)
+    return up, down, near_inner, near_outer, far_inner, far_outer, table
 
 
 def local(right_side, counts, neighbours):
     device = lax.axis_index(AXES).astype(jnp.int32).reshape(1)
     fine = f32(512, LANES)
-    faces = [f32(FINE, LANES)] * 2
+    faces = [f32(FINE, LANES)] * 4
     coarse = f32(64, LANES)
-    coarse_faces = [f32(COARSE, LANES)] * 2
+    coarse_faces = [f32(COARSE, LANES)] * 4
     fine_ghosts = pltpu.VMEM((2 * FINE, LANES), jnp.float32)
     coarse_ghosts = pltpu.VMEM((2 * COARSE, LANES), jnp.float32)
     scratch = lambda rows: pltpu.VMEM((rows, LANES), jnp.float32)
 
-    residual_in, up, down, table = call(
+    residual_in, *sides, table = call(
         start_kernel, "start", [fine, *faces, i32(TABLE_ROWS, LANES)], device, counts, right_side, neighbours,
         in_specs=[SMEM, SMEM, VMEM, VMEM],
     )
-    second, up, down = call(
-        smooth_kernel, "smooth", [fine, *faces], residual_in, *exchange(up, down, table, FINE), scratch=[fine_ghosts]
-    )
-    defect, rhs, up, down = call(
+    second, *sides = call(
+        smooth_kernel, "smooth", [fine, *faces], residual_in, *exchange(*sides, table, FINE), scratch=[fine_ghosts]
+    )
+    defect, rhs, *sides = call(
         defect_kernel, "defect", [fine, coarse, *coarse_faces],
-        residual_in, second, *exchange(up, down, table, FINE), scratch=[fine_ghosts, scratch(128), scratch(64)],
-    )
-    correction, up, down = call(
+        residual_in, second, *exchange(*sides, table, FINE), scratch=[fine_ghosts, scratch(128), scratch(64)],
+    )
+    correction, *sides = call(
         coarse_kernel, "coarse", [coarse, *coarse_faces],
-        rhs, *exchange(up, down, table, COARSE), scratch=[coarse_ghosts] + [scratch(64)] * 4,
-    )
-    direction, up, down = call(
+        rhs, *exchange(*sides, table, COARSE), scratch=[coarse_ghosts] + [scratch(64)] * 4,
+    )
+    direction, *sides = call(
         correct_kernel, "correct", [fine, *faces],
-        second, defect, correction, *exchange(up, down, table, COARSE),
+        second, defect, correction, *exchange(*sides, table, COARSE),
         scratch=[coarse_ghosts, scratch(128), scratch(128), scratch(512)],
     )
     image, sums = call(
         image_kernel, "image", [fine, f32(lax.axis_size("inner"), 1, LANES)],
-        residual_in, direction, *exchange(up, down, table, FINE), scratch=[fine_ghosts],
+        residual_in, direction, *exchange(*sides, table, FINE), scratch=[fine_ghosts],
     )
     received = lax.all_to_all(sums, "inner", 0, 0, tiled=True)
     (sums,) = call(add_kernel, "add", [f32(lax.axis_size("outer"), 1, LANES)], received)

time: 217 us -> 187 us (0.86)
  Pallas kernels: 32.6 us -> 4.58 us
  starting transfers between devices: 74.5 us -> 88.4 us
  blocking collectives: 69.4 us -> 55.6 us
  local copies, waits for them, and re-layouts: 10.6 us -> 2.15 us
  waiting for transfers between devices: 27.9 us -> 34.1 us
    pallas_call x18 -> x13, Pallas kernels: 32.6 us -> 4.58 us  [call(): pl.pallas_call(kernel, out_shape=outs, in_specs=in_specs or [VMEM] * len(...]
    ppermute x20, starting transfers between devices: 74.5 us -> 88.4 us  [swap(): return lax.ppermute(block, AXES, route)]
    all_to_all x1, blocking collectives: 55.6 us -> 43.7 us  [local(): received = lax.all_to_all(sums, 'outer', 0, 0, tiled=True)]
    unnamed x40 -> x6, local copies, waits for them, and re-layouts: 9.43 us -> 1.64 us
    ppermute x20, waiting for transfers between devices: 27.9 us -> 34.1 us  [swap(): return lax.ppermute(block, AXES, route)]
  transfers between devices with their start and end apart: 20 -> 20, of which waited for: 11 -> 11; matrix products, arithmetic and copies ran while one was open for 0% -> 0% of each run, Pallas kernels for 7% -> 0%
where the time goes in v2:
time: 187 us; the launch traced here: 186 us
  starting transfers between devices  88.4 us (47%)
  blocking collectives  55.6 us (30%)
  waiting for transfers between devices  34.1 us (18%)
  Pallas kernels  4.58 us (2%)
  local copies, waits for them, and re-layouts  2.15 us (1%)
    ppermute x20, starting transfers between devices, swap(): return lax.ppermute(block, AXES, route)  88.4 us
    all_to_all x1, blocking collectives, local(): received = lax.all_to_all(sums, 'outer', 0, 0, tiled=True)  43.7 us
    ppermute x20, waiting for transfers between devices, swap(): return lax.ppermute(block, AXES, route)  34.1 us
    all_to_all x1, blocking collectives, local(): received = lax.all_to_all(sums, 'inner', 0, 0, tiled=True)  11.9 us
    pallas_call x13, Pallas kernels, call(): pl.pallas_call(kernel, out_shape=outs, in_specs=in_specs or [VMEM] * len(...  4.58 us
  transfers between devices with their start and end apart: 20, of which 11 were waited for; matrix products, arithmetic and copies ran while one was open for 0% of the time, Pallas kernels for 0%

profile of v2, /device:TPU:1, one launch (start us, length us, event | category | flops | bytes accessed | tf_op | source)
XLA Modules:
  0.0 185.8 jit_solution(14877513684946597871)
XLA Ops:
  2.9 4.0 %collective-permute-start = (f32[192,128]{1,0:T(8,128)S(1)}, f32[192,128]{1,0:T(8,128)S(1)}, u32[]{:S(2)}, u32[]{:S(2)}) collective-permute-start(f32[192,128]{1,0:T(8,128)S(1)} %get-tuple-element.48), channel_id=1, source_target_pairs={{0,1},{1,0},{2,3},{3,2},{4,5},{5,4},{6,7},{7,6},{8,9},{9,8},{10,11... | collective-permute-start | bytes 294920 | tf_op jit(solution)/shard_map/ppermute | solution.py:331
  7.0 5.7 %collective-permute-start.1 = (f32[192,128]{1,0:T(8,128)S(1)}, f32[192,128]{1,0:T(8,128)S(1)}, u32[]{:S(2)}, u32[]{:S(2)}) collective-permute-start(f32[192,128]{1,0:T(8,128)S(1)} %get-tuple-element.49), channel_id=1, source_target_pairs={{1,2},{2,1},{3,4},{4,3},{5,6},{6,5},{7,8},{8,7},{9,10},{10,9},{11,... | collective-permute-start | bytes 294920 | tf_op jit(solution)/shard_map/ppermute | solution.py:331
  12.7 3.0 %collective-permute-done.1.near_outer.refs_3_ = f32[192,128]{1,0:T(8,128)S(1)} collective-permute-done((f32[192,128]{1,0:T(8,128)S(1)}, f32[192,128]{1,0:T(8,128)S(1)}, u32[]{:S(2)}, u32[]{:S(2)}) %collective-permute-start.1) | collective-permute-done | bytes 98336 | tf_op jit(solution)/shard_map/ppermute | solution.py:331
  15.9 1.9 %collective-permute-start.2 = (f32[288,128]{1,0:T(8,128)S(1)}, f32[288,128]{1,0:T(8,128)S(1)}, u32[]{:S(2)}, u32[]{:S(2)}) collective-permute-start(f32[288,128]{1,0:T(8,128)S(1)} %get-tuple-element.51), channel_id=1, source_target_pairs={{0,2},{2,0},{1,3},{3,1},{4,6},{6,4},{5,7},{7,5},{8,10},{10,8},{9,1... | collective-permute-start | bytes 442376 | tf_op jit(solution)/shard_map/ppermute | solution.py:331
  17.8 7.0 %collective-permute-start.3 = (f32[288,128]{1,0:T(8,128)S(1)}, f32[288,128]{1,0:T(8,128)S(1)}, u32[]{:S(2)}, u32[]{:S(2)}) collective-permute-start(f32[288,128]{1,0:T(8,128)S(1)} %get-tuple-element.52), channel_id=1, source_target_pairs={{2,4},{4,2},{3,5},{5,3},{6,8},{8,6},{7,9},{9,7},{10,12},{12,10},{1... | collective-permute-start | bytes 442376 | tf_op jit(solution)/shard_map/ppermute | solution.py:331
  24.8 6.6 %collective-permute-done.3.refs_5_ = f32[288,128]{1,0:T(8,128)S(1)} collective-permute-done((f32[288,128]{1,0:T(8,128)S(1)}, f32[288,128]{1,0:T(8,128)S(1)}, u32[]{:S(2)}, u32[]{:S(2)}) %collective-permute-start.3) | collective-permute-done | bytes 147488 | tf_op jit(solution)/shard_map/ppermute | solution.py:331
  33.9 6.8 %collective-permute-start.5 = (f32[192,128]{1,0:T(8,128)S(1)}, f32[192,128]{1,0:T(8,128)S(1)}, u32[]{:S(2)}, u32[]{:S(2)}) collective-permute-start(f32[192,128]{1,0:T(8,128)S(1)} %get-tuple-element.57), channel_id=1, source_target_pairs={{1,2},{2,1},{3,4},{4,3},{5,6},{6,5},{7,8},{8,7},{9,10},{10,9},{11,... | collective-permute-start | bytes 294920 | tf_op jit(solution)/shard_map/ppermute | solution.py:331
  40.7 2.3 %collective-permute-done.5.near_outer.refs_3_ = f32[192,128]{1,0:T(8,128)S(1)} collective-permute-done((f32[192,128]{1,0:T(8,128)S(1)}, f32[192,128]{1,0:T(8,128)S(1)}, u32[]{:S(2)}, u32[]{:S(2)}) %collective-permute-start.5) | collective-permute-done | bytes 98336 | tf_op jit(solution)/shard_map/ppermute | solution.py:331
  43.2 1.9 %collective-permute-start.6 = (f32[288,128]{1,0:T(8,128)S(1)}, f32[288,128]{1,0:T(8,128)S(1)}, u32[]{:S(2)}, u32[]{:S(2)}) collective-permute-start(f32[288,128]{1,0:T(8,128)S(1)} %get-tuple-element.58), channel_id=1, source_target_pairs={{0,2},{2,0},{1,3},{3,1},{4,6},{6,4},{5,7},{7,5},{8,10},{10,8},{9,1... | collective-permute-start | bytes 442376 | tf_op jit(solution)/shard_map/ppermute | solution.py:331
  45.1 8.6 %collective-permute-start.7 = (f32[288,128]{1,0:T(8,128)S(1)}, f32[288,128]{1,0:T(8,128)S(1)}, u32[]{:S(2)}, u32[]{:S(2)}) collective-permute-start(f32[288,128]{1,0:T(8,128)S(1)} %get-tuple-element.59), channel_id=1, source_target_pairs={{2,4},{4,2},{3,5},{5,3},{6,8},{8,6},{7,9},{9,7},{10,12},{12,10},{1... | collective-permute-start | bytes 442376 | tf_op jit(solution)/shard_map/ppermute | solution.py:331
  53.7 5.2 %collective-permute-done.7.refs_5_ = f32[288,128]{1,0:T(8,128)S(1)} collective-permute-done((f32[288,128]{1,0:T(8,128)S(1)}, f32[288,128]{1,0:T(8,128)S(1)}, u32[]{:S(2)}, u32[]{:S(2)}) %collective-permute-start.7) | collective-permute-done | bytes 147488 | tf_op jit(solution)/shard_map/ppermute | solution.py:331
  59.5 2.4 %collective-permute-start.8 = (f32[48,128]{1,0:T(8,128)S(1)}, f32[48,128]{1,0:T(8,128)S(1)}, u32[]{:S(2)}, u32[]{:S(2)}) collective-permute-start(f32[48,128]{1,0:T(8,128)S(1)} %get-tuple-element.64), channel_id=1, source_target_pairs={{0,1},{1,0},{2,3},{3,2},{4,5},{5,4},{6,7},{7,6},{8,9},{9,8},{10,11... | collective-permute-start | bytes 73736 | tf_op jit(solution)/shard_map/ppermute | solution.py:331
  61.8 6.6 %collective-permute-start.9 = (f32[48,128]{1,0:T(8,128)S(1)}, f32[48,128]{1,0:T(8,128)S(1)}, u32[]{:S(2)}, u32[]{:S(2)}) collective-permute-start(f32[48,128]{1,0:T(8,128)S(1)} %get-tuple-element.65), channel_id=1, source_target_pairs={{1,2},{2,1},{3,4},{4,3},{5,6},{6,5},{7,8},{8,7},{9,10},{10,9},{11,... | collective-permute-start | bytes 73736 | tf_op jit(solution)/shard_map/ppermute | solution.py:331
  72.1 5.2 %collective-permute-start.11 = (f32[72,128]{1,0:T(8,128)S(1)}, f32[72,128]{1,0:T(8,128)S(1)}, u32[]{:S(2)}, u32[]{:S(2)}) collective-permute-start(f32[72,128]{1,0:T(8,128)S(1)} %get-tuple-element.67), channel_id=1, source_target_pairs={{2,4},{4,2},{3,5},{5,3},{6,8},{8,6},{7,9},{9,7},{10,12},{12,10},{1... | collective-permute-start | bytes 110600 | tf_op jit(solution)/shard_map/ppermute | solution.py:331
  77.3 2.2 %collective-permute-done.11.refs_5_ = f32[72,128]{1,0:T(8,128)S(1)} collective-permute-done((f32[72,128]{1,0:T(8,128)S(1)}, f32[72,128]{1,0:T(8,128)S(1)}, u32[]{:S(2)}, u32[]{:S(2)}) %collective-permute-start.11) | collective-permute-done | bytes 36896 | tf_op jit(solution)/shard_map/ppermute | solution.py:331
  79.8 2.0 %collective-permute-start.12 = (f32[48,128]{1,0:T(8,128)S(1)}, f32[48,128]{1,0:T(8,128)S(1)}, u32[]{:S(2)}, u32[]{:S(2)}) collective-permute-start(f32[48,128]{1,0:T(8,128)S(1)} %get-tuple-element.71), channel_id=1, source_target_pairs={{0,1},{1,0},{2,3},{3,2},{4,5},{5,4},{6,7},{7,6},{8,9},{9,8},{10,11... | collective-permute-start | bytes 73736 | tf_op jit(solution)/shard_map/ppermute | solution.py:331
  81.8 5.6 %collective-permute-start.13 = (f32[48,128]{1,0:T(8,128)S(1)}, f32[48,128]{1,0:T(8,128)S(1)}, u32[]{:S(2)}, u32[]{:S(2)}) collective-permute-start(f32[48,128]{1,0:T(8,128)S(1)} %get-tuple-element.72), channel_id=1, source_target_pairs={{1,2},{2,1},{3,4},{4,3},{5,6},{6,5},{7,8},{8,7},{9,10},{10,9},{11,... | collective-permute-start | bytes 73736 | tf_op jit(solution)/shard_map/ppermute | solution.py:331
  90.9 9.3 %collective-permute-start.15 = (f32[72,128]{1,0:T(8,128)S(1)}, f32[72,128]{1,0:T(8,128)S(1)}, u32[]{:S(2)}, u32[]{:S(2)}) collective-permute-start(f32[72,128]{1,0:T(8,128)S(1)} %get-tuple-element.74), channel_id=1, source_target_pairs={{2,4},{4,2},{3,5},{5,3},{6,8},{8,6},{7,9},{9,7},{10,12},{12,10},{1... | collective-permute-start | bytes 110600 | tf_op jit(solution)/shard_map/ppermute | solution.py:331
  104.1 6.3 %collective-permute-start.17 = (f32[192,128]{1,0:T(8,128)S(1)}, f32[192,128]{1,0:T(8,128)S(1)}, u32[]{:S(2)}, u32[]{:S(2)}) collective-permute-start(f32[192,128]{1,0:T(8,128)S(1)} %get-tuple-element.79), channel_id=1, source_target_pairs={{1,2},{2,1},{3,4},{4,3},{5,6},{6,5},{7,8},{8,7},{9,10},{10,9},{11,... | collective-permute-start | bytes 294920 | tf_op jit(solution)/shard_map/ppermute | solution.py:331
  110.4 2.3 %collective-permute-done.17.near_outer.refs_3_ = f32[192,128]{1,0:T(8,128)S(1)} collective-permute-done((f32[192,128]{1,0:T(8,128)S(1)}, f32[192,128]{1,0:T(8,128)S(1)}, u32[]{:S(2)}, u32[]{:S(2)}) %collective-permute-start.17) | collective-permute-done | bytes 98336 | tf_op jit(solution)/shard_map/ppermute | solution.py:331
  114.8 5.5 %collective-permute-start.19 = (f32[288,128]{1,0:T(8,128)S(1)}, f32[288,128]{1,0:T(8,128)S(1)}, u32[]{:S(2)}, u32[]{:S(2)}) collective-permute-start(f32[288,128]{1,0:T(8,128)S(1)} %get-tuple-element.81), channel_id=1, source_target_pairs={{2,4},{4,2},{3,5},{5,3},{6,8},{8,6},{7,9},{9,7},{10,12},{12,10},{1... | collective-permute-start | bytes 442376 | tf_op jit(solution)/shard_map/ppermute | solution.py:331
  122.0 6.0 %collective-permute-done.19.refs_5_ = f32[288,128]{1,0:T(8,128)S(1)} collective-permute-done((f32[288,128]{1,0:T(8,128)S(1)}, f32[288,128]{1,0:T(8,128)S(1)}, u32[]{:S(2)}, u32[]{:S(2)}) %collective-permute-start.19) | collective-permute-done | bytes 147488 | tf_op jit(solution)/shard_map/ppermute | solution.py:331
  128.6 11.9 %all_to_all.10.received = f32[16,1,128]{2,1,0:T(1,128)S(1)} all-to-all(f32[16,1,128]{2,1,0:T(1,128)S(1)} %get-tuple-element.82), channel_id=1, replica_groups=mesh['curve'=96,'level'=8] {'curve':(48)2,'level'}, dimensions={0} | all-to-all | bytes 16384 | tf_op jit(solution)/shard_map/all_to_all | solution.py:380
  140.5 43.7 %all_to_all.11.received = f32[48,1,128]{2,1,0:T(1,128)S(1)} all-to-all(f32[48,1,128]{2,1,0:T(1,128)S(1)} %add.5), channel_id=1, replica_groups=mesh['curve'=96,'level'=8] {'curve':(1)48}, dimensions={0} | all-to-all | bytes 49152 | tf_op jit(solution)/shard_map/all_to_all | solution.py:382
  (38 shorter events, 22.8 us)
Async XLA Ops:
  0.6 0.7 copy-start.2
  0.6 0.7 copy-start.1
  1.3 0.9 copy-start
  2.9 9.8 %collective-permute-start = (f32[192,128]{1,0:T(8,128)S(1)}, f32[192,128]{1,0:T(8,128)S(1)}, u32[]{:S(2)}, u32[]{:S(2)}) collective-permute-start(f32[192,128]{1,0:T(8,128)S(1)} %get-tuple-element.48), channel_id=1, source_target_pairs={{0,1},{1,0},{2,3},{3,2},{4,5},{5,4},{6,7},{7,6},{8,9},{9,8},{10,11... | collective-permute-start | bytes 294920 | tf_op jit(solution)/shard_map/ppermute | solution.py:331
  7.0 8.7 %collective-permute-start.1 = (f32[192,128]{1,0:T(8,128)S(1)}, f32[192,128]{1,0:T(8,128)S(1)}, u32[]{:S(2)}, u32[]{:S(2)}) collective-permute-start(f32[192,128]{1,0:T(8,128)S(1)} %get-tuple-element.49), channel_id=1, source_target_pairs={{1,2},{2,1},{3,4},{4,3},{5,6},{6,5},{7,8},{8,7},{9,10},{10,9},{11,... | collective-permute-start | bytes 294920 | tf_op jit(solution)/shard_map/ppermute | solution.py:331
  15.9 8.9 %collective-permute-start.2 = (f32[288,128]{1,0:T(8,128)S(1)}, f32[288,128]{1,0:T(8,128)S(1)}, u32[]{:S(2)}, u32[]{:S(2)}) collective-permute-start(f32[288,128]{1,0:T(8,128)S(1)} %get-tuple-element.51), channel_id=1, source_target_pairs={{0,2},{2,0},{1,3},{3,1},{4,6},{6,4},{5,7},{7,5},{8,10},{10,8},{9,1... | collective-permute-start | bytes 442376 | tf_op jit(solution)/shard_map/ppermute | solution.py:331
  17.8 13.6 %collective-permute-start.3 = (f32[288,128]{1,0:T(8,128)S(1)}, f32[288,128]{1,0:T(8,128)S(1)}, u32[]{:S(2)}, u32[]{:S(2)}) collective-permute-start(f32[288,128]{1,0:T(8,128)S(1)} %get-tuple-element.52), channel_id=1, source_target_pairs={{2,4},{4,2},{3,5},{5,3},{6,8},{8,6},{7,9},{9,7},{10,12},{12,10},{1... | collective-permute-start | bytes 442376 | tf_op jit(solution)/shard_map/ppermute | solution.py:331
  32.0 8.7 %collective-permute-start.4 = (f32[192,128]{1,0:T(8,128)S(1)}, f32[192,128]{1,0:T(8,128)S(1)}, u32[]{:S(2)}, u32[]{:S(2)}) collective-permute-start(f32[192,128]{1,0:T(8,128)S(1)} %get-tuple-element.56), channel_id=1, source_target_pairs={{0,1},{1,0},{2,3},{3,2},{4,5},{5,4},{6,7},{7,6},{8,9},{9,8},{10,11... | collective-permute-start | bytes 294920 | tf_op jit(solution)/shard_map/ppermute | solution.py:331
  33.9 9.1 %collective-permute-start.5 = (f32[192,128]{1,0:T(8,128)S(1)}, f32[192,128]{1,0:T(8,128)S(1)}, u32[]{:S(2)}, u32[]{:S(2)}) collective-permute-start(f32[192,128]{1,0:T(8,128)S(1)} %get-tuple-element.57), channel_id=1, source_target_pairs={{1,2},{2,1},{3,4},{4,3},{5,6},{6,5},{7,8},{8,7},{9,10},{10,9},{11,... | collective-permute-start | bytes 294920 | tf_op jit(solution)/shard_map/ppermute | solution.py:331
  43.2 10.5 %collective-permute-start.6 = (f32[288,128]{1,0:T(8,128)S(1)}, f32[288,128]{1,0:T(8,128)S(1)}, u32[]{:S(2)}, u32[]{:S(2)}) collective-permute-start(f32[288,128]{1,0:T(8,128)S(1)} %get-tuple-element.58), channel_id=1, source_target_pairs={{0,2},{2,0},{1,3},{3,1},{4,6},{6,4},{5,7},{7,5},{8,10},{10,8},{9,1... | collective-permute-start | bytes 442376 | tf_op jit(solution)/shard_map/ppermute | solution.py:331
  45.1 13.8 %collective-permute-start.7 = (f32[288,128]{1,0:T(8,128)S(1)}, f32[288,128]{1,0:T(8,128)S(1)}, u32[]{:S(2)}, u32[]{:S(2)}) collective-permute-start(f32[288,128]{1,0:T(8,128)S(1)} %get-tuple-element.59), channel_id=1, source_target_pairs={{2,4},{4,2},{3,5},{5,3},{6,8},{8,6},{7,9},{9,7},{10,12},{12,10},{1... | collective-permute-start | bytes 442376 | tf_op jit(solution)/shard_map/ppermute | solution.py:331
  59.5 9.0 %collective-permute-start.8 = (f32[48,128]{1,0:T(8,128)S(1)}, f32[48,128]{1,0:T(8,128)S(1)}, u32[]{:S(2)}, u32[]{:S(2)}) collective-permute-start(f32[48,128]{1,0:T(8,128)S(1)} %get-tuple-element.64), channel_id=1, source_target_pairs={{0,1},{1,0},{2,3},{3,2},{4,5},{5,4},{6,7},{7,6},{8,9},{9,8},{10,11... | collective-permute-start | bytes 73736 | tf_op jit(solution)/shard_map/ppermute | solution.py:331
  61.8 8.2 %collective-permute-start.9 = (f32[48,128]{1,0:T(8,128)S(1)}, f32[48,128]{1,0:T(8,128)S(1)}, u32[]{:S(2)}, u32[]{:S(2)}) collective-permute-start(f32[48,128]{1,0:T(8,128)S(1)} %get-tuple-element.65), channel_id=1, source_target_pairs={{1,2},{2,1},{3,4},{4,3},{5,6},{6,5},{7,8},{8,7},{9,10},{10,9},{11,... | collective-permute-start | bytes 73736 | tf_op jit(solution)/shard_map/ppermute | solution.py:331
  70.1 7.2 %collective-permute-start.10 = (f32[72,128]{1,0:T(8,128)S(1)}, f32[72,128]{1,0:T(8,128)S(1)}, u32[]{:S(2)}, u32[]{:S(2)}) collective-permute-start(f32[72,128]{1,0:T(8,128)S(1)} %get-tuple-element.66), channel_id=1, source_target_pairs={{0,2},{2,0},{1,3},{3,1},{4,6},{6,4},{5,7},{7,5},{8,10},{10,8},{9,1... | collective-permute-start | bytes 110600 | tf_op jit(solution)/shard_map/ppermute | solution.py:331
  72.1 7.5 %collective-permute-start.11 = (f32[72,128]{1,0:T(8,128)S(1)}, f32[72,128]{1,0:T(8,128)S(1)}, u32[]{:S(2)}, u32[]{:S(2)}) collective-permute-start(f32[72,128]{1,0:T(8,128)S(1)} %get-tuple-element.67), channel_id=1, source_target_pairs={{2,4},{4,2},{3,5},{5,3},{6,8},{8,6},{7,9},{9,7},{10,12},{12,10},{1... | collective-permute-start | bytes 110600 | tf_op jit(solution)/shard_map/ppermute | solution.py:331
  79.8 7.6 %collective-permute-start.12 = (f32[48,128]{1,0:T(8,128)S(1)}, f32[48,128]{1,0:T(8,128)S(1)}, u32[]{:S(2)}, u32[]{:S(2)}) collective-permute-start(f32[48,128]{1,0:T(8,128)S(1)} %get-tuple-element.71), channel_id=1, source_target_pairs={{0,1},{1,0},{2,3},{3,2},{4,5},{5,4},{6,7},{7,6},{8,9},{9,8},{10,11... | collective-permute-start | bytes 73736 | tf_op jit(solution)/shard_map/ppermute | solution.py:331
  81.8 7.1 %collective-permute-start.13 = (f32[48,128]{1,0:T(8,128)S(1)}, f32[48,128]{1,0:T(8,128)S(1)}, u32[]{:S(2)}, u32[]{:S(2)}) collective-permute-start(f32[48,128]{1,0:T(8,128)S(1)} %get-tuple-element.72), channel_id=1, source_target_pairs={{1,2},{2,1},{3,4},{4,3},{5,6},{6,5},{7,8},{8,7},{9,10},{10,9},{11,... | collective-permute-start | bytes 73736 | tf_op jit(solution)/shard_map/ppermute | solution.py:331
  89.0 11.3 %collective-permute-start.14 = (f32[72,128]{1,0:T(8,128)S(1)}, f32[72,128]{1,0:T(8,128)S(1)}, u32[]{:S(2)}, u32[]{:S(2)}) collective-permute-start(f32[72,128]{1,0:T(8,128)S(1)} %get-tuple-element.73), channel_id=1, source_target_pairs={{0,2},{2,0},{1,3},{3,1},{4,6},{6,4},{5,7},{7,5},{8,10},{10,8},{9,1... | collective-permute-start | bytes 110600 | tf_op jit(solution)/shard_map/ppermute | solution.py:331
  90.9 11.0 %collective-permute-start.15 = (f32[72,128]{1,0:T(8,128)S(1)}, f32[72,128]{1,0:T(8,128)S(1)}, u32[]{:S(2)}, u32[]{:S(2)}) collective-permute-start(f32[72,128]{1,0:T(8,128)S(1)} %get-tuple-element.74), channel_id=1, source_target_pairs={{2,4},{4,2},{3,5},{5,3},{6,8},{8,6},{7,9},{9,7},{10,12},{12,10},{1... | collective-permute-start | bytes 110600 | tf_op jit(solution)/shard_map/ppermute | solution.py:331
  102.1 8.2 %collective-permute-start.16 = (f32[192,128]{1,0:T(8,128)S(1)}, f32[192,128]{1,0:T(8,128)S(1)}, u32[]{:S(2)}, u32[]{:S(2)}) collective-permute-start(f32[192,128]{1,0:T(8,128)S(1)} %get-tuple-element.78), channel_id=1, source_target_pairs={{0,1},{1,0},{2,3},{3,2},{4,5},{5,4},{6,7},{7,6},{8,9},{9,8},{10,11... | collective-permute-start | bytes 294920 | tf_op jit(solution)/shard_map/ppermute | solution.py:331
  104.1 8.6 %collective-permute-start.17 = (f32[192,128]{1,0:T(8,128)S(1)}, f32[192,128]{1,0:T(8,128)S(1)}, u32[]{:S(2)}, u32[]{:S(2)}) collective-permute-start(f32[192,128]{1,0:T(8,128)S(1)} %get-tuple-element.79), channel_id=1, source_target_pairs={{1,2},{2,1},{3,4},{4,3},{5,6},{6,5},{7,8},{8,7},{9,10},{10,9},{11,... | collective-permute-start | bytes 294920 | tf_op jit(solution)/shard_map/ppermute | solution.py:331
  112.8 9.2 %collective-permute-start.18 = (f32[288,128]{1,0:T(8,128)S(1)}, f32[288,128]{1,0:T(8,128)S(1)}, u32[]{:S(2)}, u32[]{:S(2)}) collective-permute-start(f32[288,128]{1,0:T(8,128)S(1)} %get-tuple-element.80), channel_id=1, source_target_pairs={{0,2},{2,0},{1,3},{3,1},{4,6},{6,4},{5,7},{7,5},{8,10},{10,8},{9,1... | collective-permute-start | bytes 442376 | tf_op jit(solution)/shard_map/ppermute | solution.py:331
  114.8 13.2 %collective-permute-start.19 = (f32[288,128]{1,0:T(8,128)S(1)}, f32[288,128]{1,0:T(8,128)S(1)}, u32[]{:S(2)}, u32[]{:S(2)}) collective-permute-start(f32[288,128]{1,0:T(8,128)S(1)} %get-tuple-element.81), channel_id=1, source_target_pairs={{2,4},{4,2},{3,5},{5,3},{6,8},{8,6},{7,9},{9,7},{10,12},{12,10},{1... | collective-permute-start | bytes 442376 | tf_op jit(solution)/shard_map/ppermute | solution.py:331

commit v3 on v2

--- a/solution.py
+++ b/solution.py
@@ -7,6 +7,7 @@
 from jax.experimental.pallas import tpu as pltpu
 from jax.sharding import Mesh
 from jax.sharding import PartitionSpec as P
+
 
 LANES = 128
 TAIL = 64
@@ -38,7 +39,7 @@
     return jax.ShapeDtypeStruct(shape, jnp.int32)
 
 
-def call(kernel, name, outs, *args, in_specs=None, out_specs=None, scratch=()):
+def call(kernel, outs, *args, in_specs=None, out_specs=None, scratch=()):
     return pl.pallas_call(
         kernel,
         out_shape=outs,
@@ -46,7 +47,6 @@
         out_specs=out_specs or [VMEM] * len(outs),
         scratch_shapes=list(scratch),
         compiler_params=pltpu.CompilerParams(vmem_limit_bytes=GRANT),
-        name=name,
     )(*args)
 
 
@@ -331,19 +331,17 @@
     return lax.ppermute(block, AXES, route)
 
 
-def exchange(up, down, inner, outer, table, rows):
+def exchange(rows, up, down, inner, outer, table):
     near_outer = swap(outer, 1, 1)
     near_inner = swap(inner, 1, 0)
     message = f32(rows + rows // 2, LANES)
-    inner, outer = call(
-        functools.partial(pack_kernel, rows), "pack", [message] * 2, up, down, near_inner, near_outer, table
-    )
+    inner, outer = call(functools.partial(pack_kernel, rows), [message] * 2, up, down, near_inner, near_outer, table)
     far_outer = swap(outer, 2, 2)
     far_inner = swap(inner, 2, 0)
     return up, down, near_inner, near_outer, far_inner, far_outer, table
 
 
-def local(right_side, counts, neighbours):
+def step(right_side, counts, neighbours):
     device = lax.axis_index(AXES).astype(jnp.int32).reshape(1)
     fine = f32(512, LANES)
     faces = [f32(FINE, LANES)] * 4
@@ -354,35 +352,33 @@
     scratch = lambda rows: pltpu.VMEM((rows, LANES), jnp.float32)
 
     residual_in, *sides, table = call(
-        start_kernel, "start", [fine, *faces, i32(TABLE_ROWS, LANES)], device, counts, right_side, neighbours,
+        start_kernel, [fine, *faces, i32(TABLE_ROWS, LANES)], device, counts, right_side, neighbours,
         in_specs=[SMEM, SMEM, VMEM, VMEM],
     )
     second, *sides = call(
-        smooth_kernel, "smooth", [fine, *faces], residual_in, *exchange(*sides, table, FINE), scratch=[fine_ghosts]
+        smooth_kernel, [fine, *faces], residual_in, *exchange(FINE, *sides, table), scratch=[fine_ghosts]
     )
     defect, rhs, *sides = call(
-        defect_kernel, "defect", [fine, coarse, *coarse_faces],
-        residual_in, second, *exchange(*sides, table, FINE), scratch=[fine_ghosts, scratch(128), scratch(64)],
+        defect_kernel, [fine, coarse, *coarse_faces],
+        residual_in, second, *exchange(FINE, *sides, table), scratch=[fine_ghosts, scratch(128), scratch(64)],
     )
     correction, *sides = call(
-        coarse_kernel, "coarse", [coarse, *coarse_faces],
-        rhs, *exchange(*sides, table, COARSE), scratch=[coarse_ghosts] + [scratch(64)] * 4,
+        coarse_kernel, [coarse, *coarse_faces],
+        rhs, *exchange(COARSE, *sides, table), scratch=[coarse_ghosts] + [scratch(64)] * 4,
     )
     direction, *sides = call(
-        correct_kernel, "correct", [fine, *faces],
-        second, defect, correction, *exchange(*sides, table, COARSE),
+        correct_kernel, [fine, *faces],
+        second, defect, correction, *exchange(COARSE, *sides, table),
         scratch=[coarse_ghosts, scratch(128), scratch(128), scratch(512)],
     )
     image, sums = call(
-        image_kernel, "image", [fine, f32(lax.axis_size("inner"), 1, LANES)],
-        residual_in, direction, *exchange(*sides, table, FINE), scratch=[fine_ghosts],
+        image_kernel, [fine, f32(lax.axis_size("inner"), 1, LANES)],
+        residual_in, direction, *exchange(FINE, *sides, table), scratch=[fine_ghosts],
     )
     received = lax.all_to_all(sums, "inner", 0, 0, tiled=True)
-    (sums,) = call(add_kernel, "add", [f32(lax.axis_size("outer"), 1, LANES)], received)
+    (sums,) = call(add_kernel, [f32(lax.axis_size("outer"), 1, LANES)], received)
     received = lax.all_to_all(sums, "outer", 0, 0, tiled=True)
-    solved, left, norm = call(
-        finish_kernel, "finish", [fine, fine, f32(8, LANES)], received, residual_in, direction, image
-    )
+    solved, left, norm = call(finish_kernel, [fine, fine, f32(8, LANES)], received, residual_in, direction, image)
     return solved, left, norm[0, 0]
 
 
@@ -390,7 +386,7 @@
     devices = mesh.devices.reshape(-1, GROUP)
     split = Mesh(devices, AXES)
     return jax.shard_map(
-        local,
+        step,
         mesh=split,
         in_specs=(P(None, AXES), P(), P(None, AXES)),
         out_specs=(P(None, AXES), P(None, AXES), P()),

time: 187 us -> 187 us (level)
  no operation moved by 1% of the time
where the time goes in v3:
time: 187 us; the launch traced here: 186 us
  starting transfers between devices  88.4 us (47%)
  blocking collectives  55.6 us (30%)
  waiting for transfers between devices  34.1 us (18%)
  Pallas kernels  4.58 us (2%)
  local copies, waits for them, and re-layouts  2.15 us (1%)
    ppermute x20, starting transfers between devices, swap(): return lax.ppermute(block, AXES, route)  88.4 us
    all_to_all x1, blocking collectives, step(): received = lax.all_to_all(sums, 'outer', 0, 0, tiled=True)  43.7 us
    ppermute x20, waiting for transfers between devices, swap(): return lax.ppermute(block, AXES, route)  34.1 us
    all_to_all x1, blocking collectives, step(): received = lax.all_to_all(sums, 'inner', 0, 0, tiled=True)  11.9 us
    pallas_call x13, Pallas kernels, call(): pl.pallas_call(kernel, out_shape=outs, in_specs=in_specs or [VMEM] * len(...  4.58 us
  transfers between devices with their start and end apart: 20, of which 11 were waited for; matrix products, arithmetic and copies ran while one was open for 0% of the time, Pallas kernels for 0%

profile of v3, /device:TPU:1, one launch (start us, length us, event | category | flops | bytes accessed | tf_op | source)
XLA Modules:
  0.0 185.8 jit_solution(14877513684946597871)
XLA Ops:
  2.9 4.0 %collective-permute-start = (f32[192,128]{1,0:T(8,128)S(1)}, f32[192,128]{1,0:T(8,128)S(1)}, u32[]{:S(2)}, u32[]{:S(2)}) collective-permute-start(f32[192,128]{1,0:T(8,128)S(1)} %get-tuple-element.48), channel_id=1, source_target_pairs={{0,1},{1,0},{2,3},{3,2},{4,5},{5,4},{6,7},{7,6},{8,9},{9,8},{10,11... | collective-permute-start | bytes 294920 | tf_op jit(solution)/shard_map/ppermute | solution.py:331
  7.0 5.7 %collective-permute-start.1 = (f32[192,128]{1,0:T(8,128)S(1)}, f32[192,128]{1,0:T(8,128)S(1)}, u32[]{:S(2)}, u32[]{:S(2)}) collective-permute-start(f32[192,128]{1,0:T(8,128)S(1)} %get-tuple-element.49), channel_id=1, source_target_pairs={{1,2},{2,1},{3,4},{4,3},{5,6},{6,5},{7,8},{8,7},{9,10},{10,9},{11,... | collective-permute-start | bytes 294920 | tf_op jit(solution)/shard_map/ppermute | solution.py:331
  12.7 3.0 %collective-permute-done.1.near_outer.refs_3_ = f32[192,128]{1,0:T(8,128)S(1)} collective-permute-done((f32[192,128]{1,0:T(8,128)S(1)}, f32[192,128]{1,0:T(8,128)S(1)}, u32[]{:S(2)}, u32[]{:S(2)}) %collective-permute-start.1) | collective-permute-done | bytes 98336 | tf_op jit(solution)/shard_map/ppermute | solution.py:331
  15.9 1.9 %collective-permute-start.2 = (f32[288,128]{1,0:T(8,128)S(1)}, f32[288,128]{1,0:T(8,128)S(1)}, u32[]{:S(2)}, u32[]{:S(2)}) collective-permute-start(f32[288,128]{1,0:T(8,128)S(1)} %get-tuple-element.51), channel_id=1, source_target_pairs={{0,2},{2,0},{1,3},{3,1},{4,6},{6,4},{5,7},{7,5},{8,10},{10,8},{9,1... | collective-permute-start | bytes 442376 | tf_op jit(solution)/shard_map/ppermute | solution.py:331
  17.8 7.0 %collective-permute-start.3 = (f32[288,128]{1,0:T(8,128)S(1)}, f32[288,128]{1,0:T(8,128)S(1)}, u32[]{:S(2)}, u32[]{:S(2)}) collective-permute-start(f32[288,128]{1,0:T(8,128)S(1)} %get-tuple-element.52), channel_id=1, source_target_pairs={{2,4},{4,2},{3,5},{5,3},{6,8},{8,6},{7,9},{9,7},{10,12},{12,10},{1... | collective-permute-start | bytes 442376 | tf_op jit(solution)/shard_map/ppermute | solution.py:331
  24.8 6.6 %collective-permute-done.3.refs_5_ = f32[288,128]{1,0:T(8,128)S(1)} collective-permute-done((f32[288,128]{1,0:T(8,128)S(1)}, f32[288,128]{1,0:T(8,128)S(1)}, u32[]{:S(2)}, u32[]{:S(2)}) %collective-permute-start.3) | collective-permute-done | bytes 147488 | tf_op jit(solution)/shard_map/ppermute | solution.py:331
  33.9 6.8 %collective-permute-start.5 = (f32[192,128]{1,0:T(8,128)S(1)}, f32[192,128]{1,0:T(8,128)S(1)}, u32[]{:S(2)}, u32[]{:S(2)}) collective-permute-start(f32[192,128]{1,0:T(8,128)S(1)} %get-tuple-element.57), channel_id=1, source_target_pairs={{1,2},{2,1},{3,4},{4,3},{5,6},{6,5},{7,8},{8,7},{9,10},{10,9},{11,... | collective-permute-start | bytes 294920 | tf_op jit(solution)/shard_map/ppermute | solution.py:331
  40.7 2.3 %collective-permute-done.5.near_outer.refs_3_ = f32[192,128]{1,0:T(8,128)S(1)} collective-permute-done((f32[192,128]{1,0:T(8,128)S(1)}, f32[192,128]{1,0:T(8,128)S(1)}, u32[]{:S(2)}, u32[]{:S(2)}) %collective-permute-start.5) | collective-permute-done | bytes 98336 | tf_op jit(solution)/shard_map/ppermute | solution.py:331
  45.1 8.6 %collective-permute-start.7 = (f32[288,128]{1,0:T(8,128)S(1)}, f32[288,128]{1,0:T(8,128)S(1)}, u32[]{:S(2)}, u32[]{:S(2)}) collective-permute-start(f32[288,128]{1,0:T(8,128)S(1)} %get-tuple-element.59), channel_id=1, source_target_pairs={{2,4},{4,2},{3,5},{5,3},{6,8},{8,6},{7,9},{9,7},{10,12},{12,10},{1... | collective-permute-start | bytes 442376 | tf_op jit(solution)/shard_map/ppermute | solution.py:331
  53.7 5.2 %collective-permute-done.7.refs_5_ = f32[288,128]{1,0:T(8,128)S(1)} collective-permute-done((f32[288,128]{1,0:T(8,128)S(1)}, f32[288,128]{1,0:T(8,128)S(1)}, u32[]{:S(2)}, u32[]{:S(2)}) %collective-permute-start.7) | collective-permute-done | bytes 147488 | tf_op jit(solution)/shard_map/ppermute | solution.py:331
  59.5 2.4 %collective-permute-start.8 = (f32[48,128]{1,0:T(8,128)S(1)}, f32[48,128]{1,0:T(8,128)S(1)}, u32[]{:S(2)}, u32[]{:S(2)}) collective-permute-start(f32[48,128]{1,0:T(8,128)S(1)} %get-tuple-element.64), channel_id=1, source_target_pairs={{0,1},{1,0},{2,3},{3,2},{4,5},{5,4},{6,7},{7,6},{8,9},{9,8},{10,11... | collective-permute-start | bytes 73736 | tf_op jit(solution)/shard_map/ppermute | solution.py:331
  61.8 6.6 %collective-permute-start.9 = (f32[48,128]{1,0:T(8,128)S(1)}, f32[48,128]{1,0:T(8,128)S(1)}, u32[]{:S(2)}, u32[]{:S(2)}) collective-permute-start(f32[48,128]{1,0:T(8,128)S(1)} %get-tuple-element.65), channel_id=1, source_target_pairs={{1,2},{2,1},{3,4},{4,3},{5,6},{6,5},{7,8},{8,7},{9,10},{10,9},{11,... | collective-permute-start | bytes 73736 | tf_op jit(solution)/shard_map/ppermute | solution.py:331
  72.1 5.2 %collective-permute-start.11 = (f32[72,128]{1,0:T(8,128)S(1)}, f32[72,128]{1,0:T(8,128)S(1)}, u32[]{:S(2)}, u32[]{:S(2)}) collective-permute-start(f32[72,128]{1,0:T(8,128)S(1)} %get-tuple-element.67), channel_id=1, source_target_pairs={{2,4},{4,2},{3,5},{5,3},{6,8},{8,6},{7,9},{9,7},{10,12},{12,10},{1... | collective-permute-start | bytes 110600 | tf_op jit(solution)/shard_map/ppermute | solution.py:331
  77.3 2.2 %collective-permute-done.11.refs_5_ = f32[72,128]{1,0:T(8,128)S(1)} collective-permute-done((f32[72,128]{1,0:T(8,128)S(1)}, f32[72,128]{1,0:T(8,128)S(1)}, u32[]{:S(2)}, u32[]{:S(2)}) %collective-permute-start.11) | collective-permute-done | bytes 36896 | tf_op jit(solution)/shard_map/ppermute | solution.py:331
  79.8 2.0 %collective-permute-start.12 = (f32[48,128]{1,0:T(8,128)S(1)}, f32[48,128]{1,0:T(8,128)S(1)}, u32[]{:S(2)}, u32[]{:S(2)}) collective-permute-start(f32[48,128]{1,0:T(8,128)S(1)} %get-tuple-element.71), channel_id=1, source_target_pairs={{0,1},{1,0},{2,3},{3,2},{4,5},{5,4},{6,7},{7,6},{8,9},{9,8},{10,11... | collective-permute-start | bytes 73736 | tf_op jit(solution)/shard_map/ppermute | solution.py:331
  81.8 5.6 %collective-permute-start.13 = (f32[48,128]{1,0:T(8,128)S(1)}, f32[48,128]{1,0:T(8,128)S(1)}, u32[]{:S(2)}, u32[]{:S(2)}) collective-permute-start(f32[48,128]{1,0:T(8,128)S(1)} %get-tuple-element.72), channel_id=1, source_target_pairs={{1,2},{2,1},{3,4},{4,3},{5,6},{6,5},{7,8},{8,7},{9,10},{10,9},{11,... | collective-permute-start | bytes 73736 | tf_op jit(solution)/shard_map/ppermute | solution.py:331
  90.9 9.3 %collective-permute-start.15 = (f32[72,128]{1,0:T(8,128)S(1)}, f32[72,128]{1,0:T(8,128)S(1)}, u32[]{:S(2)}, u32[]{:S(2)}) collective-permute-start(f32[72,128]{1,0:T(8,128)S(1)} %get-tuple-element.74), channel_id=1, source_target_pairs={{2,4},{4,2},{3,5},{5,3},{6,8},{8,6},{7,9},{9,7},{10,12},{12,10},{1... | collective-permute-start | bytes 110600 | tf_op jit(solution)/shard_map/ppermute | solution.py:331
  104.1 6.3 %collective-permute-start.17 = (f32[192,128]{1,0:T(8,128)S(1)}, f32[192,128]{1,0:T(8,128)S(1)}, u32[]{:S(2)}, u32[]{:S(2)}) collective-permute-start(f32[192,128]{1,0:T(8,128)S(1)} %get-tuple-element.79), channel_id=1, source_target_pairs={{1,2},{2,1},{3,4},{4,3},{5,6},{6,5},{7,8},{8,7},{9,10},{10,9},{11,... | collective-permute-start | bytes 294920 | tf_op jit(solution)/shard_map/ppermute | solution.py:331
  110.4 2.3 %collective-permute-done.17.near_outer.refs_3_ = f32[192,128]{1,0:T(8,128)S(1)} collective-permute-done((f32[192,128]{1,0:T(8,128)S(1)}, f32[192,128]{1,0:T(8,128)S(1)}, u32[]{:S(2)}, u32[]{:S(2)}) %collective-permute-start.17) | collective-permute-done | bytes 98336 | tf_op jit(solution)/shard_map/ppermute | solution.py:331
  112.8 1.9 %collective-permute-start.18 = (f32[288,128]{1,0:T(8,128)S(1)}, f32[288,128]{1,0:T(8,128)S(1)}, u32[]{:S(2)}, u32[]{:S(2)}) collective-permute-start(f32[288,128]{1,0:T(8,128)S(1)} %get-tuple-element.80), channel_id=1, source_target_pairs={{0,2},{2,0},{1,3},{3,1},{4,6},{6,4},{5,7},{7,5},{8,10},{10,8},{9,1... | collective-permute-start | bytes 442376 | tf_op jit(solution)/shard_map/ppermute | solution.py:331
  114.8 5.5 %collective-permute-start.19 = (f32[288,128]{1,0:T(8,128)S(1)}, f32[288,128]{1,0:T(8,128)S(1)}, u32[]{:S(2)}, u32[]{:S(2)}) collective-permute-start(f32[288,128]{1,0:T(8,128)S(1)} %get-tuple-element.81), channel_id=1, source_target_pairs={{2,4},{4,2},{3,5},{5,3},{6,8},{8,6},{7,9},{9,7},{10,12},{12,10},{1... | collective-permute-start | bytes 442376 | tf_op jit(solution)/shard_map/ppermute | solution.py:331
  122.0 6.0 %collective-permute-done.19.refs_5_ = f32[288,128]{1,0:T(8,128)S(1)} collective-permute-done((f32[288,128]{1,0:T(8,128)S(1)}, f32[288,128]{1,0:T(8,128)S(1)}, u32[]{:S(2)}, u32[]{:S(2)}) %collective-permute-start.19) | collective-permute-done | bytes 147488 | tf_op jit(solution)/shard_map/ppermute | solution.py:331
  128.6 11.9 %all_to_all.10.received = f32[16,1,128]{2,1,0:T(1,128)S(1)} all-to-all(f32[16,1,128]{2,1,0:T(1,128)S(1)} %get-tuple-element.82), channel_id=1, replica_groups=mesh['curve'=96,'level'=8] {'curve':(48)2,'level'}, dimensions={0} | all-to-all | bytes 16384 | tf_op jit(solution)/shard_map/all_to_all | solution.py:378
  140.5 43.7 %all_to_all.11.received = f32[48,1,128]{2,1,0:T(1,128)S(1)} all-to-all(f32[48,1,128]{2,1,0:T(1,128)S(1)} %shard_map.69), channel_id=1, replica_groups=mesh['curve'=96,'level'=8] {'curve':(1)48}, dimensions={0} | all-to-all | bytes 49152 | tf_op jit(solution)/shard_map/all_to_all | solution.py:380
  (38 shorter events, 22.8 us)
Async XLA Ops:
  0.6 0.7 copy-start.2
  0.6 0.7 copy-start.1
  1.3 0.9 copy-start
  2.9 9.8 %collective-permute-start = (f32[192,128]{1,0:T(8,128)S(1)}, f32[192,128]{1,0:T(8,128)S(1)}, u32[]{:S(2)}, u32[]{:S(2)}) collective-permute-start(f32[192,128]{1,0:T(8,128)S(1)} %get-tuple-element.48), channel_id=1, source_target_pairs={{0,1},{1,0},{2,3},{3,2},{4,5},{5,4},{6,7},{7,6},{8,9},{9,8},{10,11... | collective-permute-start | bytes 294920 | tf_op jit(solution)/shard_map/ppermute | solution.py:331
  7.0 8.7 %collective-permute-start.1 = (f32[192,128]{1,0:T(8,128)S(1)}, f32[192,128]{1,0:T(8,128)S(1)}, u32[]{:S(2)}, u32[]{:S(2)}) collective-permute-start(f32[192,128]{1,0:T(8,128)S(1)} %get-tuple-element.49), channel_id=1, source_target_pairs={{1,2},{2,1},{3,4},{4,3},{5,6},{6,5},{7,8},{8,7},{9,10},{10,9},{11,... | collective-permute-start | bytes 294920 | tf_op jit(solution)/shard_map/ppermute | solution.py:331
  15.9 8.9 %collective-permute-start.2 = (f32[288,128]{1,0:T(8,128)S(1)}, f32[288,128]{1,0:T(8,128)S(1)}, u32[]{:S(2)}, u32[]{:S(2)}) collective-permute-start(f32[288,128]{1,0:T(8,128)S(1)} %get-tuple-element.51), channel_id=1, source_target_pairs={{0,2},{2,0},{1,3},{3,1},{4,6},{6,4},{5,7},{7,5},{8,10},{10,8},{9,1... | collective-permute-start | bytes 442376 | tf_op jit(solution)/shard_map/ppermute | solution.py:331
  17.8 13.6 %collective-permute-start.3 = (f32[288,128]{1,0:T(8,128)S(1)}, f32[288,128]{1,0:T(8,128)S(1)}, u32[]{:S(2)}, u32[]{:S(2)}) collective-permute-start(f32[288,128]{1,0:T(8,128)S(1)} %get-tuple-element.52), channel_id=1, source_target_pairs={{2,4},{4,2},{3,5},{5,3},{6,8},{8,6},{7,9},{9,7},{10,12},{12,10},{1... | collective-permute-start | bytes 442376 | tf_op jit(solution)/shard_map/ppermute | solution.py:331
  32.0 8.7 %collective-permute-start.4 = (f32[192,128]{1,0:T(8,128)S(1)}, f32[192,128]{1,0:T(8,128)S(1)}, u32[]{:S(2)}, u32[]{:S(2)}) collective-permute-start(f32[192,128]{1,0:T(8,128)S(1)} %get-tuple-element.56), channel_id=1, source_target_pairs={{0,1},{1,0},{2,3},{3,2},{4,5},{5,4},{6,7},{7,6},{8,9},{9,8},{10,11... | collective-permute-start | bytes 294920 | tf_op jit(solution)/shard_map/ppermute | solution.py:331
  33.9 9.1 %collective-permute-start.5 = (f32[192,128]{1,0:T(8,128)S(1)}, f32[192,128]{1,0:T(8,128)S(1)}, u32[]{:S(2)}, u32[]{:S(2)}) collective-permute-start(f32[192,128]{1,0:T(8,128)S(1)} %get-tuple-element.57), channel_id=1, source_target_pairs={{1,2},{2,1},{3,4},{4,3},{5,6},{6,5},{7,8},{8,7},{9,10},{10,9},{11,... | collective-permute-start | bytes 294920 | tf_op jit(solution)/shard_map/ppermute | solution.py:331
  43.2 10.5 %collective-permute-start.6 = (f32[288,128]{1,0:T(8,128)S(1)}, f32[288,128]{1,0:T(8,128)S(1)}, u32[]{:S(2)}, u32[]{:S(2)}) collective-permute-start(f32[288,128]{1,0:T(8,128)S(1)} %get-tuple-element.58), channel_id=1, source_target_pairs={{0,2},{2,0},{1,3},{3,1},{4,6},{6,4},{5,7},{7,5},{8,10},{10,8},{9,1... | collective-permute-start | bytes 442376 | tf_op jit(solution)/shard_map/ppermute | solution.py:331
  45.1 13.8 %collective-permute-start.7 = (f32[288,128]{1,0:T(8,128)S(1)}, f32[288,128]{1,0:T(8,128)S(1)}, u32[]{:S(2)}, u32[]{:S(2)}) collective-permute-start(f32[288,128]{1,0:T(8,128)S(1)} %get-tuple-element.59), channel_id=1, source_target_pairs={{2,4},{4,2},{3,5},{5,3},{6,8},{8,6},{7,9},{9,7},{10,12},{12,10},{1... | collective-permute-start | bytes 442376 | tf_op jit(solution)/shard_map/ppermute | solution.py:331
  59.5 9.0 %collective-permute-start.8 = (f32[48,128]{1,0:T(8,128)S(1)}, f32[48,128]{1,0:T(8,128)S(1)}, u32[]{:S(2)}, u32[]{:S(2)}) collective-permute-start(f32[48,128]{1,0:T(8,128)S(1)} %get-tuple-element.64), channel_id=1, source_target_pairs={{0,1},{1,0},{2,3},{3,2},{4,5},{5,4},{6,7},{7,6},{8,9},{9,8},{10,11... | collective-permute-start | bytes 73736 | tf_op jit(solution)/shard_map/ppermute | solution.py:331
  61.8 8.2 %collective-permute-start.9 = (f32[48,128]{1,0:T(8,128)S(1)}, f32[48,128]{1,0:T(8,128)S(1)}, u32[]{:S(2)}, u32[]{:S(2)}) collective-permute-start(f32[48,128]{1,0:T(8,128)S(1)} %get-tuple-element.65), channel_id=1, source_target_pairs={{1,2},{2,1},{3,4},{4,3},{5,6},{6,5},{7,8},{8,7},{9,10},{10,9},{11,... | collective-permute-start | bytes 73736 | tf_op jit(solution)/shard_map/ppermute | solution.py:331
  70.1 7.2 %collective-permute-start.10 = (f32[72,128]{1,0:T(8,128)S(1)}, f32[72,128]{1,0:T(8,128)S(1)}, u32[]{:S(2)}, u32[]{:S(2)}) collective-permute-start(f32[72,128]{1,0:T(8,128)S(1)} %get-tuple-element.66), channel_id=1, source_target_pairs={{0,2},{2,0},{1,3},{3,1},{4,6},{6,4},{5,7},{7,5},{8,10},{10,8},{9,1... | collective-permute-start | bytes 110600 | tf_op jit(solution)/shard_map/ppermute | solution.py:331
  72.1 7.5 %collective-permute-start.11 = (f32[72,128]{1,0:T(8,128)S(1)}, f32[72,128]{1,0:T(8,128)S(1)}, u32[]{:S(2)}, u32[]{:S(2)}) collective-permute-start(f32[72,128]{1,0:T(8,128)S(1)} %get-tuple-element.67), channel_id=1, source_target_pairs={{2,4},{4,2},{3,5},{5,3},{6,8},{8,6},{7,9},{9,7},{10,12},{12,10},{1... | collective-permute-start | bytes 110600 | tf_op jit(solution)/shard_map/ppermute | solution.py:331
  79.8 7.6 %collective-permute-start.12 = (f32[48,128]{1,0:T(8,128)S(1)}, f32[48,128]{1,0:T(8,128)S(1)}, u32[]{:S(2)}, u32[]{:S(2)}) collective-permute-start(f32[48,128]{1,0:T(8,128)S(1)} %get-tuple-element.71), channel_id=1, source_target_pairs={{0,1},{1,0},{2,3},{3,2},{4,5},{5,4},{6,7},{7,6},{8,9},{9,8},{10,11... | collective-permute-start | bytes 73736 | tf_op jit(solution)/shard_map/ppermute | solution.py:331
  81.8 7.1 %collective-permute-start.13 = (f32[48,128]{1,0:T(8,128)S(1)}, f32[48,128]{1,0:T(8,128)S(1)}, u32[]{:S(2)}, u32[]{:S(2)}) collective-permute-start(f32[48,128]{1,0:T(8,128)S(1)} %get-tuple-element.72), channel_id=1, source_target_pairs={{1,2},{2,1},{3,4},{4,3},{5,6},{6,5},{7,8},{8,7},{9,10},{10,9},{11,... | collective-permute-start | bytes 73736 | tf_op jit(solution)/shard_map/ppermute | solution.py:331
  89.0 11.3 %collective-permute-start.14 = (f32[72,128]{1,0:T(8,128)S(1)}, f32[72,128]{1,0:T(8,128)S(1)}, u32[]{:S(2)}, u32[]{:S(2)}) collective-permute-start(f32[72,128]{1,0:T(8,128)S(1)} %get-tuple-element.73), channel_id=1, source_target_pairs={{0,2},{2,0},{1,3},{3,1},{4,6},{6,4},{5,7},{7,5},{8,10},{10,8},{9,1... | collective-permute-start | bytes 110600 | tf_op jit(solution)/shard_map/ppermute | solution.py:331
  90.9 11.0 %collective-permute-start.15 = (f32[72,128]{1,0:T(8,128)S(1)}, f32[72,128]{1,0:T(8,128)S(1)}, u32[]{:S(2)}, u32[]{:S(2)}) collective-permute-start(f32[72,128]{1,0:T(8,128)S(1)} %get-tuple-element.74), channel_id=1, source_target_pairs={{2,4},{4,2},{3,5},{5,3},{6,8},{8,6},{7,9},{9,7},{10,12},{12,10},{1... | collective-permute-start | bytes 110600 | tf_op jit(solution)/shard_map/ppermute | solution.py:331
  102.1 8.2 %collective-permute-start.16 = (f32[192,128]{1,0:T(8,128)S(1)}, f32[192,128]{1,0:T(8,128)S(1)}, u32[]{:S(2)}, u32[]{:S(2)}) collective-permute-start(f32[192,128]{1,0:T(8,128)S(1)} %get-tuple-element.78), channel_id=1, source_target_pairs={{0,1},{1,0},{2,3},{3,2},{4,5},{5,4},{6,7},{7,6},{8,9},{9,8},{10,11... | collective-permute-start | bytes 294920 | tf_op jit(solution)/shard_map/ppermute | solution.py:331
  104.1 8.6 %collective-permute-start.17 = (f32[192,128]{1,0:T(8,128)S(1)}, f32[192,128]{1,0:T(8,128)S(1)}, u32[]{:S(2)}, u32[]{:S(2)}) collective-permute-start(f32[192,128]{1,0:T(8,128)S(1)} %get-tuple-element.79), channel_id=1, source_target_pairs={{1,2},{2,1},{3,4},{4,3},{5,6},{6,5},{7,8},{8,7},{9,10},{10,9},{11,... | collective-permute-start | bytes 294920 | tf_op jit(solution)/shard_map/ppermute | solution.py:331
  112.8 9.2 %collective-permute-start.18 = (f32[288,128]{1,0:T(8,128)S(1)}, f32[288,128]{1,0:T(8,128)S(1)}, u32[]{:S(2)}, u32[]{:S(2)}) collective-permute-start(f32[288,128]{1,0:T(8,128)S(1)} %get-tuple-element.80), channel_id=1, source_target_pairs={{0,2},{2,0},{1,3},{3,1},{4,6},{6,4},{5,7},{7,5},{8,10},{10,8},{9,1... | collective-permute-start | bytes 442376 | tf_op jit(solution)/shard_map/ppermute | solution.py:331
  114.8 13.2 %collective-permute-start.19 = (f32[288,128]{1,0:T(8,128)S(1)}, f32[288,128]{1,0:T(8,128)S(1)}, u32[]{:S(2)}, u32[]{:S(2)}) collective-permute-start(f32[288,128]{1,0:T(8,128)S(1)} %get-tuple-element.81), channel_id=1, source_target_pairs={{2,4},{4,2},{3,5},{5,3},{6,8},{8,6},{7,9},{9,7},{10,12},{12,10},{1... | collective-permute-start | bytes 442376 | tf_op jit(solution)/shard_map/ppermute | solution.py:331

commit v4 on v3

--- a/solution.py
+++ b/solution.py
@@ -12,10 +12,11 @@
 LANES = 128
 TAIL = 64
 FINE = 192
-COARSE = 48
-GROUP = 16
+PAIR = 2
+BLOCK = 72
+REACH = 3
 GRANT = 8 * 1024 * 1024
-AXES = ("outer", "inner")
+AXES = ("outer", "pair", "row")
 RELAX_FINE = (2.0 / 3.0) / 6.0
 RELAX_COARSE = (2.0 / 3.0) / 1.5
 
@@ -28,7 +29,8 @@
 FORWARD_DOWN = 24
 UPPER_NEAR = 32
 UPPER_FAR = 40
-TABLE_ROWS = 48
+NEIGHBOUR_ROW = 48
+TABLE_ROWS = 56
 
 
 def f32(*shape):
@@ -81,14 +83,29 @@
     down[128:192, :] = values[pl.ds(0, 64, stride=8), :]
 
 
-def write_coarse_faces(values, up, down):
-    up[0:16, :] = values[48:64, :]
-    down[0:16, :] = values[0:16, :]
+def write_coarse_faces(values, at, faces, to):
+    faces[to : to + 16, :] = values[at : at + 16, :]
+    faces[to + 16 : to + 32, :] = values[at + 48 : at + 64, :]
     for x in range(4):
-        up[16 + 4 * x : 20 + 4 * x, :] = values[16 * x + 12 : 16 * x + 16, :]
-        down[16 + 4 * x : 20 + 4 * x, :] = values[16 * x : 16 * x + 4, :]
-    up[32:48, :] = values[pl.ds(3, 16, stride=4), :]
-    down[32:48, :] = values[pl.ds(0, 16, stride=4), :]
+        faces[to + 32 + 4 * x : to + 36 + 4 * x, :] = values[at + 16 * x : at + 16 * x + 4, :]
+        faces[to + 48 + 4 * x : to + 52 + 4 * x, :] = values[at + 16 * x + 12 : at + 16 * x + 16, :]
+    faces[to + 64 : to + 80, :] = values[pl.ds(at, 16, stride=4), :]
+    faces[to + 80 : to + 96, :] = values[pl.ds(at + 3, 16, stride=4), :]
+
+
+def read_coarse_ghosts(faces, block, slots, device, ghosts):
+    for face in range(6):
+        slot = jnp.broadcast_to(slots[face : face + 1, :], (8, LANES))
+        safe = jnp.maximum(slot, 0)
+        lane = safe & (LANES - 1)
+        distance = jnp.where(slot >= 0, jnp.abs(lax.shift_right_logical(safe, 7) - device), -1)
+        for step in (0, 8):
+            picked = jnp.zeros((8, LANES), jnp.float32)
+            for which in range(REACH + 1):
+                source = block - which if face % 2 == 0 else block + which
+                row = 96 * source + 16 * (face ^ 1) + step
+                picked = jnp.where(distance == which, take(faces[row : row + 8, :], lane), picked)
+            ghosts[16 * face + step : 16 * face + step + 8, :] = picked
 
 
 def windows_of(table, up, down, near_inner, near_outer, far_inner, far_outer):
@@ -157,6 +174,8 @@
     shifted = jnp.where((distance == 3) & (face % 2 == 0), offset - skipped, offset)
     table[LANE_ROW : LANE_ROW + 6, :] = jnp.clip(shifted, 0, LANES - 1)
     table[WINDOW_ROW : WINDOW_ROW + 6, :] = jnp.where(present, distance, -1)
+    table[NEIGHBOUR_ROW : NEIGHBOUR_ROW + 6, :] = neighbours_ref[...]
+    table[NEIGHBOUR_ROW + 6 : NEIGHBOUR_ROW + 8, :] = jnp.full((2, LANES), -1, jnp.int32)
     forward = jnp.maximum(counts_ref[jnp.maximum(device - 1, 0)] - TAIL, 0)
     table[FORWARD_UP : FORWARD_UP + 8, :] = (lane & (TAIL - 1)) + forward
     table[FORWARD_DOWN : FORWARD_DOWN + 8, :] = lane & (TAIL - 1)
@@ -200,7 +219,7 @@
 
 
 def defect_kernel(residual, second, *refs):
-    *faces, table, defect, coarse, out_up, out_down, out_inner, out_outer, ghosts, sums, scaled = refs
+    *faces, table, defect, block, ghosts, sums = refs
     read_ghosts(table, faces, ghosts, FINE)
     for big_x in range(4):
         for big_y in range(4):
@@ -215,40 +234,70 @@
             at = 32 * big_x + 8 * big_y
             sums[at : at + 8, :] = total
     restricted = (sums[pl.ds(0, 64, stride=2), :] + sums[pl.ds(1, 64, stride=2), :]) * 0.125
-    coarse[...] = restricted
-    scaled[...] = RELAX_COARSE * restricted
-    write_coarse_faces(scaled, out_up, out_down)
-    write_pair(table, UPPER_NEAR, out_up, out_down, out_inner, out_outer, COARSE)
-
-
-def coarse_kernel(coarse, *refs):
-    *faces, table, out, out_up, out_down, out_inner, out_outer, ghosts, low_y, high_y, low_z, high_z = refs
-    read_ghosts(table, faces, ghosts, COARSE)
+    block[0:64, :] = restricted
+    block[64:72, :] = table[NEIGHBOUR_ROW : NEIGHBOUR_ROW + 8, :].astype(jnp.float32)
+
+
+def spread_kernel(device_ref, own, across, beside_row, out):
+    column = device_ref[0] % out.shape[0]
+    odd_row = (device_ref[0] // out.shape[0]) % 2
+    for target in range(out.shape[0]):
+        out[target, 0:BLOCK, :] = own[...]
+        from_before = jnp.where(column > target, 1, 0)
+        same = jnp.full((8, LANES), jnp.where(odd_row == from_before, 1, 0), jnp.int32) > 0
+        for row in range(0, BLOCK, 8):
+            other = jnp.where(same, beside_row[row : row + 8, :], across[row : row + 8, :])
+            out[target, BLOCK + row : BLOCK + row + 8, :] = other
+
+
+def coarse_update(first, at, ghosts, low_y, high_y, low_z, high_z):
     for x in range(4):
         low_y[16 * x : 16 * x + 4, :] = ghosts[32 + 4 * x : 36 + 4 * x, :]
         high_y[16 * x + 12 : 16 * x + 16, :] = ghosts[48 + 4 * x : 52 + 4 * x, :]
     low_z[pl.ds(0, 16, stride=4), :] = ghosts[64:80, :]
     high_z[pl.ds(3, 16, stride=4), :] = ghosts[80:96, :]
-    rhs = coarse[...]
-    first = RELAX_COARSE * rhs
+    centre = first[at : at + 64, :]
     row = lax.broadcasted_iota(jnp.int32, (64, LANES), 0)
-    below_x = jnp.concatenate([ghosts[0:16, :], first[0:48, :]], axis=0)
-    above_x = jnp.concatenate([first[16:64, :], ghosts[16:32, :]], axis=0)
-    below_y = jnp.where((row & 15) < 4, low_y[...], pltpu.roll(first, 4, 0))
-    above_y = jnp.where((row & 15) >= 12, high_y[...], pltpu.roll(first, 60, 0))
-    below_z = jnp.where((row & 3) == 0, low_z[...], pltpu.roll(first, 1, 0))
-    above_z = jnp.where((row & 3) == 3, high_z[...], pltpu.roll(first, 63, 0))
+    below_x = jnp.concatenate([ghosts[0:16, :], first[at : at + 48, :]], axis=0)
+    above_x = jnp.concatenate([first[at + 16 : at + 64, :], ghosts[16:32, :]], axis=0)
+    below_y = jnp.where((row & 15) < 4, low_y[...], pltpu.roll(centre, 4, 0))
+    above_y = jnp.where((row & 15) >= 12, high_y[...], pltpu.roll(centre, 60, 0))
+    below_z = jnp.where((row & 3) == 0, low_z[...], pltpu.roll(centre, 1, 0))
+    above_z = jnp.where((row & 3) == 3, high_z[...], pltpu.roll(centre, 63, 0))
     around = ((above_x + below_x) + (above_y + below_y)) + (above_z + below_z)
-    out[...] = first + RELAX_COARSE * (rhs - (6.0 * first - around) * 0.25)
-    write_coarse_faces(out, out_up, out_down)
-    write_pair(table, UPPER_NEAR, out_up, out_down, out_inner, out_outer, COARSE)
-
-
-def correct_kernel(second, defect, coarse, *refs):
-    *faces, table, out, out_up, out_down, out_inner, out_outer, ghosts, wide, wide_ghosts, spread = refs
-    read_ghosts(table, faces, ghosts, COARSE)
-    wide[pl.ds(0, 64, stride=2), :] = coarse[...]
-    wide[pl.ds(1, 64, stride=2), :] = coarse[...]
+    return centre + (centre - RELAX_COARSE * ((6.0 * centre - around) * 0.25))
+
+
+def correct_kernel(device_ref, second, defect, received, *refs):
+    table, out, out_up, out_down, out_inner, out_outer, *scratch = refs
+    first, first_faces, slots, coarse, coarse_faces, ghosts, low_y, high_y, low_z, high_z, *scratch = scratch
+    wide, wide_ghosts, spread = scratch
+    device = device_ref[0]
+    row_length = received.shape[0]
+    column = device % row_length
+    for block in range(4 * REACH + 1):
+        place = column + (block - 2 * REACH)
+        in_row = (place >= 0) & (place < row_length)
+        sender = lax.rem(place + row_length, row_length)
+        start = jnp.where(in_row, 0, BLOCK)
+        for row in range(0, 64, 8):
+            at = pl.multiple_of(start + row, 8)
+            first[64 * block + row : 64 * block + row + 8, :] = RELAX_COARSE * received[sender, pl.ds(at, 8), :]
+        write_coarse_faces(first, 64 * block, first_faces, 96 * block)
+        if REACH <= block <= 3 * REACH:
+            at = pl.multiple_of(start + 64, 8)
+            to = 8 * (block - REACH)
+            slots[to : to + 8, :] = received[sender, pl.ds(at, 8), :].astype(jnp.int32)
+    for block in range(2 * REACH + 1):
+        block_slots = slots.at[8 * block : 8 * block + 8, :]
+        read_coarse_ghosts(first_faces, block + REACH, block_slots, device + (block - REACH), ghosts)
+        updated = coarse_update(first, 64 * (block + REACH), ghosts, low_y, high_y, low_z, high_z)
+        coarse[64 * block : 64 * block + 64, :] = updated
+        write_coarse_faces(coarse, 64 * block, coarse_faces, 96 * block)
+    read_coarse_ghosts(coarse_faces, REACH, slots.at[8 * REACH : 8 * REACH + 8, :], device, ghosts)
+    own = coarse[64 * REACH : 64 * REACH + 64, :]
+    wide[pl.ds(0, 64, stride=2), :] = own
+    wide[pl.ds(1, 64, stride=2), :] = own
     wide_ghosts[pl.ds(0, 64, stride=2), :] = ghosts[0:64, :]
     wide_ghosts[pl.ds(1, 64, stride=2), :] = ghosts[0:64, :]
     for x in range(8):
@@ -331,6 +380,17 @@
     return lax.ppermute(block, AXES, route)
 
 
+def share(block, device):
+    row_length = lax.axis_size("row")
+    across = swap(block, row_length, row_length)
+    beside_row = swap(block, row_length, 0)
+    (blocks,) = call(
+        spread_kernel, [f32(row_length, 2 * BLOCK, LANES)], device, block, across, beside_row,
+        in_specs=[SMEM, VMEM, VMEM, VMEM],
+    )
+    return lax.all_to_all(blocks, "row", 0, 0, tiled=True)
+
+
 def exchange(rows, up, down, inner, outer, table):
     near_outer = swap(outer, 1, 1)
     near_inner = swap(inner, 1, 0)
@@ -345,10 +405,7 @@
     device = lax.axis_index(AXES).astype(jnp.int32).reshape(1)
     fine = f32(512, LANES)
     faces = [f32(FINE, LANES)] * 4
-    coarse = f32(64, LANES)
-    coarse_faces = [f32(COARSE, LANES)] * 4
     fine_ghosts = pltpu.VMEM((2 * FINE, LANES), jnp.float32)
-    coarse_ghosts = pltpu.VMEM((2 * COARSE, LANES), jnp.float32)
     scratch = lambda rows: pltpu.VMEM((rows, LANES), jnp.float32)
 
     residual_in, *sides, table = call(
@@ -358,24 +415,25 @@
     second, *sides = call(
         smooth_kernel, [fine, *faces], residual_in, *exchange(FINE, *sides, table), scratch=[fine_ghosts]
     )
-    defect, rhs, *sides = call(
-        defect_kernel, [fine, coarse, *coarse_faces],
-        residual_in, second, *exchange(FINE, *sides, table), scratch=[fine_ghosts, scratch(128), scratch(64)],
-    )
-    correction, *sides = call(
-        coarse_kernel, [coarse, *coarse_faces],
-        rhs, *exchange(COARSE, *sides, table), scratch=[coarse_ghosts] + [scratch(64)] * 4,
-    )
+    defect, block = call(
+        defect_kernel, [fine, f32(BLOCK, LANES)],
+        residual_in, second, *exchange(FINE, *sides, table), scratch=[fine_ghosts, scratch(128)],
+    )
+    blocks = 2 * REACH + 1
     direction, *sides = call(
-        correct_kernel, [fine, *faces],
-        second, defect, correction, *exchange(COARSE, *sides, table),
-        scratch=[coarse_ghosts, scratch(128), scratch(128), scratch(512)],
+        correct_kernel, [fine, *faces], device, second, defect, share(block, device), table,
+        in_specs=[SMEM] + [VMEM] * 4,
+        scratch=[
+            scratch(64 * (4 * REACH + 1)), scratch(96 * (4 * REACH + 1)), pltpu.VMEM((8 * blocks, LANES), jnp.int32),
+            scratch(64 * blocks), scratch(96 * blocks), scratch(96), *[scratch(64)] * 4,
+            scratch(128), scratch(128), scratch(512),
+        ],
     )
     image, sums = call(
-        image_kernel, [fine, f32(lax.axis_size("inner"), 1, LANES)],
+        image_kernel, [fine, f32(lax.axis_size(AXES[1:]), 1, LANES)],
         residual_in, direction, *exchange(FINE, *sides, table), scratch=[fine_ghosts],
     )
-    received = lax.all_to_all(sums, "inner", 0, 0, tiled=True)
+    received = lax.all_to_all(sums, AXES[1:], 0, 0, tiled=True)
     (sums,) = call(add_kernel, [f32(lax.axis_size("outer"), 1, LANES)], received)
     received = lax.all_to_all(sums, "outer", 0, 0, tiled=True)
     solved, left, norm = call(finish_kernel, [fine, fine, f32(8, LANES)], received, residual_in, direction, image)
@@ -383,7 +441,7 @@
 
 
 def solution(mesh):
-    devices = mesh.devices.reshape(-1, GROUP)
+    devices = mesh.devices.reshape(-1, PAIR, mesh.shape["level"])
     split = Mesh(devices, AXES)
     return jax.shard_map(
         step,

time: 187 us -> 164 us (0.88)
  starting transfers between devices: 88.4 us -> 50.1 us
  blocking collectives: 55.6 us -> 71.9 us
    ppermute x20 -> x14, starting transfers between devices: 88.4 us -> 50.1 us  [swap(): return lax.ppermute(block, AXES, route)]
    all_to_all x1 -> x2, blocking collectives: 11.9 us -> 36.3 us  [the longest x1 21.6 us: share(): return lax.all_to_all(blocks, 'row', 0, 0, tiled=True)]
    all_to_all x1, blocking collectives: 43.7 us -> 35.6 us  [step(): received = lax.all_to_all(sums, 'outer', 0, 0, tiled=True)]
    ppermute x20 -> x14, waiting for transfers between devices: 34.1 us -> 33 us  [swap(): return lax.ppermute(block, AXES, route)]
    pallas_call x13 -> x11, Pallas kernels: 4.58 us -> 4.91 us  [call(): pl.pallas_call(kernel, out_shape=outs, in_specs=in_specs or [VMEM] * len(...]
  transfers between devices with their start and end apart: 20 -> 14, of which waited for: 11 -> 9; matrix products, arithmetic and copies ran while one was open for 0% -> 0% of each run, Pallas kernels for 0% -> 0%
where the time goes in v4:
time: 164 us; the launch traced here: 163 us
  blocking collectives  71.9 us (44%)
  starting transfers between devices  50.1 us (31%)
  waiting for transfers between devices  33 us (20%)
  Pallas kernels  4.91 us (3%)
  local copies, waits for them, and re-layouts  2.15 us (1%)
    ppermute x14, starting transfers between devices, swap(): return lax.ppermute(block, AXES, route)  50.1 us
    all_to_all x1, blocking collectives, step(): received = lax.all_to_all(sums, 'outer', 0, 0, tiled=True)  35.6 us
    ppermute x14, waiting for transfers between devices, swap(): return lax.ppermute(block, AXES, route)  33 us
    all_to_all x1, blocking collectives, share(): return lax.all_to_all(blocks, 'row', 0, 0, tiled=True)  21.6 us
    all_to_all x1, blocking collectives, step(): received = lax.all_to_all(sums, AXES[1:], 0, 0, tiled=True)  14.7 us
    pallas_call x11, Pallas kernels, call(): pl.pallas_call(kernel, out_shape=outs, in_specs=in_specs or [VMEM] * len(...  4.91 us
  transfers between devices with their start and end apart: 14, of which 9 were waited for; matrix products, arithmetic and copies ran while one was open for 0% of the time, Pallas kernels for 0%

profile of v4, /device:TPU:1, one launch (start us, length us, event | category | flops | bytes accessed | tf_op | source)
XLA Modules:
  0.0 162.9 jit_solution(14157560893385798432)
XLA Ops:
  2.9 4.0 %collective-permute-start = (f32[192,128]{1,0:T(8,128)S(1)}, f32[192,128]{1,0:T(8,128)S(1)}, u32[]{:S(2)}, u32[]{:S(2)}) collective-permute-start(f32[192,128]{1,0:T(8,128)S(1)} %get-tuple-element.35), channel_id=1, source_target_pairs={{0,1},{1,0},{2,3},{3,2},{4,5},{5,4},{6,7},{7,6},{8,9},{9,8},{10,11... | collective-permute-start | bytes 294920 | tf_op jit(solution)/shard_map/ppermute | solution.py:380
  7.0 5.7 %collective-permute-start.1 = (f32[192,128]{1,0:T(8,128)S(1)}, f32[192,128]{1,0:T(8,128)S(1)}, u32[]{:S(2)}, u32[]{:S(2)}) collective-permute-start(f32[192,128]{1,0:T(8,128)S(1)} %get-tuple-element.36), channel_id=1, source_target_pairs={{1,2},{2,1},{3,4},{4,3},{5,6},{6,5},{7,8},{8,7},{9,10},{10,9},{11,... | collective-permute-start | bytes 294920 | tf_op jit(solution)/shard_map/ppermute | solution.py:380
  12.7 3.0 %collective-permute-done.1.near_outer.refs_3_ = f32[192,128]{1,0:T(8,128)S(1)} collective-permute-done((f32[192,128]{1,0:T(8,128)S(1)}, f32[192,128]{1,0:T(8,128)S(1)}, u32[]{:S(2)}, u32[]{:S(2)}) %collective-permute-start.1) | collective-permute-done | bytes 98336 | tf_op jit(solution)/shard_map/ppermute | solution.py:380
  15.9 1.9 %collective-permute-start.2 = (f32[288,128]{1,0:T(8,128)S(1)}, f32[288,128]{1,0:T(8,128)S(1)}, u32[]{:S(2)}, u32[]{:S(2)}) collective-permute-start(f32[288,128]{1,0:T(8,128)S(1)} %get-tuple-element.38), channel_id=1, source_target_pairs={{0,2},{2,0},{1,3},{3,1},{4,6},{6,4},{5,7},{7,5},{8,10},{10,8},{9,1... | collective-permute-start | bytes 442376 | tf_op jit(solution)/shard_map/ppermute | solution.py:380
  17.8 7.0 %collective-permute-start.3 = (f32[288,128]{1,0:T(8,128)S(1)}, f32[288,128]{1,0:T(8,128)S(1)}, u32[]{:S(2)}, u32[]{:S(2)}) collective-permute-start(f32[288,128]{1,0:T(8,128)S(1)} %get-tuple-element.39), channel_id=1, source_target_pairs={{2,4},{4,2},{3,5},{5,3},{6,8},{8,6},{7,9},{9,7},{10,12},{12,10},{1... | collective-permute-start | bytes 442376 | tf_op jit(solution)/shard_map/ppermute | solution.py:380
  24.8 6.6 %collective-permute-done.3.refs_5_ = f32[288,128]{1,0:T(8,128)S(1)} collective-permute-done((f32[288,128]{1,0:T(8,128)S(1)}, f32[288,128]{1,0:T(8,128)S(1)}, u32[]{:S(2)}, u32[]{:S(2)}) %collective-permute-start.3) | collective-permute-done | bytes 147488 | tf_op jit(solution)/shard_map/ppermute | solution.py:380
  31.9 1.9 %collective-permute-start.4 = (f32[192,128]{1,0:T(8,128)S(1)}, f32[192,128]{1,0:T(8,128)S(1)}, u32[]{:S(2)}, u32[]{:S(2)}) collective-permute-start(f32[192,128]{1,0:T(8,128)S(1)} %get-tuple-element.43), channel_id=1, source_target_pairs={{0,1},{1,0},{2,3},{3,2},{4,5},{5,4},{6,7},{7,6},{8,9},{9,8},{10,11... | collective-permute-start | bytes 294920 | tf_op jit(solution)/shard_map/ppermute | solution.py:380
  33.9 6.8 %collective-permute-start.5 = (f32[192,128]{1,0:T(8,128)S(1)}, f32[192,128]{1,0:T(8,128)S(1)}, u32[]{:S(2)}, u32[]{:S(2)}) collective-permute-start(f32[192,128]{1,0:T(8,128)S(1)} %get-tuple-element.44), channel_id=1, source_target_pairs={{1,2},{2,1},{3,4},{4,3},{5,6},{6,5},{7,8},{8,7},{9,10},{10,9},{11,... | collective-permute-start | bytes 294920 | tf_op jit(solution)/shard_map/ppermute | solution.py:380
  40.7 2.3 %collective-permute-done.5.near_outer.refs_3_ = f32[192,128]{1,0:T(8,128)S(1)} collective-permute-done((f32[192,128]{1,0:T(8,128)S(1)}, f32[192,128]{1,0:T(8,128)S(1)}, u32[]{:S(2)}, u32[]{:S(2)}) %collective-permute-start.5) | collective-permute-done | bytes 98336 | tf_op jit(solution)/shard_map/ppermute | solution.py:380
  43.2 1.9 %collective-permute-start.6 = (f32[288,128]{1,0:T(8,128)S(1)}, f32[288,128]{1,0:T(8,128)S(1)}, u32[]{:S(2)}, u32[]{:S(2)}) collective-permute-start(f32[288,128]{1,0:T(8,128)S(1)} %get-tuple-element.45), channel_id=1, source_target_pairs={{0,2},{2,0},{1,3},{3,1},{4,6},{6,4},{5,7},{7,5},{8,10},{10,8},{9,1... | collective-permute-start | bytes 442376 | tf_op jit(solution)/shard_map/ppermute | solution.py:380
  45.1 8.6 %collective-permute-start.7 = (f32[288,128]{1,0:T(8,128)S(1)}, f32[288,128]{1,0:T(8,128)S(1)}, u32[]{:S(2)}, u32[]{:S(2)}) collective-permute-start(f32[288,128]{1,0:T(8,128)S(1)} %get-tuple-element.46), channel_id=1, source_target_pairs={{2,4},{4,2},{3,5},{5,3},{6,8},{8,6},{7,9},{9,7},{10,12},{12,10},{1... | collective-permute-start | bytes 442376 | tf_op jit(solution)/shard_map/ppermute | solution.py:380
  53.7 5.2 %collective-permute-done.7.refs_5_ = f32[288,128]{1,0:T(8,128)S(1)} collective-permute-done((f32[288,128]{1,0:T(8,128)S(1)}, f32[288,128]{1,0:T(8,128)S(1)}, u32[]{:S(2)}, u32[]{:S(2)}) %collective-permute-start.7) | collective-permute-done | bytes 147488 | tf_op jit(solution)/shard_map/ppermute | solution.py:380
  59.4 1.9 %collective-permute-start.9 = (f32[72,128]{1,0:T(8,128)S(1)}, f32[72,128]{1,0:T(8,128)S(1)}, u32[]{:S(2)}, u32[]{:S(2)}) collective-permute-start(f32[72,128]{1,0:T(8,128)S(1)} %get-tuple-element.48.own), channel_id=1, source_target_pairs={{0,8},{8,0},{1,9},{9,1},{2,10},{10,2},{3,11},{11,3},{4,12},{12,4},... | collective-permute-start | bytes 110600 | tf_op jit(solution)/shard_map/ppermute | solution.py:380
  63.3 3.3 %collective-permute-done.8.across = f32[72,128]{1,0:T(8,128)S(1)} collective-permute-done((f32[72,128]{1,0:T(8,128)S(1)}, f32[72,128]{1,0:T(8,128)S(1)}, u32[]{:S(2)}, u32[]{:S(2)}) %collective-permute-start.8) | collective-permute-done | bytes 36896 | tf_op jit(solution)/shard_map/ppermute | solution.py:380
  66.7 21.6 %all_to_all.15.received = f32[8,144,128]{2,1,0:T(8,128)S(1)} all-to-all(f32[8,144,128]{2,1,0:T(8,128)S(1)} %shard_map.63), channel_id=1, replica_groups=mesh['outer'=48,'pair'=2,'row'=8] {'row'}, dimensions={0} | all-to-all | bytes 1179648 | tf_op jit(solution)/shard_map/all_to_all | solution.py:391
  89.3 2.2 %collective-permute-start.10 = (f32[192,128]{1,0:T(8,128)S(1)}, f32[192,128]{1,0:T(8,128)S(1)}, u32[]{:S(2)}, u32[]{:S(2)}) collective-permute-start(f32[192,128]{1,0:T(8,128)S(1)} %get-tuple-element.52), channel_id=1, source_target_pairs={{0,1},{1,0},{2,3},{3,2},{4,5},{5,4},{6,7},{7,6},{8,9},{9,8},{10,11... | collective-permute-start | bytes 294920 | tf_op jit(solution)/shard_map/ppermute | solution.py:380
  91.5 1.9 %collective-permute-start.11 = (f32[192,128]{1,0:T(8,128)S(1)}, f32[192,128]{1,0:T(8,128)S(1)}, u32[]{:S(2)}, u32[]{:S(2)}) collective-permute-start(f32[192,128]{1,0:T(8,128)S(1)} %get-tuple-element.53), channel_id=1, source_target_pairs={{1,2},{2,1},{3,4},{4,3},{5,6},{6,5},{7,8},{8,7},{9,10},{10,9},{11,... | collective-permute-start | bytes 294920 | tf_op jit(solution)/shard_map/ppermute | solution.py:380
  94.6 4.0 %collective-permute-done.11.near_outer.refs_3_ = f32[192,128]{1,0:T(8,128)S(1)} collective-permute-done((f32[192,128]{1,0:T(8,128)S(1)}, f32[192,128]{1,0:T(8,128)S(1)}, u32[]{:S(2)}, u32[]{:S(2)}) %collective-permute-start.11) | collective-permute-done | bytes 98336 | tf_op jit(solution)/shard_map/ppermute | solution.py:380
  98.8 1.9 %collective-permute-start.12 = (f32[288,128]{1,0:T(8,128)S(1)}, f32[288,128]{1,0:T(8,128)S(1)}, u32[]{:S(2)}, u32[]{:S(2)}) collective-permute-start(f32[288,128]{1,0:T(8,128)S(1)} %get-tuple-element.54), channel_id=1, source_target_pairs={{0,2},{2,0},{1,3},{3,1},{4,6},{6,4},{5,7},{7,5},{8,10},{10,8},{9,1... | collective-permute-start | bytes 442376 | tf_op jit(solution)/shard_map/ppermute | solution.py:380
  100.7 2.4 %collective-permute-start.13 = (f32[288,128]{1,0:T(8,128)S(1)}, f32[288,128]{1,0:T(8,128)S(1)}, u32[]{:S(2)}, u32[]{:S(2)}) collective-permute-start(f32[288,128]{1,0:T(8,128)S(1)} %get-tuple-element.55), channel_id=1, source_target_pairs={{2,4},{4,2},{3,5},{5,3},{6,8},{8,6},{7,9},{9,7},{10,12},{12,10},{1... | collective-permute-start | bytes 442376 | tf_op jit(solution)/shard_map/ppermute | solution.py:380
  103.1 3.4 %collective-permute-done.12.refs_4_ = f32[288,128]{1,0:T(8,128)S(1)} collective-permute-done((f32[288,128]{1,0:T(8,128)S(1)}, f32[288,128]{1,0:T(8,128)S(1)}, u32[]{:S(2)}, u32[]{:S(2)}) %collective-permute-start.12) | collective-permute-done | bytes 147488 | tf_op jit(solution)/shard_map/ppermute | solution.py:380
  106.5 3.9 %collective-permute-done.13.refs_5_ = f32[288,128]{1,0:T(8,128)S(1)} collective-permute-done((f32[288,128]{1,0:T(8,128)S(1)}, f32[288,128]{1,0:T(8,128)S(1)}, u32[]{:S(2)}, u32[]{:S(2)}) %collective-permute-start.13) | collective-permute-done | bytes 147488 | tf_op jit(solution)/shard_map/ppermute | solution.py:380
  111.1 14.7 %all_to_all.16.received = f32[16,1,128]{2,1,0:T(1,128)S(1)} all-to-all(f32[16,1,128]{2,1,0:T(1,128)S(1)} %get-tuple-element.56), channel_id=1, replica_groups=mesh['outer'=48,'pair'=2,'row'=8] {'pair','row'}, dimensions={0} | all-to-all | bytes 16384 | tf_op jit(solution)/shard_map/all_to_all | solution.py:436
  125.8 35.6 %all_to_all.17.received = f32[48,1,128]{2,1,0:T(1,128)S(1)} all-to-all(f32[48,1,128]{2,1,0:T(1,128)S(1)} %shard_map.67), channel_id=1, replica_groups=mesh['outer'=48,'pair'=2,'row'=8] {'outer'}, dimensions={0} | all-to-all | bytes 49152 | tf_op jit(solution)/shard_map/all_to_all | solution.py:438
  (25 shorter events, 10.2 us)
Async XLA Ops:
  0.6 0.7 copy-start.2
  0.7 0.7 copy-start.1
  1.3 0.9 copy-start
  2.9 9.8 %collective-permute-start = (f32[192,128]{1,0:T(8,128)S(1)}, f32[192,128]{1,0:T(8,128)S(1)}, u32[]{:S(2)}, u32[]{:S(2)}) collective-permute-start(f32[192,128]{1,0:T(8,128)S(1)} %get-tuple-element.35), channel_id=1, source_target_pairs={{0,1},{1,0},{2,3},{3,2},{4,5},{5,4},{6,7},{7,6},{8,9},{9,8},{10,11... | collective-permute-start | bytes 294920 | tf_op jit(solution)/shard_map/ppermute | solution.py:380
  7.0 8.7 %collective-permute-start.1 = (f32[192,128]{1,0:T(8,128)S(1)}, f32[192,128]{1,0:T(8,128)S(1)}, u32[]{:S(2)}, u32[]{:S(2)}) collective-permute-start(f32[192,128]{1,0:T(8,128)S(1)} %get-tuple-element.36), channel_id=1, source_target_pairs={{1,2},{2,1},{3,4},{4,3},{5,6},{6,5},{7,8},{8,7},{9,10},{10,9},{11,... | collective-permute-start | bytes 294920 | tf_op jit(solution)/shard_map/ppermute | solution.py:380
  15.9 8.9 %collective-permute-start.2 = (f32[288,128]{1,0:T(8,128)S(1)}, f32[288,128]{1,0:T(8,128)S(1)}, u32[]{:S(2)}, u32[]{:S(2)}) collective-permute-start(f32[288,128]{1,0:T(8,128)S(1)} %get-tuple-element.38), channel_id=1, source_target_pairs={{0,2},{2,0},{1,3},{3,1},{4,6},{6,4},{5,7},{7,5},{8,10},{10,8},{9,1... | collective-permute-start | bytes 442376 | tf_op jit(solution)/shard_map/ppermute | solution.py:380
  17.8 13.6 %collective-permute-start.3 = (f32[288,128]{1,0:T(8,128)S(1)}, f32[288,128]{1,0:T(8,128)S(1)}, u32[]{:S(2)}, u32[]{:S(2)}) collective-permute-start(f32[288,128]{1,0:T(8,128)S(1)} %get-tuple-element.39), channel_id=1, source_target_pairs={{2,4},{4,2},{3,5},{5,3},{6,8},{8,6},{7,9},{9,7},{10,12},{12,10},{1... | collective-permute-start | bytes 442376 | tf_op jit(solution)/shard_map/ppermute | solution.py:380
  31.9 8.7 %collective-permute-start.4 = (f32[192,128]{1,0:T(8,128)S(1)}, f32[192,128]{1,0:T(8,128)S(1)}, u32[]{:S(2)}, u32[]{:S(2)}) collective-permute-start(f32[192,128]{1,0:T(8,128)S(1)} %get-tuple-element.43), channel_id=1, source_target_pairs={{0,1},{1,0},{2,3},{3,2},{4,5},{5,4},{6,7},{7,6},{8,9},{9,8},{10,11... | collective-permute-start | bytes 294920 | tf_op jit(solution)/shard_map/ppermute | solution.py:380
  33.9 9.1 %collective-permute-start.5 = (f32[192,128]{1,0:T(8,128)S(1)}, f32[192,128]{1,0:T(8,128)S(1)}, u32[]{:S(2)}, u32[]{:S(2)}) collective-permute-start(f32[192,128]{1,0:T(8,128)S(1)} %get-tuple-element.44), channel_id=1, source_target_pairs={{1,2},{2,1},{3,4},{4,3},{5,6},{6,5},{7,8},{8,7},{9,10},{10,9},{11,... | collective-permute-start | bytes 294920 | tf_op jit(solution)/shard_map/ppermute | solution.py:380
  43.2 10.5 %collective-permute-start.6 = (f32[288,128]{1,0:T(8,128)S(1)}, f32[288,128]{1,0:T(8,128)S(1)}, u32[]{:S(2)}, u32[]{:S(2)}) collective-permute-start(f32[288,128]{1,0:T(8,128)S(1)} %get-tuple-element.45), channel_id=1, source_target_pairs={{0,2},{2,0},{1,3},{3,1},{4,6},{6,4},{5,7},{7,5},{8,10},{10,8},{9,1... | collective-permute-start | bytes 442376 | tf_op jit(solution)/shard_map/ppermute | solution.py:380
  45.1 13.8 %collective-permute-start.7 = (f32[288,128]{1,0:T(8,128)S(1)}, f32[288,128]{1,0:T(8,128)S(1)}, u32[]{:S(2)}, u32[]{:S(2)}) collective-permute-start(f32[288,128]{1,0:T(8,128)S(1)} %get-tuple-element.46), channel_id=1, source_target_pairs={{2,4},{4,2},{3,5},{5,3},{6,8},{8,6},{7,9},{9,7},{10,12},{12,10},{1... | collective-permute-start | bytes 442376 | tf_op jit(solution)/shard_map/ppermute | solution.py:380
  59.4 3.9 %collective-permute-start.9 = (f32[72,128]{1,0:T(8,128)S(1)}, f32[72,128]{1,0:T(8,128)S(1)}, u32[]{:S(2)}, u32[]{:S(2)}) collective-permute-start(f32[72,128]{1,0:T(8,128)S(1)} %get-tuple-element.48.own), channel_id=1, source_target_pairs={{0,8},{8,0},{1,9},{9,1},{2,10},{10,2},{3,11},{11,3},{4,12},{12,4},... | collective-permute-start | bytes 110600 | tf_op jit(solution)/shard_map/ppermute | solution.py:380
  61.4 5.3 %collective-permute-start.8 = (f32[72,128]{1,0:T(8,128)S(1)}, f32[72,128]{1,0:T(8,128)S(1)}, u32[]{:S(2)}, u32[]{:S(2)}) collective-permute-start(f32[72,128]{1,0:T(8,128)S(1)} %get-tuple-element.48.own), channel_id=1, source_target_pairs={{8,16},{16,8},{9,17},{17,9},{10,18},{18,10},{11,19},{19,11},{12,20... | collective-permute-start | bytes 110600 | tf_op jit(solution)/shard_map/ppermute | solution.py:380
  89.3 5.4 %collective-permute-start.10 = (f32[192,128]{1,0:T(8,128)S(1)}, f32[192,128]{1,0:T(8,128)S(1)}, u32[]{:S(2)}, u32[]{:S(2)}) collective-permute-start(f32[192,128]{1,0:T(8,128)S(1)} %get-tuple-element.52), channel_id=1, source_target_pairs={{0,1},{1,0},{2,3},{3,2},{4,5},{5,4},{6,7},{7,6},{8,9},{9,8},{10,11... | collective-permute-start | bytes 294920 | tf_op jit(solution)/shard_map/ppermute | solution.py:380
  91.5 7.1 %collective-permute-start.11 = (f32[192,128]{1,0:T(8,128)S(1)}, f32[192,128]{1,0:T(8,128)S(1)}, u32[]{:S(2)}, u32[]{:S(2)}) collective-permute-start(f32[192,128]{1,0:T(8,128)S(1)} %get-tuple-element.53), channel_id=1, source_target_pairs={{1,2},{2,1},{3,4},{4,3},{5,6},{6,5},{7,8},{8,7},{9,10},{10,9},{11,... | collective-permute-start | bytes 294920 | tf_op jit(solution)/shard_map/ppermute | solution.py:380
  98.8 7.7 %collective-permute-start.12 = (f32[288,128]{1,0:T(8,128)S(1)}, f32[288,128]{1,0:T(8,128)S(1)}, u32[]{:S(2)}, u32[]{:S(2)}) collective-permute-start(f32[288,128]{1,0:T(8,128)S(1)} %get-tuple-element.54), channel_id=1, source_target_pairs={{0,2},{2,0},{1,3},{3,1},{4,6},{6,4},{5,7},{7,5},{8,10},{10,8},{9,1... | collective-permute-start | bytes 442376 | tf_op jit(solution)/shard_map/ppermute | solution.py:380
  100.7 9.7 %collective-permute-start.13 = (f32[288,128]{1,0:T(8,128)S(1)}, f32[288,128]{1,0:T(8,128)S(1)}, u32[]{:S(2)}, u32[]{:S(2)}) collective-permute-start(f32[288,128]{1,0:T(8,128)S(1)} %get-tuple-element.55), channel_id=1, source_target_pairs={{2,4},{4,2},{3,5},{5,3},{6,8},{8,6},{7,9},{9,7},{10,12},{12,10},{1... | collective-permute-start | bytes 442376 | tf_op jit(solution)/shard_map/ppermute | solution.py:380

commit v5 on v4

--- a/solution.py
+++ b/solution.py
@@ -30,7 +30,8 @@
 UPPER_NEAR = 32
 UPPER_FAR = 40
 NEIGHBOUR_ROW = 48
-TABLE_ROWS = 56
+CROSSES = 56
+TABLE_ROWS = 64
 
 
 def f32(*shape):
@@ -153,7 +154,7 @@
     return centre, ((above_x + below_x) + (above_y + below_y)) + (above_z + below_z)
 
 
-def start_kernel(device_ref, counts_ref, right_ref, neighbours_ref, residual, up, down, inner, outer, table):
+def start_kernel(row_length, device_ref, counts_ref, right_ref, neighbours_ref, residual, up, down, inner, outer, table):
     device = device_ref[0]
     own_count = counts_ref[device]
     lane = lax.broadcasted_iota(jnp.int32, (8, LANES), 1)
@@ -163,6 +164,9 @@
     write_faces(residual, up, down)
     table[UPPER_NEAR : UPPER_NEAR + 8, :] = jnp.full((8, LANES), device & 1, jnp.int32)
     table[UPPER_FAR : UPPER_FAR + 8, :] = jnp.full((8, LANES), device & 2, jnp.int32)
+    place = lax.rem(device, row_length)
+    crosses = jnp.where((place == 0) | (place == row_length - 1), 1, 0)
+    table[CROSSES : CROSSES + 8, :] = jnp.full((8, LANES), crosses, jnp.int32)
     write_pair(table, UPPER_NEAR, up, down, inner, outer, FINE)
     slot = neighbours_ref[...]
     present = slot >= 0
@@ -181,27 +185,39 @@
     table[FORWARD_DOWN : FORWARD_DOWN + 8, :] = lane & (TAIL - 1)
 
 
-def pack_kernel(rows, up, down, near_inner, near_outer, table, inner, outer):
+def pack(rows, flag_row, table, up, down, near_up, near_down, message):
     half = rows // 2
     lane = lax.broadcasted_iota(jnp.int32, (8, LANES), 1)
-    write_pair(table, UPPER_FAR, up, down, inner, outer, rows)
+    upper = table[UPPER_FAR : UPPER_FAR + 8, :] > 0
+    downwards = upper if flag_row else jnp.logical_not(upper)
+    lanes_up = table[FORWARD_UP : FORWARD_UP + 8, :]
+    lanes_down = table[FORWARD_DOWN : FORWARD_DOWN + 8, :]
+    lanes = jnp.where(downwards, lanes_down, lanes_up)
+    own = Chosen(downwards, down, up)
+    near = Chosen(downwards, near_down, near_up)
+    for row in range(0, rows, 8):
+        message[row : row + 8, :] = own[row : row + 8, :]
+    for row in range(0, half, 8):
+        first = take(near[row : row + 8, :], lanes)
+        second = take(near[half + row : half + row + 8, :], lanes)
+        message[rows + row : rows + row + 8, :] = jnp.where(lane < TAIL, first, second)
+
+
+def pack_outer_kernel(rows, up, down, near_inner, near_outer, table, message):
     near = table[UPPER_NEAR : UPPER_NEAR + 8, :] > 0
-    upper = table[UPPER_FAR : UPPER_FAR + 8, :] > 0
     near_up = Chosen(near, near_inner, near_outer)
     near_down = Chosen(near, near_outer, near_inner)
-
-    def packed(block, lanes, row):
-        first = take(block[row : row + 8, :], lanes)
-        second = take(block[half + row : half + row + 8, :], lanes)
-        return jnp.where(lane < TAIL, first, second)
-
-    lanes_up = table[FORWARD_UP : FORWARD_UP + 8, :]
-    lanes_down = table[FORWARD_DOWN : FORWARD_DOWN + 8, :]
-    for row in range(0, half, 8):
-        high = packed(near_up, lanes_up, row)
-        low = packed(near_down, lanes_down, row)
-        inner[rows + row : rows + row + 8, :] = jnp.where(upper, low, high)
-        outer[rows + row : rows + row + 8, :] = jnp.where(upper, high, low)
+    pack(rows, False, table, up, down, near_up, near_down, message)
+
+
+def pack_inner_kernel(rows, up, down, near_inner, near_outer, near_across, table, message, merged):
+    near = table[UPPER_NEAR : UPPER_NEAR + 8, :] > 0
+    either = Chosen(table[CROSSES : CROSSES + 8, :] > 0, near_across, near_outer)
+    for row in range(0, rows, 8):
+        merged[row : row + 8, :] = either[row : row + 8, :]
+    near_up = Chosen(near, near_inner, merged)
+    near_down = Chosen(near, merged, near_inner)
+    pack(rows, True, table, up, down, near_up, near_down, message)
 
 
 def smooth_kernel(residual, *refs):
@@ -371,13 +387,30 @@
     norm[...] = jnp.sqrt(old_square - 2.0 * step_size * cross_term + step_size * step_size * image_square)
 
 
-def swap(block, distance, offset):
+def swap(block, distance, offset, keep=lambda low: True):
     count = lax.axis_size(AXES)
     route = []
-    for low in range(offset - 2 * distance, count):
-        if low >= 0 and low + distance < count and (low - offset) % (2 * distance) < distance:
+    for low in range(count - distance):
+        if (low - offset) % (2 * distance) < distance and keep(low):
             route += [(low, low + distance), (low + distance, low)]
     return lax.ppermute(block, AXES, route)
+
+
+def exchange(rows, up, down, inner, outer, table):
+    row_length = lax.axis_size("row")
+    crosses = lambda low: low % row_length == row_length - 1
+    message = f32(rows + rows // 2, LANES)
+    near_outer = swap(outer, 1, 1, lambda low: not crosses(low))
+    near_inner = swap(inner, 1, 0)
+    near_across = swap(outer, 1, 1, crosses)
+    (outer,) = call(functools.partial(pack_outer_kernel, rows), [message], up, down, near_inner, near_outer, table)
+    far_outer = swap(outer, 2, 2)
+    inner, near_outer = call(
+        functools.partial(pack_inner_kernel, rows), [message, f32(rows, LANES)],
+        up, down, near_inner, near_outer, near_across, table,
+    )
+    far_inner = swap(inner, 2, 0)
+    return up, down, near_inner, near_outer, far_inner, far_outer, table
 
 
 def share(block, device):
@@ -391,16 +424,6 @@
     return lax.all_to_all(blocks, "row", 0, 0, tiled=True)
 
 
-def exchange(rows, up, down, inner, outer, table):
-    near_outer = swap(outer, 1, 1)
-    near_inner = swap(inner, 1, 0)
-    message = f32(rows + rows // 2, LANES)
-    inner, outer = call(functools.partial(pack_kernel, rows), [message] * 2, up, down, near_inner, near_outer, table)
-    far_outer = swap(outer, 2, 2)
-    far_inner = swap(inner, 2, 0)
-    return up, down, near_inner, near_outer, far_inner, far_outer, table
-
-
 def step(right_side, counts, neighbours):
     device = lax.axis_index(AXES).astype(jnp.int32).reshape(1)
     fine = f32(512, LANES)
@@ -409,7 +432,7 @@
     scratch = lambda rows: pltpu.VMEM((rows, LANES), jnp.float32)
 
     residual_in, *sides, table = call(
-        start_kernel, [fine, *faces, i32(TABLE_ROWS, LANES)], device, counts, right_side, neighbours,
+        functools.partial(start_kernel, lax.axis_size("row")), [fine, *faces, i32(TABLE_ROWS, LANES)], device, counts, right_side, neighbours,
         in_specs=[SMEM, SMEM, VMEM, VMEM],
     )
     second, *sides = call(

time: 164 us -> 164 us (level)
  starting transfers between devices: 50.1 us -> 53.6 us
  blocking collectives: 71.9 us -> 69.7 us
    ppermute x14 -> x17, starting transfers between devices: 50.1 us -> 53.6 us  [swap(): return lax.ppermute(block, AXES, route)]
    ppermute x14 -> x17, waiting for transfers between devices: 33 us -> 31.7 us  [swap(): return lax.ppermute(block, AXES, route)]
    pallas_call x11 -> x14, Pallas kernels: 4.91 us -> 5.02 us  [call(): pl.pallas_call(kernel, out_shape=outs, in_specs=in_specs or [VMEM] * len(...]
  transfers between devices with their start and end apart: 14 -> 17, of which waited for: 9 -> 9; matrix products, arithmetic and copies ran while one was open for 0% -> 0% of each run, Pallas kernels for 0% -> 0%
where the time goes in v5:
time: 164 us; the launch traced here: 163 us
  blocking collectives  69.7 us (42%)
  starting transfers between devices  53.6 us (33%)
  waiting for transfers between devices  31.7 us (19%)
  Pallas kernels  5.02 us (3%)
  local copies, waits for them, and re-layouts  2.15 us (1%)
    ppermute x17, starting transfers between devices, swap(): return lax.ppermute(block, AXES, route)  53.6 us
    all_to_all x1, blocking collectives, step(): received = lax.all_to_all(sums, 'outer', 0, 0, tiled=True)  34.3 us
    ppermute x17, waiting for transfers between devices, swap(): return lax.ppermute(block, AXES, route)  31.7 us
    all_to_all x1, blocking collectives, share(): return lax.all_to_all(blocks, 'row', 0, 0, tiled=True)  21.6 us
    all_to_all x1, blocking collectives, step(): received = lax.all_to_all(sums, AXES[1:], 0, 0, tiled=True)  13.8 us
    pallas_call x14, Pallas kernels, call(): pl.pallas_call(kernel, out_shape=outs, in_specs=in_specs or [VMEM] * len(...  5.02 us
  transfers between devices with their start and end apart: 17, of which 9 were waited for; matrix products, arithmetic and copies ran while one was open for 0% of the time, Pallas kernels for 0%

profile of v5, /device:TPU:1, one launch (start us, length us, event | category | flops | bytes accessed | tf_op | source)
XLA Modules:
  0.0 163.1 jit_solution(10439667937351086013)
XLA Ops:
  2.9 4.0 %collective-permute-start = (f32[192,128]{1,0:T(8,128)S(1)}, f32[192,128]{1,0:T(8,128)S(1)}, u32[]{:S(2)}, u32[]{:S(2)}) collective-permute-start(f32[192,128]{1,0:T(8,128)S(1)} %get-tuple-element.35), channel_id=1, source_target_pairs={{0,1},{1,0},{2,3},{3,2},{4,5},{5,4},{6,7},{7,6},{8,9},{9,8},{10,11... | collective-permute-start | bytes 294920 | tf_op jit(solution)/shard_map/ppermute | solution.py:396
  7.0 5.7 %collective-permute-start.2 = (f32[192,128]{1,0:T(8,128)S(1)}, f32[192,128]{1,0:T(8,128)S(1)}, u32[]{:S(2)}, u32[]{:S(2)}) collective-permute-start(f32[192,128]{1,0:T(8,128)S(1)} %get-tuple-element.36), channel_id=1, source_target_pairs={{7,8},{8,7},{15,16},{16,15},{23,24},{24,23},{31,32},{32,31},{39,40... | collective-permute-start | bytes 294920 | tf_op jit(solution)/shard_map/ppermute | solution.py:396
  13.4 2.3 %collective-permute-done.2.near_across = f32[192,128]{1,0:T(8,128)S(1)} collective-permute-done((f32[192,128]{1,0:T(8,128)S(1)}, f32[192,128]{1,0:T(8,128)S(1)}, u32[]{:S(2)}, u32[]{:S(2)}) %collective-permute-start.2) | collective-permute-done | bytes 98336 | tf_op jit(solution)/shard_map/ppermute | solution.py:396
  15.8 1.9 %collective-permute-start.3 = (f32[288,128]{1,0:T(8,128)S(1)}, f32[288,128]{1,0:T(8,128)S(1)}, u32[]{:S(2)}, u32[]{:S(2)}) collective-permute-start(f32[288,128]{1,0:T(8,128)S(1)} %get-tuple-element.39), channel_id=1, source_target_pairs={{0,2},{2,0},{1,3},{3,1},{4,6},{6,4},{5,7},{7,5},{8,10},{10,8},{9,1... | collective-permute-start | bytes 442376 | tf_op jit(solution)/shard_map/ppermute | solution.py:396
  17.8 7.6 %collective-permute-start.4 = (f32[288,128]{1,0:T(8,128)S(1)}, f32[288,128]{1,0:T(8,128)S(1)}, u32[]{:S(2)}, u32[]{:S(2)}) collective-permute-start(f32[288,128]{1,0:T(8,128)S(1)} %shard_map.60), channel_id=1, source_target_pairs={{2,4},{4,2},{3,5},{5,3},{6,8},{8,6},{7,9},{9,7},{10,12},{12,10},{1... | collective-permute-start | bytes 442376 | tf_op jit(solution)/shard_map/ppermute | solution.py:396
  25.5 6.4 %collective-permute-done.4.refs_5_ = f32[288,128]{1,0:T(8,128)S(1)} collective-permute-done((f32[288,128]{1,0:T(8,128)S(1)}, f32[288,128]{1,0:T(8,128)S(1)}, u32[]{:S(2)}, u32[]{:S(2)}) %collective-permute-start.4) | collective-permute-done | bytes 147488 | tf_op jit(solution)/shard_map/ppermute | solution.py:396
  32.4 1.9 %collective-permute-start.5 = (f32[192,128]{1,0:T(8,128)S(1)}, f32[192,128]{1,0:T(8,128)S(1)}, u32[]{:S(2)}, u32[]{:S(2)}) collective-permute-start(f32[192,128]{1,0:T(8,128)S(1)} %get-tuple-element.43), channel_id=1, source_target_pairs={{0,1},{1,0},{2,3},{3,2},{4,5},{5,4},{6,7},{7,6},{8,9},{9,8},{10,11... | collective-permute-start | bytes 294920 | tf_op jit(solution)/shard_map/ppermute | solution.py:396
  34.4 7.0 %collective-permute-start.7 = (f32[192,128]{1,0:T(8,128)S(1)}, f32[192,128]{1,0:T(8,128)S(1)}, u32[]{:S(2)}, u32[]{:S(2)}) collective-permute-start(f32[192,128]{1,0:T(8,128)S(1)} %get-tuple-element.44), channel_id=1, source_target_pairs={{7,8},{8,7},{15,16},{16,15},{23,24},{24,23},{31,32},{32,31},{39,40... | collective-permute-start | bytes 294920 | tf_op jit(solution)/shard_map/ppermute | solution.py:396
  42.1 2.4 %collective-permute-done.7.near_across = f32[192,128]{1,0:T(8,128)S(1)} collective-permute-done((f32[192,128]{1,0:T(8,128)S(1)}, f32[192,128]{1,0:T(8,128)S(1)}, u32[]{:S(2)}, u32[]{:S(2)}) %collective-permute-start.7) | collective-permute-done | bytes 98336 | tf_op jit(solution)/shard_map/ppermute | solution.py:396
  44.6 1.9 %collective-permute-start.8 = (f32[288,128]{1,0:T(8,128)S(1)}, f32[288,128]{1,0:T(8,128)S(1)}, u32[]{:S(2)}, u32[]{:S(2)}) collective-permute-start(f32[288,128]{1,0:T(8,128)S(1)} %get-tuple-element.46), channel_id=1, source_target_pairs={{0,2},{2,0},{1,3},{3,1},{4,6},{6,4},{5,7},{7,5},{8,10},{10,8},{9,1... | collective-permute-start | bytes 442376 | tf_op jit(solution)/shard_map/ppermute | solution.py:396
  46.6 8.1 %collective-permute-start.9 = (f32[288,128]{1,0:T(8,128)S(1)}, f32[288,128]{1,0:T(8,128)S(1)}, u32[]{:S(2)}, u32[]{:S(2)}) collective-permute-start(f32[288,128]{1,0:T(8,128)S(1)} %shard_map.63), channel_id=1, source_target_pairs={{2,4},{4,2},{3,5},{5,3},{6,8},{8,6},{7,9},{9,7},{10,12},{12,10},{1... | collective-permute-start | bytes 442376 | tf_op jit(solution)/shard_map/ppermute | solution.py:396
  54.8 5.6 %collective-permute-done.9.refs_5_ = f32[288,128]{1,0:T(8,128)S(1)} collective-permute-done((f32[288,128]{1,0:T(8,128)S(1)}, f32[288,128]{1,0:T(8,128)S(1)}, u32[]{:S(2)}, u32[]{:S(2)}) %collective-permute-start.9) | collective-permute-done | bytes 147488 | tf_op jit(solution)/shard_map/ppermute | solution.py:396
  61.0 1.9 %collective-permute-start.11 = (f32[72,128]{1,0:T(8,128)S(1)}, f32[72,128]{1,0:T(8,128)S(1)}, u32[]{:S(2)}, u32[]{:S(2)}) collective-permute-start(f32[72,128]{1,0:T(8,128)S(1)} %get-tuple-element.48.own), channel_id=1, source_target_pairs={{0,8},{8,0},{1,9},{9,1},{2,10},{10,2},{3,11},{11,3},{4,12},{12,4},... | collective-permute-start | bytes 110600 | tf_op jit(solution)/shard_map/ppermute | solution.py:396
  62.9 2.3 %collective-permute-start.10 = (f32[72,128]{1,0:T(8,128)S(1)}, f32[72,128]{1,0:T(8,128)S(1)}, u32[]{:S(2)}, u32[]{:S(2)}) collective-permute-start(f32[72,128]{1,0:T(8,128)S(1)} %get-tuple-element.48.own), channel_id=1, source_target_pairs={{8,16},{16,8},{9,17},{17,9},{10,18},{18,10},{11,19},{19,11},{12,20... | collective-permute-start | bytes 110600 | tf_op jit(solution)/shard_map/ppermute | solution.py:396
  65.2 3.0 %collective-permute-done.10.across = f32[72,128]{1,0:T(8,128)S(1)} collective-permute-done((f32[72,128]{1,0:T(8,128)S(1)}, f32[72,128]{1,0:T(8,128)S(1)}, u32[]{:S(2)}, u32[]{:S(2)}) %collective-permute-start.10) | collective-permute-done | bytes 36896 | tf_op jit(solution)/shard_map/ppermute | solution.py:396
  68.2 21.6 %all_to_all.15.received = f32[8,144,128]{2,1,0:T(8,128)S(1)} all-to-all(f32[8,144,128]{2,1,0:T(8,128)S(1)} %shard_map.65), channel_id=1, replica_groups=mesh['outer'=48,'pair'=2,'row'=8] {'row'}, dimensions={0} | all-to-all | bytes 1179648 | tf_op jit(solution)/shard_map/all_to_all | solution.py:424
  90.8 2.2 %collective-permute-start.12 = (f32[192,128]{1,0:T(8,128)S(1)}, f32[192,128]{1,0:T(8,128)S(1)}, u32[]{:S(2)}, u32[]{:S(2)}) collective-permute-start(f32[192,128]{1,0:T(8,128)S(1)} %get-tuple-element.52), channel_id=1, source_target_pairs={{0,1},{1,0},{2,3},{3,2},{4,5},{5,4},{6,7},{7,6},{8,9},{9,8},{10,11... | collective-permute-start | bytes 294920 | tf_op jit(solution)/shard_map/ppermute | solution.py:396
  93.0 1.9 %collective-permute-start.14 = (f32[192,128]{1,0:T(8,128)S(1)}, f32[192,128]{1,0:T(8,128)S(1)}, u32[]{:S(2)}, u32[]{:S(2)}) collective-permute-start(f32[192,128]{1,0:T(8,128)S(1)} %get-tuple-element.53), channel_id=1, source_target_pairs={{7,8},{8,7},{15,16},{16,15},{23,24},{24,23},{31,32},{32,31},{39,40... | collective-permute-start | bytes 294920 | tf_op jit(solution)/shard_map/ppermute | solution.py:396
  96.1 4.0 %collective-permute-done.14.near_across = f32[192,128]{1,0:T(8,128)S(1)} collective-permute-done((f32[192,128]{1,0:T(8,128)S(1)}, f32[192,128]{1,0:T(8,128)S(1)}, u32[]{:S(2)}, u32[]{:S(2)}) %collective-permute-start.14) | collective-permute-done | bytes 98336 | tf_op jit(solution)/shard_map/ppermute | solution.py:396
  102.3 3.1 %collective-permute-start.16 = (f32[288,128]{1,0:T(8,128)S(1)}, f32[288,128]{1,0:T(8,128)S(1)}, u32[]{:S(2)}, u32[]{:S(2)}) collective-permute-start(f32[288,128]{1,0:T(8,128)S(1)} %shard_map.68), channel_id=1, source_target_pairs={{2,4},{4,2},{3,5},{5,3},{6,8},{8,6},{7,9},{9,7},{10,12},{12,10},{1... | collective-permute-start | bytes 442376 | tf_op jit(solution)/shard_map/ppermute | solution.py:396
  105.3 3.3 %collective-permute-done.15.refs_4_ = f32[288,128]{1,0:T(8,128)S(1)} collective-permute-done((f32[288,128]{1,0:T(8,128)S(1)}, f32[288,128]{1,0:T(8,128)S(1)}, u32[]{:S(2)}, u32[]{:S(2)}) %collective-permute-start.15) | collective-permute-done | bytes 147488 | tf_op jit(solution)/shard_map/ppermute | solution.py:396
  108.6 4.2 %collective-permute-done.16.refs_5_ = f32[288,128]{1,0:T(8,128)S(1)} collective-permute-done((f32[288,128]{1,0:T(8,128)S(1)}, f32[288,128]{1,0:T(8,128)S(1)}, u32[]{:S(2)}, u32[]{:S(2)}) %collective-permute-start.16) | collective-permute-done | bytes 147488 | tf_op jit(solution)/shard_map/ppermute | solution.py:396
  113.5 13.8 %all_to_all.16.received = f32[16,1,128]{2,1,0:T(1,128)S(1)} all-to-all(f32[16,1,128]{2,1,0:T(1,128)S(1)} %get-tuple-element.56), channel_id=1, replica_groups=mesh['outer'=48,'pair'=2,'row'=8] {'pair','row'}, dimensions={0} | all-to-all | bytes 16384 | tf_op jit(solution)/shard_map/all_to_all | solution.py:459
  127.3 34.3 %all_to_all.17.received = f32[48,1,128]{2,1,0:T(1,128)S(1)} all-to-all(f32[48,1,128]{2,1,0:T(1,128)S(1)} %shard_map.70), channel_id=1, replica_groups=mesh['outer'=48,'pair'=2,'row'=8] {'outer'}, dimensions={0} | all-to-all | bytes 49152 | tf_op jit(solution)/shard_map/all_to_all | solution.py:461
  (34 shorter events, 11.7 us)
Async XLA Ops:
  0.6 0.7 copy-start.2
  0.7 0.7 copy-start.1
  1.3 0.9 copy-start
  2.9 10.4 %collective-permute-start = (f32[192,128]{1,0:T(8,128)S(1)}, f32[192,128]{1,0:T(8,128)S(1)}, u32[]{:S(2)}, u32[]{:S(2)}) collective-permute-start(f32[192,128]{1,0:T(8,128)S(1)} %get-tuple-element.35), channel_id=1, source_target_pairs={{0,1},{1,0},{2,3},{3,2},{4,5},{5,4},{6,7},{7,6},{8,9},{9,8},{10,11... | collective-permute-start | bytes 294920 | tf_op jit(solution)/shard_map/ppermute | solution.py:396
  7.0 8.7 %collective-permute-start.2 = (f32[192,128]{1,0:T(8,128)S(1)}, f32[192,128]{1,0:T(8,128)S(1)}, u32[]{:S(2)}, u32[]{:S(2)}) collective-permute-start(f32[192,128]{1,0:T(8,128)S(1)} %get-tuple-element.36), channel_id=1, source_target_pairs={{7,8},{8,7},{15,16},{16,15},{23,24},{24,23},{31,32},{32,31},{39,40... | collective-permute-start | bytes 294920 | tf_op jit(solution)/shard_map/ppermute | solution.py:396
  12.7 3.0 %collective-permute-start.1 = (f32[192,128]{1,0:T(8,128)S(1)}, f32[192,128]{1,0:T(8,128)S(1)}, u32[]{:S(2)}, u32[]{:S(2)}) collective-permute-start(f32[192,128]{1,0:T(8,128)S(1)} %get-tuple-element.36), channel_id=1, source_target_pairs={{1,2},{2,1},{3,4},{4,3},{5,6},{6,5},{9,10},{10,9},{11,12},{12,11},... | collective-permute-start | bytes 294920 | tf_op jit(solution)/shard_map/ppermute | solution.py:396
  15.8 9.7 %collective-permute-start.3 = (f32[288,128]{1,0:T(8,128)S(1)}, f32[288,128]{1,0:T(8,128)S(1)}, u32[]{:S(2)}, u32[]{:S(2)}) collective-permute-start(f32[288,128]{1,0:T(8,128)S(1)} %get-tuple-element.39), channel_id=1, source_target_pairs={{0,2},{2,0},{1,3},{3,1},{4,6},{6,4},{5,7},{7,5},{8,10},{10,8},{9,1... | collective-permute-start | bytes 442376 | tf_op jit(solution)/shard_map/ppermute | solution.py:396
  17.8 14.0 %collective-permute-start.4 = (f32[288,128]{1,0:T(8,128)S(1)}, f32[288,128]{1,0:T(8,128)S(1)}, u32[]{:S(2)}, u32[]{:S(2)}) collective-permute-start(f32[288,128]{1,0:T(8,128)S(1)} %shard_map.60), channel_id=1, source_target_pairs={{2,4},{4,2},{3,5},{5,3},{6,8},{8,6},{7,9},{9,7},{10,12},{12,10},{1... | collective-permute-start | bytes 442376 | tf_op jit(solution)/shard_map/ppermute | solution.py:396
  32.4 9.7 %collective-permute-start.5 = (f32[192,128]{1,0:T(8,128)S(1)}, f32[192,128]{1,0:T(8,128)S(1)}, u32[]{:S(2)}, u32[]{:S(2)}) collective-permute-start(f32[192,128]{1,0:T(8,128)S(1)} %get-tuple-element.43), channel_id=1, source_target_pairs={{0,1},{1,0},{2,3},{3,2},{4,5},{5,4},{6,7},{7,6},{8,9},{9,8},{10,11... | collective-permute-start | bytes 294920 | tf_op jit(solution)/shard_map/ppermute | solution.py:396
  34.4 10.1 %collective-permute-start.7 = (f32[192,128]{1,0:T(8,128)S(1)}, f32[192,128]{1,0:T(8,128)S(1)}, u32[]{:S(2)}, u32[]{:S(2)}) collective-permute-start(f32[192,128]{1,0:T(8,128)S(1)} %get-tuple-element.44), channel_id=1, source_target_pairs={{7,8},{8,7},{15,16},{16,15},{23,24},{24,23},{31,32},{32,31},{39,40... | collective-permute-start | bytes 294920 | tf_op jit(solution)/shard_map/ppermute | solution.py:396
  41.4 3.1 %collective-permute-start.6 = (f32[192,128]{1,0:T(8,128)S(1)}, f32[192,128]{1,0:T(8,128)S(1)}, u32[]{:S(2)}, u32[]{:S(2)}) collective-permute-start(f32[192,128]{1,0:T(8,128)S(1)} %get-tuple-element.44), channel_id=1, source_target_pairs={{1,2},{2,1},{3,4},{4,3},{5,6},{6,5},{9,10},{10,9},{11,12},{12,11},... | collective-permute-start | bytes 294920 | tf_op jit(solution)/shard_map/ppermute | solution.py:396
  44.6 10.2 %collective-permute-start.8 = (f32[288,128]{1,0:T(8,128)S(1)}, f32[288,128]{1,0:T(8,128)S(1)}, u32[]{:S(2)}, u32[]{:S(2)}) collective-permute-start(f32[288,128]{1,0:T(8,128)S(1)} %get-tuple-element.46), channel_id=1, source_target_pairs={{0,2},{2,0},{1,3},{3,1},{4,6},{6,4},{5,7},{7,5},{8,10},{10,8},{9,1... | collective-permute-start | bytes 442376 | tf_op jit(solution)/shard_map/ppermute | solution.py:396
  46.6 13.8 %collective-permute-start.9 = (f32[288,128]{1,0:T(8,128)S(1)}, f32[288,128]{1,0:T(8,128)S(1)}, u32[]{:S(2)}, u32[]{:S(2)}) collective-permute-start(f32[288,128]{1,0:T(8,128)S(1)} %shard_map.63), channel_id=1, source_target_pairs={{2,4},{4,2},{3,5},{5,3},{6,8},{8,6},{7,9},{9,7},{10,12},{12,10},{1... | collective-permute-start | bytes 442376 | tf_op jit(solution)/shard_map/ppermute | solution.py:396
  61.0 4.2 %collective-permute-start.11 = (f32[72,128]{1,0:T(8,128)S(1)}, f32[72,128]{1,0:T(8,128)S(1)}, u32[]{:S(2)}, u32[]{:S(2)}) collective-permute-start(f32[72,128]{1,0:T(8,128)S(1)} %get-tuple-element.48.own), channel_id=1, source_target_pairs={{0,8},{8,0},{1,9},{9,1},{2,10},{10,2},{3,11},{11,3},{4,12},{12,4},... | collective-permute-start | bytes 110600 | tf_op jit(solution)/shard_map/ppermute | solution.py:396
  62.9 5.3 %collective-permute-start.10 = (f32[72,128]{1,0:T(8,128)S(1)}, f32[72,128]{1,0:T(8,128)S(1)}, u32[]{:S(2)}, u32[]{:S(2)}) collective-permute-start(f32[72,128]{1,0:T(8,128)S(1)} %get-tuple-element.48.own), channel_id=1, source_target_pairs={{8,16},{16,8},{9,17},{17,9},{10,18},{18,10},{11,19},{19,11},{12,20... | collective-permute-start | bytes 110600 | tf_op jit(solution)/shard_map/ppermute | solution.py:396
  90.8 5.4 %collective-permute-start.12 = (f32[192,128]{1,0:T(8,128)S(1)}, f32[192,128]{1,0:T(8,128)S(1)}, u32[]{:S(2)}, u32[]{:S(2)}) collective-permute-start(f32[192,128]{1,0:T(8,128)S(1)} %get-tuple-element.52), channel_id=1, source_target_pairs={{0,1},{1,0},{2,3},{3,2},{4,5},{5,4},{6,7},{7,6},{8,9},{9,8},{10,11... | collective-permute-start | bytes 294920 | tf_op jit(solution)/shard_map/ppermute | solution.py:396
  93.0 7.1 %collective-permute-start.14 = (f32[192,128]{1,0:T(8,128)S(1)}, f32[192,128]{1,0:T(8,128)S(1)}, u32[]{:S(2)}, u32[]{:S(2)}) collective-permute-start(f32[192,128]{1,0:T(8,128)S(1)} %get-tuple-element.53), channel_id=1, source_target_pairs={{7,8},{8,7},{15,16},{16,15},{23,24},{24,23},{31,32},{32,31},{39,40... | collective-permute-start | bytes 294920 | tf_op jit(solution)/shard_map/ppermute | solution.py:396
  94.9 5.2 %collective-permute-start.13 = (f32[192,128]{1,0:T(8,128)S(1)}, f32[192,128]{1,0:T(8,128)S(1)}, u32[]{:S(2)}, u32[]{:S(2)}) collective-permute-start(f32[192,128]{1,0:T(8,128)S(1)} %get-tuple-element.53), channel_id=1, source_target_pairs={{1,2},{2,1},{3,4},{4,3},{5,6},{6,5},{9,10},{10,9},{11,12},{12,11},... | collective-permute-start | bytes 294920 | tf_op jit(solution)/shard_map/ppermute | solution.py:396
  100.2 8.4 %collective-permute-start.15 = (f32[288,128]{1,0:T(8,128)S(1)}, f32[288,128]{1,0:T(8,128)S(1)}, u32[]{:S(2)}, u32[]{:S(2)}) collective-permute-start(f32[288,128]{1,0:T(8,128)S(1)} %get-tuple-element.55), channel_id=1, source_target_pairs={{0,2},{2,0},{1,3},{3,1},{4,6},{6,4},{5,7},{7,5},{8,10},{10,8},{9,1... | collective-permute-start | bytes 442376 | tf_op jit(solution)/shard_map/ppermute | solution.py:396
  102.3 10.5 %collective-permute-start.16 = (f32[288,128]{1,0:T(8,128)S(1)}, f32[288,128]{1,0:T(8,128)S(1)}, u32[]{:S(2)}, u32[]{:S(2)}) collective-permute-start(f32[288,128]{1,0:T(8,128)S(1)} %shard_map.68), channel_id=1, source_target_pairs={{2,4},{4,2},{3,5},{5,3},{6,8},{8,6},{7,9},{9,7},{10,12},{12,10},{1... | collective-permute-start | bytes 442376 | tf_op jit(solution)/shard_map/ppermute | solution.py:396

commit v6 on v5

--- a/solution.py
+++ b/solution.py
@@ -15,6 +15,7 @@
 PAIR = 2
 BLOCK = 72
 REACH = 3
+WIDEST = 8
 GRANT = 8 * 1024 * 1024
 AXES = ("outer", "pair", "row")
 RELAX_FINE = (2.0 / 3.0) / 6.0
@@ -94,19 +95,38 @@
     faces[to + 80 : to + 96, :] = values[pl.ds(at + 3, 16, stride=4), :]
 
 
-def read_coarse_ghosts(faces, block, slots, device, ghosts):
+def read_planes(planes, rows, block, slots, device, out):
+    blocks = planes.shape[0] // (6 * rows)
     for face in range(6):
         slot = jnp.broadcast_to(slots[face : face + 1, :], (8, LANES))
         safe = jnp.maximum(slot, 0)
         lane = safe & (LANES - 1)
         distance = jnp.where(slot >= 0, jnp.abs(lax.shift_right_logical(safe, 7) - device), -1)
-        for step in (0, 8):
+        for step in range(0, rows, 8):
             picked = jnp.zeros((8, LANES), jnp.float32)
             for which in range(REACH + 1):
                 source = block - which if face % 2 == 0 else block + which
-                row = 96 * source + 16 * (face ^ 1) + step
-                picked = jnp.where(distance == which, take(faces[row : row + 8, :], lane), picked)
-            ghosts[16 * face + step : 16 * face + step + 8, :] = picked
+                if 0 <= source < blocks:
+                    row = rows * (6 * source + (face ^ 1)) + step
+                    picked = jnp.where(distance == which, take(planes[row : row + 8, :], lane), picked)
+            out[rows * face + step : rows * face + step + 8, :] = picked
+
+
+def write_rims(faces, at, ghosts, extended, to):
+    for face in range(6):
+        axis, side = face // 2, 3 * (face % 2)
+        row = to + 32 * face
+        extended[row : row + 16, :] = faces[at + 16 * face : at + 16 * face + 16, :]
+        row += 16
+        for other in (other for other in range(3) if other != axis):
+            along = 3 - axis - other
+            for lateral in (2 * other, 2 * other + 1):
+                if axis < along:
+                    edge = ghosts[16 * lateral + 4 * side : 16 * lateral + 4 * side + 4, :]
+                else:
+                    edge = ghosts[pl.ds(16 * lateral + side, 4, stride=4), :]
+                extended[row : row + 4, :] = edge
+                row += 4
 
 
 def windows_of(table, up, down, near_inner, near_outer, far_inner, far_outer):
@@ -235,7 +255,7 @@
 
 
 def defect_kernel(residual, second, *refs):
-    *faces, table, defect, block, ghosts, sums = refs
+    *faces, table, smoothed, block, out_up, out_down, out_inner, out_outer, ghosts, sums = refs
     read_ghosts(table, faces, ghosts, FINE)
     for big_x in range(4):
         for big_y in range(4):
@@ -245,25 +265,30 @@
                     centre, around = beside(second, ghosts, x, y)
                     at = 64 * x + 8 * y
                     part = residual[at : at + 8, :] - (6.0 * centre - around)
-                    defect[at : at + 8, :] = part
+                    smoothed[at : at + 8, :] = centre + RELAX_FINE * part
                     total = part if total is None else total + part
             at = 32 * big_x + 8 * big_y
             sums[at : at + 8, :] = total
-    restricted = (sums[pl.ds(0, 64, stride=2), :] + sums[pl.ds(1, 64, stride=2), :]) * 0.125
-    block[0:64, :] = restricted
+    block[0:64, :] = (sums[pl.ds(0, 64, stride=2), :] + sums[pl.ds(1, 64, stride=2), :]) * 0.125
     block[64:72, :] = table[NEIGHBOUR_ROW : NEIGHBOUR_ROW + 8, :].astype(jnp.float32)
+    write_faces(smoothed, out_up, out_down)
+    write_pair(table, UPPER_NEAR, out_up, out_down, out_inner, out_outer, FINE)
 
 
 def spread_kernel(device_ref, own, across, beside_row, out):
     column = device_ref[0] % out.shape[0]
     odd_row = (device_ref[0] // out.shape[0]) % 2
+    after_is_beside = jnp.full((8, LANES), odd_row, jnp.int32) == 0
     for target in range(out.shape[0]):
-        out[target, 0:BLOCK, :] = own[...]
-        from_before = jnp.where(column > target, 1, 0)
+        stays = jnp.full((8, LANES), column, jnp.int32) == target
+        from_before = jnp.where(column >= target, 1, 0)
         same = jnp.full((8, LANES), jnp.where(odd_row == from_before, 1, 0), jnp.int32) > 0
         for row in range(0, BLOCK, 8):
-            other = jnp.where(same, beside_row[row : row + 8, :], across[row : row + 8, :])
-            out[target, BLOCK + row : BLOCK + row + 8, :] = other
+            near = beside_row[row : row + 8, :]
+            far = across[row : row + 8, :]
+            after = jnp.where(after_is_beside, near, far)
+            out[target, row : row + 8, :] = jnp.where(stays, after, own[row : row + 8, :])
+            out[target, BLOCK + row : BLOCK + row + 8, :] = jnp.where(same, near, far)
 
 
 def coarse_update(first, at, ghosts, low_y, high_y, low_z, high_z):
@@ -284,44 +309,58 @@
     return centre + (centre - RELAX_COARSE * ((6.0 * centre - around) * 0.25))
 
 
-def correct_kernel(device_ref, second, defect, received, *refs):
-    table, out, out_up, out_down, out_inner, out_outer, *scratch = refs
-    first, first_faces, slots, coarse, coarse_faces, ghosts, low_y, high_y, low_z, high_z, *scratch = scratch
-    wide, wide_ghosts, spread = scratch
-    device = device_ref[0]
+def coarse_correction(device, block, received, scratch):
+    first, first_faces, slots, coarse, coarse_faces, ghosts, low_y, high_y, low_z, high_z, extended, across = scratch
     row_length = received.shape[0]
-    column = device % row_length
-    for block in range(4 * REACH + 1):
-        place = column + (block - 2 * REACH)
-        in_row = (place >= 0) & (place < row_length)
-        sender = lax.rem(place + row_length, row_length)
-        start = jnp.where(in_row, 0, BLOCK)
+    column = lax.rem(device, row_length)
+    for index in range(2 * WIDEST + 1):
+        offset = index - WIDEST
+        if offset:
+            place = column + offset
+            sender = lax.rem(place + row_length, row_length)
+            in_row = (place >= 0) & (place < row_length)
+            start = 0 if offset == WIDEST else jnp.where(in_row, 0, BLOCK)
+            rows = lambda row: received[sender, pl.ds(pl.multiple_of(start + row, 8), 8), :]
+        else:
+            rows = lambda row: block[row : row + 8, :]
         for row in range(0, 64, 8):
-            at = pl.multiple_of(start + row, 8)
-            first[64 * block + row : 64 * block + row + 8, :] = RELAX_COARSE * received[sender, pl.ds(at, 8), :]
-        write_coarse_faces(first, 64 * block, first_faces, 96 * block)
-        if REACH <= block <= 3 * REACH:
-            at = pl.multiple_of(start + 64, 8)
-            to = 8 * (block - REACH)
-            slots[to : to + 8, :] = received[sender, pl.ds(at, 8), :].astype(jnp.int32)
-    for block in range(2 * REACH + 1):
-        block_slots = slots.at[8 * block : 8 * block + 8, :]
-        read_coarse_ghosts(first_faces, block + REACH, block_slots, device + (block - REACH), ghosts)
-        updated = coarse_update(first, 64 * (block + REACH), ghosts, low_y, high_y, low_z, high_z)
-        coarse[64 * block : 64 * block + 64, :] = updated
-        write_coarse_faces(coarse, 64 * block, coarse_faces, 96 * block)
-    read_coarse_ghosts(coarse_faces, REACH, slots.at[8 * REACH : 8 * REACH + 8, :], device, ghosts)
-    own = coarse[64 * REACH : 64 * REACH + 64, :]
-    wide[pl.ds(0, 64, stride=2), :] = own
-    wide[pl.ds(1, 64, stride=2), :] = own
-    wide_ghosts[pl.ds(0, 64, stride=2), :] = ghosts[0:64, :]
-    wide_ghosts[pl.ds(1, 64, stride=2), :] = ghosts[0:64, :]
+            first[64 * index + row : 64 * index + row + 8, :] = RELAX_COARSE * rows(row)
+        write_coarse_faces(first, 64 * index, first_faces, 96 * index)
+        if abs(offset) <= 2 * REACH:
+            to = 8 * (offset + 2 * REACH)
+            slots[to : to + 8, :] = rows(64).astype(jnp.int32)
+    slots_of = lambda offset: slots.at[8 * (offset + 2 * REACH) : 8 * (offset + 2 * REACH) + 8, :]
+    for offset in range(-2 * REACH, 2 * REACH + 1):
+        index = offset + 2 * REACH
+        read_planes(first_faces, 16, offset + WIDEST, slots_of(offset), device + offset, ghosts)
+        updated = coarse_update(first, 64 * (offset + WIDEST), ghosts, low_y, high_y, low_z, high_z)
+        coarse[...] = updated
+        write_coarse_faces(coarse, 0, coarse_faces, 96 * index)
+        if offset == 0:
+            first[0:64, :] = updated
+    for offset in range(-REACH, REACH + 1):
+        index = offset + 2 * REACH
+        read_planes(coarse_faces, 16, index, slots_of(offset), device + offset, ghosts)
+        write_rims(coarse_faces, 96 * index, ghosts, extended, 192 * (offset + REACH))
+    read_planes(extended, 32, REACH, slots_of(0), device, across)
+    return first[0:64, :]
+
+
+def image_kernel(device_ref, residual, smoothed, block, received, *refs):
+    *faces, table, direction, image, sums, fine_ghosts, wide, wide_across, wide_own, spread = refs[: 7 + 3 + 5]
+    scratch = refs[7 + 3 + 5 :]
+    coarse_faces, across = scratch[4], scratch[-1]
+    own = coarse_correction(device_ref[0], block, received, scratch)
+    sub = lax.broadcasted_iota(jnp.int32, (8, LANES), 0)
+    for half in (0, 1):
+        wide[pl.ds(half, 64, stride=2), :] = own
+        wide_across[pl.ds(half, 192, stride=2), :] = across[...]
+        wide_own[pl.ds(half, 96, stride=2), :] = coarse_faces[192 * REACH : 192 * REACH + 96, :]
     for x in range(8):
         for y in range(8):
             at = 64 * x + 8 * y
             source = 32 * (x // 2) + 8 * (y // 2)
             spread[at : at + 8, :] = wide[source : source + 8, :]
-    sub = lax.broadcasted_iota(jnp.int32, (8, LANES), 0)
     for x in range(8):
         for y in range(8):
             at = 64 * x + 8 * y
@@ -329,27 +368,37 @@
             centre = spread[at : at + 8, :]
             side_x = 8 * (y // 2)
             side_y = 8 * (x // 2)
-            below_x = spread[at - 64 : at - 56, :] if x > 0 else wide_ghosts[side_x : side_x + 8, :]
-            above_x = spread[at + 64 : at + 72, :] if x < 7 else wide_ghosts[32 + side_x : 40 + side_x, :]
-            below_y = spread[at - 8 : at, :] if y > 0 else wide_ghosts[64 + side_y : 72 + side_y, :]
-            above_y = spread[at + 8 : at + 16, :] if y < 7 else wide_ghosts[96 + side_y : 104 + side_y, :]
-            below_z = jnp.where(sub == 0, ghosts[64 + cell : 65 + cell, :], pltpu.roll(centre, 1, 0))
-            above_z = jnp.where(sub == 7, ghosts[80 + cell : 81 + cell, :], pltpu.roll(centre, 7, 0))
+            below_x = spread[at - 64 : at - 56, :] if x > 0 else wide_across[side_x : side_x + 8, :]
+            above_x = spread[at + 64 : at + 72, :] if x < 7 else wide_across[64 + side_x : 72 + side_x, :]
+            below_y = spread[at - 8 : at, :] if y > 0 else wide_across[128 + side_y : 136 + side_y, :]
+            above_y = spread[at + 8 : at + 16, :] if y < 7 else wide_across[192 + side_y : 200 + side_y, :]
+            below_z = jnp.where(sub == 0, across[128 + cell : 129 + cell, :], pltpu.roll(centre, 1, 0))
+            above_z = jnp.where(sub == 7, across[160 + cell : 161 + cell, :], pltpu.roll(centre, 7, 0))
             around = ((above_x + below_x) + (above_y + below_y)) + (above_z + below_z)
-            left = defect[at : at + 8, :] - (6.0 * centre - around)
-            out[at : at + 8, :] = (second[at : at + 8, :] + centre) + RELAX_FINE * left
-    write_faces(out, out_up, out_down)
-    write_pair(table, UPPER_NEAR, out_up, out_down, out_inner, out_outer, FINE)
-
-
-def image_kernel(residual, direction, *refs):
-    *faces, table, image, sums, ghosts = refs
-    read_ghosts(table, faces, ghosts, FINE)
+            change = centre - RELAX_FINE * (6.0 * centre - around)
+            direction[at : at + 8, :] = smoothed[at : at + 8, :] + change
+    read_ghosts(table, faces, fine_ghosts, FINE)
+    for face in range(6):
+        for i in range(8):
+            line = i // 2
+            centre = wide_across[64 * face + 8 * line : 64 * face + 8 * line + 8, :]
+            below = 64 * face + (8 * ((i - 1) // 2) if i > 0 else 32)
+            above = 64 * face + (8 * ((i + 1) // 2) if i < 7 else 40)
+            low = across[32 * face + 24 + line : 32 * face + 25 + line, :]
+            high = across[32 * face + 28 + line : 32 * face + 29 + line, :]
+            around = wide_across[below : below + 8, :] + wide_across[above : above + 8, :]
+            around = around + jnp.where(sub == 0, low, pltpu.roll(centre, 1, 0))
+            around = around + jnp.where(sub == 7, high, pltpu.roll(centre, 7, 0))
+            around = around + wide_own[32 * face + 8 * line : 32 * face + 8 * line + 8, :]
+            at = 64 * face + 8 * i
+            change = centre - RELAX_FINE * (5.0 * centre - around)
+            present = jnp.broadcast_to(table[WINDOW_ROW + face : WINDOW_ROW + face + 1, :], (8, LANES)) >= 0
+            fine_ghosts[at : at + 8, :] = fine_ghosts[at : at + 8, :] + jnp.where(present, change, 0.0)
     zero = jnp.zeros((8, LANES), jnp.float32)
     parts = [zero] * 5
     for x in range(8):
         for y in range(8):
-            centre, around = beside(direction, ghosts, x, y)
+            centre, around = beside(direction, fine_ghosts, x, y)
             at = 64 * x + 8 * y
             applied = 6.0 * centre - around
             image[at : at + 8, :] = applied
@@ -438,23 +487,22 @@
     second, *sides = call(
         smooth_kernel, [fine, *faces], residual_in, *exchange(FINE, *sides, table), scratch=[fine_ghosts]
     )
-    defect, block = call(
-        defect_kernel, [fine, f32(BLOCK, LANES)],
+    smoothed, block, *sides = call(
+        defect_kernel, [fine, f32(BLOCK, LANES), *faces],
         residual_in, second, *exchange(FINE, *sides, table), scratch=[fine_ghosts, scratch(128)],
     )
-    blocks = 2 * REACH + 1
-    direction, *sides = call(
-        correct_kernel, [fine, *faces], device, second, defect, share(block, device), table,
-        in_specs=[SMEM] + [VMEM] * 4,
+    blocks, wide_blocks, near_blocks = 2 * WIDEST + 1, 4 * REACH + 1, 2 * REACH + 1
+    exchanged = exchange(FINE, *sides, table)
+    direction, image, sums = call(
+        image_kernel, [fine, fine, f32(lax.axis_size(AXES[1:]), 1, LANES)],
+        device, residual_in, smoothed, block, share(block, device), *exchanged,
+        in_specs=[SMEM] + [VMEM] * 11,
         scratch=[
-            scratch(64 * (4 * REACH + 1)), scratch(96 * (4 * REACH + 1)), pltpu.VMEM((8 * blocks, LANES), jnp.int32),
-            scratch(64 * blocks), scratch(96 * blocks), scratch(96), *[scratch(64)] * 4,
-            scratch(128), scratch(128), scratch(512),
+            fine_ghosts, scratch(128), scratch(384), scratch(192), scratch(512),
+            scratch(64 * blocks), scratch(96 * blocks), pltpu.VMEM((8 * wide_blocks, LANES), jnp.int32),
+            scratch(64), scratch(96 * wide_blocks), scratch(96), *[scratch(64)] * 4,
+            scratch(192 * near_blocks), scratch(192),
         ],
-    )
-    image, sums = call(
-        image_kernel, [fine, f32(lax.axis_size(AXES[1:]), 1, LANES)],
-        residual_in, direction, *exchange(FINE, *sides, table), scratch=[fine_ghosts],
     )
     received = lax.all_to_all(sums, AXES[1:], 0, 0, tiled=True)
     (sums,) = call(add_kernel, [f32(lax.axis_size("outer"), 1, LANES)], received)

time: 164 us -> 156 us (0.951)
  blocking collectives: 69.7 us -> 47.1 us
  starting transfers between devices: 53.6 us -> 63.1 us
  waiting for transfers between devices: 31.7 us -> 35.2 us
  Pallas kernels: 5.02 us -> 6.89 us
    all_to_all x1 -> x0, blocking collectives: 21.6 us -> none  [share(): return lax.all_to_all(blocks, 'row', 0, 0, tiled=True)]
    all_to_all x0 -> x1, starting transfers between devices: none -> 4.79 us  [share(): return lax.all_to_all(blocks, 'row', 0, 0, tiled=True)]
    ppermute x17, starting transfers between devices: 53.6 us -> 58.3 us  [swap(): return lax.ppermute(block, AXES, route)]
    ppermute x17, waiting for transfers between devices: 31.7 us -> 35.2 us  [swap(): return lax.ppermute(block, AXES, route)]
    pallas_call x14 -> x13, Pallas kernels: 5.02 us -> 6.89 us  [call(): pl.pallas_call(kernel, out_shape=outs, in_specs=in_specs or [VMEM] * len(...]
  transfers between devices with their start and end apart: 17 -> 18, of which waited for: 9 -> 9; matrix products, arithmetic and copies ran while one was open for 0% -> 0% of each run, Pallas kernels for 0% -> 0%
where the time goes in v6:
time: 156 us; the launch traced here: 155 us
  starting transfers between devices  63.1 us (40%)
  blocking collectives  47.1 us (30%)
  waiting for transfers between devices  35.2 us (23%)
  Pallas kernels  6.89 us (4%)
  local copies, waits for them, and re-layouts  2.15 us (1%)
    ppermute x17, starting transfers between devices, swap(): return lax.ppermute(block, AXES, route)  58.3 us
    ppermute x17, waiting for transfers between devices, swap(): return lax.ppermute(block, AXES, route)  35.2 us
    all_to_all x1, blocking collectives, step(): received = lax.all_to_all(sums, 'outer', 0, 0, tiled=True)  34.8 us
    all_to_all x1, blocking collectives, step(): received = lax.all_to_all(sums, AXES[1:], 0, 0, tiled=True)  12.4 us
    pallas_call x13, Pallas kernels, call(): pl.pallas_call(kernel, out_shape=outs, in_specs=in_specs or [VMEM] * len(...  6.89 us
    all_to_all x1, starting transfers between devices, share(): return lax.all_to_all(blocks, 'row', 0, 0, tiled=True)  4.79 us
  transfers between devices with their start and end apart: 18, of which 9 were waited for; matrix products, arithmetic and copies ran while one was open for 0% of the time, Pallas kernels for 0%

profile of v6, /device:TPU:1, one launch (start us, length us, event | category | flops | bytes accessed | tf_op | source)
XLA Modules:
  0.0 155.3 jit_solution(17056349987617005035)
XLA Ops:
  2.9 4.0 %collective-permute-start = (f32[192,128]{1,0:T(8,128)S(1)}, f32[192,128]{1,0:T(8,128)S(1)}, u32[]{:S(2)}, u32[]{:S(2)}) collective-permute-start(f32[192,128]{1,0:T(8,128)S(1)} %get-tuple-element.35), channel_id=1, source_target_pairs={{0,1},{1,0},{2,3},{3,2},{4,5},{5,4},{6,7},{7,6},{8,9},{9,8},{10,11... | collective-permute-start | bytes 294920 | tf_op jit(solution)/shard_map/ppermute | solution.py:445
  7.6 5.7 %collective-permute-start.2 = (f32[192,128]{1,0:T(8,128)S(1)}, f32[192,128]{1,0:T(8,128)S(1)}, u32[]{:S(2)}, u32[]{:S(2)}) collective-permute-start(f32[192,128]{1,0:T(8,128)S(1)} %get-tuple-element.36), channel_id=1, source_target_pairs={{7,8},{8,7},{15,16},{16,15},{23,24},{24,23},{31,32},{32,31},{39,40... | collective-permute-start | bytes 294920 | tf_op jit(solution)/shard_map/ppermute | solution.py:445
  13.4 3.0 %collective-permute-done.2.near_across = f32[192,128]{1,0:T(8,128)S(1)} collective-permute-done((f32[192,128]{1,0:T(8,128)S(1)}, f32[192,128]{1,0:T(8,128)S(1)}, u32[]{:S(2)}, u32[]{:S(2)}) %collective-permute-start.2) | collective-permute-done | bytes 98336 | tf_op jit(solution)/shard_map/ppermute | solution.py:445
  16.5 1.9 %collective-permute-start.3 = (f32[288,128]{1,0:T(8,128)S(1)}, f32[288,128]{1,0:T(8,128)S(1)}, u32[]{:S(2)}, u32[]{:S(2)}) collective-permute-start(f32[288,128]{1,0:T(8,128)S(1)} %get-tuple-element.39), channel_id=1, source_target_pairs={{0,2},{2,0},{1,3},{3,1},{4,6},{6,4},{5,7},{7,5},{8,10},{10,8},{9,1... | collective-permute-start | bytes 442376 | tf_op jit(solution)/shard_map/ppermute | solution.py:445
  18.5 6.3 %collective-permute-start.4 = (f32[288,128]{1,0:T(8,128)S(1)}, f32[288,128]{1,0:T(8,128)S(1)}, u32[]{:S(2)}, u32[]{:S(2)}) collective-permute-start(f32[288,128]{1,0:T(8,128)S(1)} %shard_map.60), channel_id=1, source_target_pairs={{2,4},{4,2},{3,5},{5,3},{6,8},{8,6},{7,9},{9,7},{10,12},{12,10},{1... | collective-permute-start | bytes 442376 | tf_op jit(solution)/shard_map/ppermute | solution.py:445
  24.8 6.5 %collective-permute-done.4.refs_5_ = f32[288,128]{1,0:T(8,128)S(1)} collective-permute-done((f32[288,128]{1,0:T(8,128)S(1)}, f32[288,128]{1,0:T(8,128)S(1)}, u32[]{:S(2)}, u32[]{:S(2)}) %collective-permute-start.4) | collective-permute-done | bytes 147488 | tf_op jit(solution)/shard_map/ppermute | solution.py:445
  31.8 1.9 %collective-permute-start.5 = (f32[192,128]{1,0:T(8,128)S(1)}, f32[192,128]{1,0:T(8,128)S(1)}, u32[]{:S(2)}, u32[]{:S(2)}) collective-permute-start(f32[192,128]{1,0:T(8,128)S(1)} %get-tuple-element.43), channel_id=1, source_target_pairs={{0,1},{1,0},{2,3},{3,2},{4,5},{5,4},{6,7},{7,6},{8,9},{9,8},{10,11... | collective-permute-start | bytes 294920 | tf_op jit(solution)/shard_map/ppermute | solution.py:445
  34.4 5.4 %collective-permute-start.7 = (f32[192,128]{1,0:T(8,128)S(1)}, f32[192,128]{1,0:T(8,128)S(1)}, u32[]{:S(2)}, u32[]{:S(2)}) collective-permute-start(f32[192,128]{1,0:T(8,128)S(1)} %get-tuple-element.44), channel_id=1, source_target_pairs={{7,8},{8,7},{15,16},{16,15},{23,24},{24,23},{31,32},{32,31},{39,40... | collective-permute-start | bytes 294920 | tf_op jit(solution)/shard_map/ppermute | solution.py:445
  39.8 2.9 %collective-permute-done.7.near_across = f32[192,128]{1,0:T(8,128)S(1)} collective-permute-done((f32[192,128]{1,0:T(8,128)S(1)}, f32[192,128]{1,0:T(8,128)S(1)}, u32[]{:S(2)}, u32[]{:S(2)}) %collective-permute-start.7) | collective-permute-done | bytes 98336 | tf_op jit(solution)/shard_map/ppermute | solution.py:445
  42.8 1.9 %collective-permute-start.8 = (f32[288,128]{1,0:T(8,128)S(1)}, f32[288,128]{1,0:T(8,128)S(1)}, u32[]{:S(2)}, u32[]{:S(2)}) collective-permute-start(f32[288,128]{1,0:T(8,128)S(1)} %get-tuple-element.46), channel_id=1, source_target_pairs={{0,2},{2,0},{1,3},{3,1},{4,6},{6,4},{5,7},{7,5},{8,10},{10,8},{9,1... | collective-permute-start | bytes 442376 | tf_op jit(solution)/shard_map/ppermute | solution.py:445
  44.8 8.8 %collective-permute-start.9 = (f32[288,128]{1,0:T(8,128)S(1)}, f32[288,128]{1,0:T(8,128)S(1)}, u32[]{:S(2)}, u32[]{:S(2)}) collective-permute-start(f32[288,128]{1,0:T(8,128)S(1)} %shard_map.63), channel_id=1, source_target_pairs={{2,4},{4,2},{3,5},{5,3},{6,8},{8,6},{7,9},{9,7},{10,12},{12,10},{1... | collective-permute-start | bytes 442376 | tf_op jit(solution)/shard_map/ppermute | solution.py:445
  53.7 5.5 %collective-permute-done.9.refs_5_ = f32[288,128]{1,0:T(8,128)S(1)} collective-permute-done((f32[288,128]{1,0:T(8,128)S(1)}, f32[288,128]{1,0:T(8,128)S(1)}, u32[]{:S(2)}, u32[]{:S(2)}) %collective-permute-start.9) | collective-permute-done | bytes 147488 | tf_op jit(solution)/shard_map/ppermute | solution.py:445
  59.7 1.9 %collective-permute-start.10 = (f32[72,128]{1,0:T(8,128)S(1)}, f32[72,128]{1,0:T(8,128)S(1)}, u32[]{:S(2)}, u32[]{:S(2)}) collective-permute-start(f32[72,128]{1,0:T(8,128)S(1)} %get-tuple-element.48.own.block), channel_id=1, source_target_pairs={{8,16},{16,8},{9,17},{17,9},{10,18},{18,10},{11,19},{19,11},{12,20... | collective-permute-start | bytes 110600 | tf_op jit(solution)/shard_map/ppermute | solution.py:445
  65.8 4.8 %all-to-all-start = ((f32[8,144,128]{2,1,0:T(8,128)}), f32[8,144,128]{2,1,0:T(8,128)S(1)}, u32[]{:S(2)}, u32[]{:S(2)}) async-start(f32[8,144,128]{2,1,0:T(8,128)} %shard_map.65), calls=%async_computation | async-start | bytes 1179648 | tf_op jit(solution)/shard_map/all_to_all | solution.py:473
  70.6 3.4 %collective-permute-start.12 = (f32[192,128]{1,0:T(8,128)S(1)}, f32[192,128]{1,0:T(8,128)S(1)}, u32[]{:S(2)}, u32[]{:S(2)}) collective-permute-start(f32[192,128]{1,0:T(8,128)S(1)} %get-tuple-element.51), channel_id=1, source_target_pairs={{0,1},{1,0},{2,3},{3,2},{4,5},{5,4},{6,7},{7,6},{8,9},{9,8},{10,11... | collective-permute-start | bytes 294920 | tf_op jit(solution)/shard_map/ppermute | solution.py:445
  74.7 5.2 %collective-permute-start.14 = (f32[192,128]{1,0:T(8,128)S(1)}, f32[192,128]{1,0:T(8,128)S(1)}, u32[]{:S(2)}, u32[]{:S(2)}) collective-permute-start(f32[192,128]{1,0:T(8,128)S(1)} %get-tuple-element.52), channel_id=1, source_target_pairs={{7,8},{8,7},{15,16},{16,15},{23,24},{24,23},{31,32},{32,31},{39,40... | collective-permute-start | bytes 294920 | tf_op jit(solution)/shard_map/ppermute | solution.py:445
  79.9 7.5 %collective-permute-done.12.near_inner.refs_2_ = f32[192,128]{1,0:T(8,128)S(1)} collective-permute-done((f32[192,128]{1,0:T(8,128)S(1)}, f32[192,128]{1,0:T(8,128)S(1)}, u32[]{:S(2)}, u32[]{:S(2)}) %collective-permute-start.12) | collective-permute-done | bytes 98336 | tf_op jit(solution)/shard_map/ppermute | solution.py:445
  89.3 1.9 %collective-permute-start.15 = (f32[288,128]{1,0:T(8,128)S(1)}, f32[288,128]{1,0:T(8,128)S(1)}, u32[]{:S(2)}, u32[]{:S(2)}) collective-permute-start(f32[288,128]{1,0:T(8,128)S(1)} %get-tuple-element.54), channel_id=1, source_target_pairs={{0,2},{2,0},{1,3},{3,1},{4,6},{6,4},{5,7},{7,5},{8,10},{10,8},{9,1... | collective-permute-start | bytes 442376 | tf_op jit(solution)/shard_map/ppermute | solution.py:445
  91.3 6.0 %collective-permute-start.16 = (f32[288,128]{1,0:T(8,128)S(1)}, f32[288,128]{1,0:T(8,128)S(1)}, u32[]{:S(2)}, u32[]{:S(2)}) collective-permute-start(f32[288,128]{1,0:T(8,128)S(1)} %shard_map.67), channel_id=1, source_target_pairs={{2,4},{4,2},{3,5},{5,3},{6,8},{8,6},{7,9},{9,7},{10,12},{12,10},{1... | collective-permute-start | bytes 442376 | tf_op jit(solution)/shard_map/ppermute | solution.py:445
  97.4 3.7 %collective-permute-done.15.refs_4_ = f32[288,128]{1,0:T(8,128)S(1)} collective-permute-done((f32[288,128]{1,0:T(8,128)S(1)}, f32[288,128]{1,0:T(8,128)S(1)}, u32[]{:S(2)}, u32[]{:S(2)}) %collective-permute-start.15) | collective-permute-done | bytes 147488 | tf_op jit(solution)/shard_map/ppermute | solution.py:445
  101.0 3.0 %collective-permute-done.16.refs_5_ = f32[288,128]{1,0:T(8,128)S(1)} collective-permute-done((f32[288,128]{1,0:T(8,128)S(1)}, f32[288,128]{1,0:T(8,128)S(1)}, u32[]{:S(2)}, u32[]{:S(2)}) %collective-permute-start.16) | collective-permute-done | bytes 147488 | tf_op jit(solution)/shard_map/ppermute | solution.py:445
  104.0 2.6 %shard_map.68 = (f32[512,128]{1,0:T(8,128)S(1)}, f32[512,128]{1,0:T(8,128)S(1)}, f32[16,1,128]{2,1,0:T(1,128)S(1)}) custom-call(s32[1]{0:T(128)} %bitcast.device_ref, f32[512,128]{1,0:T(8,128)S(1)} %get-tuple-element.32.residual, f32[512,128]{1,0:T(8,128)S(1)} %get-tuple-element.47.smoothed, f32[72,128]{1,0:T(8,128)S(1)} %get-tuple-element.48.own.block, ...), custom_call_target="tpu_custom_call" | custom-call | tf_op jit(solution)/shard_map/pallas_call | solution.py:47
  106.7 12.4 %all_to_all.15.received = f32[16,1,128]{2,1,0:T(1,128)S(1)} all-to-all(f32[16,1,128]{2,1,0:T(1,128)S(1)} %get-tuple-element.55), channel_id=1, replica_groups=mesh['outer'=48,'pair'=2,'row'=8] {'pair','row'}, dimensions={0} | all-to-all | bytes 16384 | tf_op jit(solution)/shard_map/all_to_all | solution.py:507
  119.1 34.8 %all_to_all.16.received = f32[48,1,128]{2,1,0:T(1,128)S(1)} all-to-all(f32[48,1,128]{2,1,0:T(1,128)S(1)} %shard_map.69), channel_id=1, replica_groups=mesh['outer'=48,'pair'=2,'row'=8] {'outer'}, dimensions={0} | all-to-all | bytes 49152 | tf_op jit(solution)/shard_map/all_to_all | solution.py:509
  (34 shorter events, 13.5 us)
Async XLA Ops:
  0.6 0.7 copy-start.2
  0.7 0.7 copy-start.1
  1.3 0.9 copy-start
  2.9 10.4 %collective-permute-start = (f32[192,128]{1,0:T(8,128)S(1)}, f32[192,128]{1,0:T(8,128)S(1)}, u32[]{:S(2)}, u32[]{:S(2)}) collective-permute-start(f32[192,128]{1,0:T(8,128)S(1)} %get-tuple-element.35), channel_id=1, source_target_pairs={{0,1},{1,0},{2,3},{3,2},{4,5},{5,4},{6,7},{7,6},{8,9},{9,8},{10,11... | collective-permute-start | bytes 294920 | tf_op jit(solution)/shard_map/ppermute | solution.py:445
  7.0 6.4 %collective-permute-start.1 = (f32[192,128]{1,0:T(8,128)S(1)}, f32[192,128]{1,0:T(8,128)S(1)}, u32[]{:S(2)}, u32[]{:S(2)}) collective-permute-start(f32[192,128]{1,0:T(8,128)S(1)} %get-tuple-element.36), channel_id=1, source_target_pairs={{1,2},{2,1},{3,4},{4,3},{5,6},{6,5},{9,10},{10,9},{11,12},{12,11},... | collective-permute-start | bytes 294920 | tf_op jit(solution)/shard_map/ppermute | solution.py:445
  7.6 8.7 %collective-permute-start.2 = (f32[192,128]{1,0:T(8,128)S(1)}, f32[192,128]{1,0:T(8,128)S(1)}, u32[]{:S(2)}, u32[]{:S(2)}) collective-permute-start(f32[192,128]{1,0:T(8,128)S(1)} %get-tuple-element.36), channel_id=1, source_target_pairs={{7,8},{8,7},{15,16},{16,15},{23,24},{24,23},{31,32},{32,31},{39,40... | collective-permute-start | bytes 294920 | tf_op jit(solution)/shard_map/ppermute | solution.py:445
  16.5 8.3 %collective-permute-start.3 = (f32[288,128]{1,0:T(8,128)S(1)}, f32[288,128]{1,0:T(8,128)S(1)}, u32[]{:S(2)}, u32[]{:S(2)}) collective-permute-start(f32[288,128]{1,0:T(8,128)S(1)} %get-tuple-element.39), channel_id=1, source_target_pairs={{0,2},{2,0},{1,3},{3,1},{4,6},{6,4},{5,7},{7,5},{8,10},{10,8},{9,1... | collective-permute-start | bytes 442376 | tf_op jit(solution)/shard_map/ppermute | solution.py:445
  18.5 12.8 %collective-permute-start.4 = (f32[288,128]{1,0:T(8,128)S(1)}, f32[288,128]{1,0:T(8,128)S(1)}, u32[]{:S(2)}, u32[]{:S(2)}) collective-permute-start(f32[288,128]{1,0:T(8,128)S(1)} %shard_map.60), channel_id=1, source_target_pairs={{2,4},{4,2},{3,5},{5,3},{6,8},{8,6},{7,9},{9,7},{10,12},{12,10},{1... | collective-permute-start | bytes 442376 | tf_op jit(solution)/shard_map/ppermute | solution.py:445
  31.8 8.0 %collective-permute-start.5 = (f32[192,128]{1,0:T(8,128)S(1)}, f32[192,128]{1,0:T(8,128)S(1)}, u32[]{:S(2)}, u32[]{:S(2)}) collective-permute-start(f32[192,128]{1,0:T(8,128)S(1)} %get-tuple-element.43), channel_id=1, source_target_pairs={{0,1},{1,0},{2,3},{3,2},{4,5},{5,4},{6,7},{7,6},{8,9},{9,8},{10,11... | collective-permute-start | bytes 294920 | tf_op jit(solution)/shard_map/ppermute | solution.py:445
  33.8 6.1 %collective-permute-start.6 = (f32[192,128]{1,0:T(8,128)S(1)}, f32[192,128]{1,0:T(8,128)S(1)}, u32[]{:S(2)}, u32[]{:S(2)}) collective-permute-start(f32[192,128]{1,0:T(8,128)S(1)} %get-tuple-element.44), channel_id=1, source_target_pairs={{1,2},{2,1},{3,4},{4,3},{5,6},{6,5},{9,10},{10,9},{11,12},{12,11},... | collective-permute-start | bytes 294920 | tf_op jit(solution)/shard_map/ppermute | solution.py:445
  34.4 8.3 %collective-permute-start.7 = (f32[192,128]{1,0:T(8,128)S(1)}, f32[192,128]{1,0:T(8,128)S(1)}, u32[]{:S(2)}, u32[]{:S(2)}) collective-permute-start(f32[192,128]{1,0:T(8,128)S(1)} %get-tuple-element.44), channel_id=1, source_target_pairs={{7,8},{8,7},{15,16},{16,15},{23,24},{24,23},{31,32},{32,31},{39,40... | collective-permute-start | bytes 294920 | tf_op jit(solution)/shard_map/ppermute | solution.py:445
  42.8 10.8 %collective-permute-start.8 = (f32[288,128]{1,0:T(8,128)S(1)}, f32[288,128]{1,0:T(8,128)S(1)}, u32[]{:S(2)}, u32[]{:S(2)}) collective-permute-start(f32[288,128]{1,0:T(8,128)S(1)} %get-tuple-element.46), channel_id=1, source_target_pairs={{0,2},{2,0},{1,3},{3,1},{4,6},{6,4},{5,7},{7,5},{8,10},{10,8},{9,1... | collective-permute-start | bytes 442376 | tf_op jit(solution)/shard_map/ppermute | solution.py:445
  44.8 14.3 %collective-permute-start.9 = (f32[288,128]{1,0:T(8,128)S(1)}, f32[288,128]{1,0:T(8,128)S(1)}, u32[]{:S(2)}, u32[]{:S(2)}) collective-permute-start(f32[288,128]{1,0:T(8,128)S(1)} %shard_map.63), channel_id=1, source_target_pairs={{2,4},{4,2},{3,5},{5,3},{6,8},{8,6},{7,9},{9,7},{10,12},{12,10},{1... | collective-permute-start | bytes 442376 | tf_op jit(solution)/shard_map/ppermute | solution.py:445
  59.7 5.3 %collective-permute-start.10 = (f32[72,128]{1,0:T(8,128)S(1)}, f32[72,128]{1,0:T(8,128)S(1)}, u32[]{:S(2)}, u32[]{:S(2)}) collective-permute-start(f32[72,128]{1,0:T(8,128)S(1)} %get-tuple-element.48.own.block), channel_id=1, source_target_pairs={{8,16},{16,8},{9,17},{17,9},{10,18},{18,10},{11,19},{19,11},{12,20... | collective-permute-start | bytes 110600 | tf_op jit(solution)/shard_map/ppermute | solution.py:445
  61.6 3.4 %collective-permute-start.11 = (f32[72,128]{1,0:T(8,128)S(1)}, f32[72,128]{1,0:T(8,128)S(1)}, u32[]{:S(2)}, u32[]{:S(2)}) collective-permute-start(f32[72,128]{1,0:T(8,128)S(1)} %get-tuple-element.48.own.block), channel_id=1, source_target_pairs={{0,8},{8,0},{1,9},{9,1},{2,10},{10,2},{3,11},{11,3},{4,12},{12,4},... | collective-permute-start | bytes 110600 | tf_op jit(solution)/shard_map/ppermute | solution.py:445
  65.8 38.2 %all-to-all-start = ((f32[8,144,128]{2,1,0:T(8,128)}), f32[8,144,128]{2,1,0:T(8,128)S(1)}, u32[]{:S(2)}, u32[]{:S(2)}) async-start(f32[8,144,128]{2,1,0:T(8,128)} %shard_map.65), calls=%async_computation | async-start | bytes 1179648 | tf_op jit(solution)/shard_map/all_to_all | solution.py:473
  70.6 16.8 %collective-permute-start.12 = (f32[192,128]{1,0:T(8,128)S(1)}, f32[192,128]{1,0:T(8,128)S(1)}, u32[]{:S(2)}, u32[]{:S(2)}) collective-permute-start(f32[192,128]{1,0:T(8,128)S(1)} %get-tuple-element.51), channel_id=1, source_target_pairs={{0,1},{1,0},{2,3},{3,2},{4,5},{5,4},{6,7},{7,6},{8,9},{9,8},{10,11... | collective-permute-start | bytes 294920 | tf_op jit(solution)/shard_map/ppermute | solution.py:445
  74.0 13.4 %collective-permute-start.13 = (f32[192,128]{1,0:T(8,128)S(1)}, f32[192,128]{1,0:T(8,128)S(1)}, u32[]{:S(2)}, u32[]{:S(2)}) collective-permute-start(f32[192,128]{1,0:T(8,128)S(1)} %get-tuple-element.52), channel_id=1, source_target_pairs={{1,2},{2,1},{3,4},{4,3},{5,6},{6,5},{9,10},{10,9},{11,12},{12,11},... | collective-permute-start | bytes 294920 | tf_op jit(solution)/shard_map/ppermute | solution.py:445
  74.7 14.5 %collective-permute-start.14 = (f32[192,128]{1,0:T(8,128)S(1)}, f32[192,128]{1,0:T(8,128)S(1)}, u32[]{:S(2)}, u32[]{:S(2)}) collective-permute-start(f32[192,128]{1,0:T(8,128)S(1)} %get-tuple-element.52), channel_id=1, source_target_pairs={{7,8},{8,7},{15,16},{16,15},{23,24},{24,23},{31,32},{32,31},{39,40... | collective-permute-start | bytes 294920 | tf_op jit(solution)/shard_map/ppermute | solution.py:445
  89.3 11.7 %collective-permute-start.15 = (f32[288,128]{1,0:T(8,128)S(1)}, f32[288,128]{1,0:T(8,128)S(1)}, u32[]{:S(2)}, u32[]{:S(2)}) collective-permute-start(f32[288,128]{1,0:T(8,128)S(1)} %get-tuple-element.54), channel_id=1, source_target_pairs={{0,2},{2,0},{1,3},{3,1},{4,6},{6,4},{5,7},{7,5},{8,10},{10,8},{9,1... | collective-permute-start | bytes 442376 | tf_op jit(solution)/shard_map/ppermute | solution.py:445
  91.3 12.7 %collective-permute-start.16 = (f32[288,128]{1,0:T(8,128)S(1)}, f32[288,128]{1,0:T(8,128)S(1)}, u32[]{:S(2)}, u32[]{:S(2)}) collective-permute-start(f32[288,128]{1,0:T(8,128)S(1)} %shard_map.67), channel_id=1, source_target_pairs={{2,4},{4,2},{3,5},{5,3},{6,8},{8,6},{7,9},{9,7},{10,12},{12,10},{1... | collective-permute-start | bytes 442376 | tf_op jit(solution)/shard_map/ppermute | solution.py:445

commit v7 on v6

--- a/solution.py
+++ b/solution.py
@@ -255,7 +255,7 @@
 
 
 def defect_kernel(residual, second, *refs):
-    *faces, table, smoothed, block, out_up, out_down, out_inner, out_outer, ghosts, sums = refs
+    *faces, table, smoothed, blocks, out_up, out_down, out_inner, out_outer, ghosts, sums = refs
     read_ghosts(table, faces, ghosts, FINE)
     for big_x in range(4):
         for big_y in range(4):
@@ -269,26 +269,13 @@
                     total = part if total is None else total + part
             at = 32 * big_x + 8 * big_y
             sums[at : at + 8, :] = total
-    block[0:64, :] = (sums[pl.ds(0, 64, stride=2), :] + sums[pl.ds(1, 64, stride=2), :]) * 0.125
-    block[64:72, :] = table[NEIGHBOUR_ROW : NEIGHBOUR_ROW + 8, :].astype(jnp.float32)
+    restricted = (sums[pl.ds(0, 64, stride=2), :] + sums[pl.ds(1, 64, stride=2), :]) * 0.125
+    marks = table[NEIGHBOUR_ROW : NEIGHBOUR_ROW + 8, :].astype(jnp.float32)
+    for copy in range(blocks.shape[0]):
+        blocks[copy, 0:64, :] = restricted
+        blocks[copy, 64:72, :] = marks
     write_faces(smoothed, out_up, out_down)
     write_pair(table, UPPER_NEAR, out_up, out_down, out_inner, out_outer, FINE)
-
-
-def spread_kernel(device_ref, own, across, beside_row, out):
-    column = device_ref[0] % out.shape[0]
-    odd_row = (device_ref[0] // out.shape[0]) % 2
-    after_is_beside = jnp.full((8, LANES), odd_row, jnp.int32) == 0
-    for target in range(out.shape[0]):
-        stays = jnp.full((8, LANES), column, jnp.int32) == target
-        from_before = jnp.where(column >= target, 1, 0)
-        same = jnp.full((8, LANES), jnp.where(odd_row == from_before, 1, 0), jnp.int32) > 0
-        for row in range(0, BLOCK, 8):
-            near = beside_row[row : row + 8, :]
-            far = across[row : row + 8, :]
-            after = jnp.where(after_is_beside, near, far)
-            out[target, row : row + 8, :] = jnp.where(stays, after, own[row : row + 8, :])
-            out[target, BLOCK + row : BLOCK + row + 8, :] = jnp.where(same, near, far)
 
 
 def coarse_update(first, at, ghosts, low_y, high_y, low_z, high_z):
@@ -309,20 +296,24 @@
     return centre + (centre - RELAX_COARSE * ((6.0 * centre - around) * 0.25))
 
 
-def coarse_correction(device, block, received, scratch):
+def coarse_correction(device, in_rows, across_rows, beside_rows, scratch):
     first, first_faces, slots, coarse, coarse_faces, ghosts, low_y, high_y, low_z, high_z, extended, across = scratch
-    row_length = received.shape[0]
+    row_length = in_rows.shape[0]
     column = lax.rem(device, row_length)
+    odd_row = lax.rem(device // row_length, 2)
     for index in range(2 * WIDEST + 1):
         offset = index - WIDEST
-        if offset:
-            place = column + offset
-            sender = lax.rem(place + row_length, row_length)
-            in_row = (place >= 0) & (place < row_length)
-            start = 0 if offset == WIDEST else jnp.where(in_row, 0, BLOCK)
-            rows = lambda row: received[sender, pl.ds(pl.multiple_of(start + row, 8), 8), :]
-        else:
-            rows = lambda row: block[row : row + 8, :]
+        place = column + offset
+        sender = lax.rem(place + row_length, row_length)
+        inside = jnp.where((place >= 0) & (place < row_length), 1, 0)
+        same = jnp.where(odd_row == jnp.where(place < 0, 1, 0), 1, 0)
+        is_inside = jnp.full((8, LANES), inside, jnp.int32) > 0
+        is_beside = jnp.full((8, LANES), same, jnp.int32) > 0
+
+        def rows(row):
+            outside = jnp.where(is_beside, beside_rows[sender, row : row + 8, :], across_rows[sender, row : row + 8, :])
+            return jnp.where(is_inside, in_rows[sender, row : row + 8, :], outside)
+
         for row in range(0, 64, 8):
             first[64 * index + row : 64 * index + row + 8, :] = RELAX_COARSE * rows(row)
         write_coarse_faces(first, 64 * index, first_faces, 96 * index)
@@ -346,11 +337,11 @@
     return first[0:64, :]
 
 
-def image_kernel(device_ref, residual, smoothed, block, received, *refs):
+def image_kernel(device_ref, residual, smoothed, in_rows, across_rows, beside_rows, *refs):
     *faces, table, direction, image, sums, fine_ghosts, wide, wide_across, wide_own, spread = refs[: 7 + 3 + 5]
     scratch = refs[7 + 3 + 5 :]
     coarse_faces, across = scratch[4], scratch[-1]
-    own = coarse_correction(device_ref[0], block, received, scratch)
+    own = coarse_correction(device_ref[0], in_rows, across_rows, beside_rows, scratch)
     sub = lax.broadcasted_iota(jnp.int32, (8, LANES), 0)
     for half in (0, 1):
         wide[pl.ds(half, 64, stride=2), :] = own
@@ -462,15 +453,12 @@
     return up, down, near_inner, near_outer, far_inner, far_outer, table
 
 
-def share(block, device):
+def share(blocks):
     row_length = lax.axis_size("row")
-    across = swap(block, row_length, row_length)
-    beside_row = swap(block, row_length, 0)
-    (blocks,) = call(
-        spread_kernel, [f32(row_length, 2 * BLOCK, LANES)], device, block, across, beside_row,
-        in_specs=[SMEM, VMEM, VMEM, VMEM],
-    )
-    return lax.all_to_all(blocks, "row", 0, 0, tiled=True)
+    in_rows = lax.all_to_all(blocks, "row", 0, 0, tiled=True)
+    across_rows = swap(in_rows, row_length, row_length)
+    beside_rows = swap(in_rows, row_length, 0)
+    return in_rows, across_rows, beside_rows
 
 
 def step(right_side, counts, neighbours):
@@ -487,19 +475,19 @@
     second, *sides = call(
         smooth_kernel, [fine, *faces], residual_in, *exchange(FINE, *sides, table), scratch=[fine_ghosts]
     )
-    smoothed, block, *sides = call(
-        defect_kernel, [fine, f32(BLOCK, LANES), *faces],
+    smoothed, blocks, *sides = call(
+        defect_kernel, [fine, f32(lax.axis_size("row"), BLOCK, LANES), *faces],
         residual_in, second, *exchange(FINE, *sides, table), scratch=[fine_ghosts, scratch(128)],
     )
-    blocks, wide_blocks, near_blocks = 2 * WIDEST + 1, 4 * REACH + 1, 2 * REACH + 1
+    all_blocks, wide_blocks, near_blocks = 2 * WIDEST + 1, 4 * REACH + 1, 2 * REACH + 1
     exchanged = exchange(FINE, *sides, table)
     direction, image, sums = call(
         image_kernel, [fine, fine, f32(lax.axis_size(AXES[1:]), 1, LANES)],
-        device, residual_in, smoothed, block, share(block, device), *exchanged,
-        in_specs=[SMEM] + [VMEM] * 11,
+        device, residual_in, smoothed, *share(blocks), *exchanged,
+        in_specs=[SMEM] + [VMEM] * 12,
         scratch=[
             fine_ghosts, scratch(128), scratch(384), scratch(192), scratch(512),
-            scratch(64 * blocks), scratch(96 * blocks), pltpu.VMEM((8 * wide_blocks, LANES), jnp.int32),
+            scratch(64 * all_blocks), scratch(96 * all_blocks), pltpu.VMEM((8 * wide_blocks, LANES), jnp.int32),
             scratch(64), scratch(96 * wide_blocks), scratch(96), *[scratch(64)] * 4,
             scratch(192 * near_blocks), scratch(192),
         ],

time: 156 us -> 156 us (level)
  blocking collectives: 47.1 us -> 57.6 us
  waiting for transfers between devices: 35.2 us -> 29.4 us
  starting transfers between devices: 63.1 us -> 59.3 us
    all_to_all x0 -> x1, blocking collectives: none -> 12.1 us  [share(): in_rows = lax.all_to_all(blocks, 'row', 0, 0, tiled=True)]
    ppermute x17, waiting for transfers between devices: 35.2 us -> 29.4 us  [swap(): return lax.ppermute(block, AXES, route)]
    all_to_all x1 -> x0, starting transfers between devices: 4.79 us -> none  [share(): return lax.all_to_all(blocks, 'row', 0, 0, tiled=True)]
    pallas_call x13 -> x12, Pallas kernels: 6.89 us -> 6.18 us  [call(): pl.pallas_call(kernel, out_shape=outs, in_specs=in_specs or [VMEM] * len(...]
  transfers between devices with their start and end apart: 18 -> 17, of which waited for: 9 -> 8; matrix products, arithmetic and copies ran while one was open for 0% -> 0% of each run, Pallas kernels for 0% -> 0%
where the time goes in v7:
time: 156 us
  starting transfers between devices  59.3 us (38%)
  blocking collectives  57.6 us (37%)
  waiting for transfers between devices  29.4 us (19%)
  Pallas kernels  6.18 us (4%)
  local copies, waits for them, and re-layouts  2.15 us (1%)
    ppermute x17, starting transfers between devices, swap(): return lax.ppermute(block, AXES, route)  59.3 us
    all_to_all x1, blocking collectives, step(): received = lax.all_to_all(sums, 'outer', 0, 0, tiled=True)  33.4 us
    ppermute x17, waiting for transfers between devices, swap(): return lax.ppermute(block, AXES, route)  29.4 us
    all_to_all x1, blocking collectives, step(): received = lax.all_to_all(sums, AXES[1:], 0, 0, tiled=True)  12.2 us
    all_to_all x1, blocking collectives, share(): in_rows = lax.all_to_all(blocks, 'row', 0, 0, tiled=True)  12.1 us
    pallas_call x12, Pallas kernels, call(): pl.pallas_call(kernel, out_shape=outs, in_specs=in_specs or [VMEM] * len(...  6.18 us
  transfers between devices with their start and end apart: 17, of which 8 were waited for; matrix products, arithmetic and copies ran while one was open for 0% of the time, Pallas kernels for 0%

profile of v7, /device:TPU:1, one launch (start us, length us, event | category | flops | bytes accessed | tf_op | source)
XLA Modules:
  0.0 155.5 jit_solution(16693883167896433987)
XLA Ops:
  2.9 4.0 %collective-permute-start = (f32[192,128]{1,0:T(8,128)S(1)}, f32[192,128]{1,0:T(8,128)S(1)}, u32[]{:S(2)}, u32[]{:S(2)}) collective-permute-start(f32[192,128]{1,0:T(8,128)S(1)} %get-tuple-element.35), channel_id=1, source_target_pairs={{0,1},{1,0},{2,3},{3,2},{4,5},{5,4},{6,7},{7,6},{8,9},{9,8},{10,11... | collective-permute-start | bytes 294920 | tf_op jit(solution)/shard_map/ppermute | solution.py:436
  7.0 5.7 %collective-permute-start.2 = (f32[192,128]{1,0:T(8,128)S(1)}, f32[192,128]{1,0:T(8,128)S(1)}, u32[]{:S(2)}, u32[]{:S(2)}) collective-permute-start(f32[192,128]{1,0:T(8,128)S(1)} %get-tuple-element.36), channel_id=1, source_target_pairs={{7,8},{8,7},{15,16},{16,15},{23,24},{24,23},{31,32},{32,31},{39,40... | collective-permute-start | bytes 294920 | tf_op jit(solution)/shard_map/ppermute | solution.py:436
  13.4 2.3 %collective-permute-done.2.near_across = f32[192,128]{1,0:T(8,128)S(1)} collective-permute-done((f32[192,128]{1,0:T(8,128)S(1)}, f32[192,128]{1,0:T(8,128)S(1)}, u32[]{:S(2)}, u32[]{:S(2)}) %collective-permute-start.2) | collective-permute-done | bytes 98336 | tf_op jit(solution)/shard_map/ppermute | solution.py:436
  15.8 1.9 %collective-permute-start.3 = (f32[288,128]{1,0:T(8,128)S(1)}, f32[288,128]{1,0:T(8,128)S(1)}, u32[]{:S(2)}, u32[]{:S(2)}) collective-permute-start(f32[288,128]{1,0:T(8,128)S(1)} %get-tuple-element.39), channel_id=1, source_target_pairs={{0,2},{2,0},{1,3},{3,1},{4,6},{6,4},{5,7},{7,5},{8,10},{10,8},{9,1... | collective-permute-start | bytes 442376 | tf_op jit(solution)/shard_map/ppermute | solution.py:436
  17.8 7.6 %collective-permute-start.4 = (f32[288,128]{1,0:T(8,128)S(1)}, f32[288,128]{1,0:T(8,128)S(1)}, u32[]{:S(2)}, u32[]{:S(2)}) collective-permute-start(f32[288,128]{1,0:T(8,128)S(1)} %shard_map.60), channel_id=1, source_target_pairs={{2,4},{4,2},{3,5},{5,3},{6,8},{8,6},{7,9},{9,7},{10,12},{12,10},{1... | collective-permute-start | bytes 442376 | tf_op jit(solution)/shard_map/ppermute | solution.py:436
  25.5 6.4 %collective-permute-done.4.refs_5_ = f32[288,128]{1,0:T(8,128)S(1)} collective-permute-done((f32[288,128]{1,0:T(8,128)S(1)}, f32[288,128]{1,0:T(8,128)S(1)}, u32[]{:S(2)}, u32[]{:S(2)}) %collective-permute-start.4) | collective-permute-done | bytes 147488 | tf_op jit(solution)/shard_map/ppermute | solution.py:436
  32.4 1.9 %collective-permute-start.5 = (f32[192,128]{1,0:T(8,128)S(1)}, f32[192,128]{1,0:T(8,128)S(1)}, u32[]{:S(2)}, u32[]{:S(2)}) collective-permute-start(f32[192,128]{1,0:T(8,128)S(1)} %get-tuple-element.43), channel_id=1, source_target_pairs={{0,1},{1,0},{2,3},{3,2},{4,5},{5,4},{6,7},{7,6},{8,9},{9,8},{10,11... | collective-permute-start | bytes 294920 | tf_op jit(solution)/shard_map/ppermute | solution.py:436
  34.4 7.0 %collective-permute-start.7 = (f32[192,128]{1,0:T(8,128)S(1)}, f32[192,128]{1,0:T(8,128)S(1)}, u32[]{:S(2)}, u32[]{:S(2)}) collective-permute-start(f32[192,128]{1,0:T(8,128)S(1)} %get-tuple-element.44), channel_id=1, source_target_pairs={{7,8},{8,7},{15,16},{16,15},{23,24},{24,23},{31,32},{32,31},{39,40... | collective-permute-start | bytes 294920 | tf_op jit(solution)/shard_map/ppermute | solution.py:436
  42.1 2.4 %collective-permute-done.7.near_across = f32[192,128]{1,0:T(8,128)S(1)} collective-permute-done((f32[192,128]{1,0:T(8,128)S(1)}, f32[192,128]{1,0:T(8,128)S(1)}, u32[]{:S(2)}, u32[]{:S(2)}) %collective-permute-start.7) | collective-permute-done | bytes 98336 | tf_op jit(solution)/shard_map/ppermute | solution.py:436
  44.6 1.9 %collective-permute-start.8 = (f32[288,128]{1,0:T(8,128)S(1)}, f32[288,128]{1,0:T(8,128)S(1)}, u32[]{:S(2)}, u32[]{:S(2)}) collective-permute-start(f32[288,128]{1,0:T(8,128)S(1)} %get-tuple-element.46), channel_id=1, source_target_pairs={{0,2},{2,0},{1,3},{3,1},{4,6},{6,4},{5,7},{7,5},{8,10},{10,8},{9,1... | collective-permute-start | bytes 442376 | tf_op jit(solution)/shard_map/ppermute | solution.py:436
  46.6 8.1 %collective-permute-start.9 = (f32[288,128]{1,0:T(8,128)S(1)}, f32[288,128]{1,0:T(8,128)S(1)}, u32[]{:S(2)}, u32[]{:S(2)}) collective-permute-start(f32[288,128]{1,0:T(8,128)S(1)} %shard_map.63), channel_id=1, source_target_pairs={{2,4},{4,2},{3,5},{5,3},{6,8},{8,6},{7,9},{9,7},{10,12},{12,10},{1... | collective-permute-start | bytes 442376 | tf_op jit(solution)/shard_map/ppermute | solution.py:436
  54.8 5.7 %collective-permute-done.9.refs_5_ = f32[288,128]{1,0:T(8,128)S(1)} collective-permute-done((f32[288,128]{1,0:T(8,128)S(1)}, f32[288,128]{1,0:T(8,128)S(1)}, u32[]{:S(2)}, u32[]{:S(2)}) %collective-permute-start.9) | collective-permute-done | bytes 147488 | tf_op jit(solution)/shard_map/ppermute | solution.py:436
  61.0 12.1 %all_to_all.15.in_rows = f32[8,72,128]{2,1,0:T(8,128)S(1)} all-to-all(f32[8,72,128]{2,1,0:T(8,128)S(1)} %get-tuple-element.48), channel_id=1, replica_groups=mesh['outer'=48,'pair'=2,'row'=8] {'row'}, dimensions={0} | all-to-all | bytes 589824 | tf_op jit(solution)/shard_map/all_to_all | solution.py:458
  73.1 6.7 %collective-permute-start.11 = (f32[8,72,128]{2,1,0:T(8,128)S(1)}, f32[8,72,128]{2,1,0:T(8,128)S(1)}, u32[]{:S(2)}, u32[]{:S(2)}) collective-permute-start(f32[8,72,128]{2,1,0:T(8,128)S(1)} %all_to_all.15.in_rows), channel_id=1, source_target_pairs={{0,8},{8,0},{1,9},{9,1},{2,10},{10,2},{3,11},{11,3},{4,12},{12,4},... | collective-permute-start | bytes 884744 | tf_op jit(solution)/shard_map/ppermute | solution.py:436
  79.8 1.9 %collective-permute-start.10 = (f32[8,72,128]{2,1,0:T(8,128)S(1)}, f32[8,72,128]{2,1,0:T(8,128)S(1)}, u32[]{:S(2)}, u32[]{:S(2)}) collective-permute-start(f32[8,72,128]{2,1,0:T(8,128)S(1)} %all_to_all.15.in_rows), channel_id=1, source_target_pairs={{8,16},{16,8},{9,17},{17,9},{10,18},{18,10},{11,19},{19,11},{12,20... | collective-permute-start | bytes 884744 | tf_op jit(solution)/shard_map/ppermute | solution.py:436
  81.8 2.1 %collective-permute-start.12 = (f32[192,128]{1,0:T(8,128)S(1)}, f32[192,128]{1,0:T(8,128)S(1)}, u32[]{:S(2)}, u32[]{:S(2)}) collective-permute-start(f32[192,128]{1,0:T(8,128)S(1)} %get-tuple-element.51), channel_id=1, source_target_pairs={{0,1},{1,0},{2,3},{3,2},{4,5},{5,4},{6,7},{7,6},{8,9},{9,8},{10,11... | collective-permute-start | bytes 294920 | tf_op jit(solution)/shard_map/ppermute | solution.py:436
  87.4 3.7 %collective-permute-done.14.near_across = f32[192,128]{1,0:T(8,128)S(1)} collective-permute-done((f32[192,128]{1,0:T(8,128)S(1)}, f32[192,128]{1,0:T(8,128)S(1)}, u32[]{:S(2)}, u32[]{:S(2)}) %collective-permute-start.14) | collective-permute-done | bytes 98336 | tf_op jit(solution)/shard_map/ppermute | solution.py:436
  91.2 2.0 %collective-permute-start.15 = (f32[288,128]{1,0:T(8,128)S(1)}, f32[288,128]{1,0:T(8,128)S(1)}, u32[]{:S(2)}, u32[]{:S(2)}) collective-permute-start(f32[288,128]{1,0:T(8,128)S(1)} %get-tuple-element.54), channel_id=1, source_target_pairs={{0,2},{2,0},{1,3},{3,1},{4,6},{6,4},{5,7},{7,5},{8,10},{10,8},{9,1... | collective-permute-start | bytes 442376 | tf_op jit(solution)/shard_map/ppermute | solution.py:436
  93.3 4.3 %collective-permute-start.16 = (f32[288,128]{1,0:T(8,128)S(1)}, f32[288,128]{1,0:T(8,128)S(1)}, u32[]{:S(2)}, u32[]{:S(2)}) collective-permute-start(f32[288,128]{1,0:T(8,128)S(1)} %shard_map.66), channel_id=1, source_target_pairs={{2,4},{4,2},{3,5},{5,3},{6,8},{8,6},{7,9},{9,7},{10,12},{12,10},{1... | collective-permute-start | bytes 442376 | tf_op jit(solution)/shard_map/ppermute | solution.py:436
  97.6 3.5 %collective-permute-done.15.refs_4_ = f32[288,128]{1,0:T(8,128)S(1)} collective-permute-done((f32[288,128]{1,0:T(8,128)S(1)}, f32[288,128]{1,0:T(8,128)S(1)}, u32[]{:S(2)}, u32[]{:S(2)}) %collective-permute-start.15) | collective-permute-done | bytes 147488 | tf_op jit(solution)/shard_map/ppermute | solution.py:436
  101.1 4.6 %collective-permute-done.16.refs_5_ = f32[288,128]{1,0:T(8,128)S(1)} collective-permute-done((f32[288,128]{1,0:T(8,128)S(1)}, f32[288,128]{1,0:T(8,128)S(1)}, u32[]{:S(2)}, u32[]{:S(2)}) %collective-permute-start.16) | collective-permute-done | bytes 147488 | tf_op jit(solution)/shard_map/ppermute | solution.py:436
  105.7 2.7 %shard_map.67 = (f32[512,128]{1,0:T(8,128)S(1)}, f32[512,128]{1,0:T(8,128)S(1)}, f32[16,1,128]{2,1,0:T(1,128)S(1)}) custom-call(s32[1]{0:T(128)} %bitcast.device_ref, f32[512,128]{1,0:T(8,128)S(1)} %get-tuple-element.32.residual, f32[512,128]{1,0:T(8,128)S(1)} %get-tuple-element.47.smoothed, f32[8,72,128]{2,1,0:T(8,128)S(1)} %all_to_all.15.in_rows, ...), custom_call_target="tpu_custom_call" | custom-call | tf_op jit(solution)/shard_map/pallas_call | solution.py:47
  108.4 12.2 %all_to_all.16.received = f32[16,1,128]{2,1,0:T(1,128)S(1)} all-to-all(f32[16,1,128]{2,1,0:T(1,128)S(1)} %get-tuple-element.55), channel_id=1, replica_groups=mesh['outer'=48,'pair'=2,'row'=8] {'pair','row'}, dimensions={0} | all-to-all | bytes 16384 | tf_op jit(solution)/shard_map/all_to_all | solution.py:495
  120.6 33.4 %all_to_all.17.received = f32[48,1,128]{2,1,0:T(1,128)S(1)} all-to-all(f32[48,1,128]{2,1,0:T(1,128)S(1)} %shard_map.68), channel_id=1, replica_groups=mesh['outer'=48,'pair'=2,'row'=8] {'outer'}, dimensions={0} | all-to-all | bytes 49152 | tf_op jit(solution)/shard_map/all_to_all | solution.py:497
  (32 shorter events, 10.4 us)
Async XLA Ops:
  0.6 0.7 copy-start.2
  0.7 0.7 copy-start.1
  1.3 0.9 copy-start
  2.9 10.4 %collective-permute-start = (f32[192,128]{1,0:T(8,128)S(1)}, f32[192,128]{1,0:T(8,128)S(1)}, u32[]{:S(2)}, u32[]{:S(2)}) collective-permute-start(f32[192,128]{1,0:T(8,128)S(1)} %get-tuple-element.35), channel_id=1, source_target_pairs={{0,1},{1,0},{2,3},{3,2},{4,5},{5,4},{6,7},{7,6},{8,9},{9,8},{10,11... | collective-permute-start | bytes 294920 | tf_op jit(solution)/shard_map/ppermute | solution.py:436
  7.0 8.7 %collective-permute-start.2 = (f32[192,128]{1,0:T(8,128)S(1)}, f32[192,128]{1,0:T(8,128)S(1)}, u32[]{:S(2)}, u32[]{:S(2)}) collective-permute-start(f32[192,128]{1,0:T(8,128)S(1)} %get-tuple-element.36), channel_id=1, source_target_pairs={{7,8},{8,7},{15,16},{16,15},{23,24},{24,23},{31,32},{32,31},{39,40... | collective-permute-start | bytes 294920 | tf_op jit(solution)/shard_map/ppermute | solution.py:436
  12.7 3.0 %collective-permute-start.1 = (f32[192,128]{1,0:T(8,128)S(1)}, f32[192,128]{1,0:T(8,128)S(1)}, u32[]{:S(2)}, u32[]{:S(2)}) collective-permute-start(f32[192,128]{1,0:T(8,128)S(1)} %get-tuple-element.36), channel_id=1, source_target_pairs={{1,2},{2,1},{3,4},{4,3},{5,6},{6,5},{9,10},{10,9},{11,12},{12,11},... | collective-permute-start | bytes 294920 | tf_op jit(solution)/shard_map/ppermute | solution.py:436
  15.8 9.7 %collective-permute-start.3 = (f32[288,128]{1,0:T(8,128)S(1)}, f32[288,128]{1,0:T(8,128)S(1)}, u32[]{:S(2)}, u32[]{:S(2)}) collective-permute-start(f32[288,128]{1,0:T(8,128)S(1)} %get-tuple-element.39), channel_id=1, source_target_pairs={{0,2},{2,0},{1,3},{3,1},{4,6},{6,4},{5,7},{7,5},{8,10},{10,8},{9,1... | collective-permute-start | bytes 442376 | tf_op jit(solution)/shard_map/ppermute | solution.py:436
  17.8 14.0 %collective-permute-start.4 = (f32[288,128]{1,0:T(8,128)S(1)}, f32[288,128]{1,0:T(8,128)S(1)}, u32[]{:S(2)}, u32[]{:S(2)}) collective-permute-start(f32[288,128]{1,0:T(8,128)S(1)} %shard_map.60), channel_id=1, source_target_pairs={{2,4},{4,2},{3,5},{5,3},{6,8},{8,6},{7,9},{9,7},{10,12},{12,10},{1... | collective-permute-start | bytes 442376 | tf_op jit(solution)/shard_map/ppermute | solution.py:436
  32.4 9.7 %collective-permute-start.5 = (f32[192,128]{1,0:T(8,128)S(1)}, f32[192,128]{1,0:T(8,128)S(1)}, u32[]{:S(2)}, u32[]{:S(2)}) collective-permute-start(f32[192,128]{1,0:T(8,128)S(1)} %get-tuple-element.43), channel_id=1, source_target_pairs={{0,1},{1,0},{2,3},{3,2},{4,5},{5,4},{6,7},{7,6},{8,9},{9,8},{10,11... | collective-permute-start | bytes 294920 | tf_op jit(solution)/shard_map/ppermute | solution.py:436
  34.4 10.1 %collective-permute-start.7 = (f32[192,128]{1,0:T(8,128)S(1)}, f32[192,128]{1,0:T(8,128)S(1)}, u32[]{:S(2)}, u32[]{:S(2)}) collective-permute-start(f32[192,128]{1,0:T(8,128)S(1)} %get-tuple-element.44), channel_id=1, source_target_pairs={{7,8},{8,7},{15,16},{16,15},{23,24},{24,23},{31,32},{32,31},{39,40... | collective-permute-start | bytes 294920 | tf_op jit(solution)/shard_map/ppermute | solution.py:436
  41.4 3.1 %collective-permute-start.6 = (f32[192,128]{1,0:T(8,128)S(1)}, f32[192,128]{1,0:T(8,128)S(1)}, u32[]{:S(2)}, u32[]{:S(2)}) collective-permute-start(f32[192,128]{1,0:T(8,128)S(1)} %get-tuple-element.44), channel_id=1, source_target_pairs={{1,2},{2,1},{3,4},{4,3},{5,6},{6,5},{9,10},{10,9},{11,12},{12,11},... | collective-permute-start | bytes 294920 | tf_op jit(solution)/shard_map/ppermute | solution.py:436
  44.6 10.2 %collective-permute-start.8 = (f32[288,128]{1,0:T(8,128)S(1)}, f32[288,128]{1,0:T(8,128)S(1)}, u32[]{:S(2)}, u32[]{:S(2)}) collective-permute-start(f32[288,128]{1,0:T(8,128)S(1)} %get-tuple-element.46), channel_id=1, source_target_pairs={{0,2},{2,0},{1,3},{3,1},{4,6},{6,4},{5,7},{7,5},{8,10},{10,8},{9,1... | collective-permute-start | bytes 442376 | tf_op jit(solution)/shard_map/ppermute | solution.py:436
  46.6 13.8 %collective-permute-start.9 = (f32[288,128]{1,0:T(8,128)S(1)}, f32[288,128]{1,0:T(8,128)S(1)}, u32[]{:S(2)}, u32[]{:S(2)}) collective-permute-start(f32[288,128]{1,0:T(8,128)S(1)} %shard_map.63), channel_id=1, source_target_pairs={{2,4},{4,2},{3,5},{5,3},{6,8},{8,6},{7,9},{9,7},{10,12},{12,10},{1... | collective-permute-start | bytes 442376 | tf_op jit(solution)/shard_map/ppermute | solution.py:436
  73.1 32.6 %collective-permute-start.11 = (f32[8,72,128]{2,1,0:T(8,128)S(1)}, f32[8,72,128]{2,1,0:T(8,128)S(1)}, u32[]{:S(2)}, u32[]{:S(2)}) collective-permute-start(f32[8,72,128]{2,1,0:T(8,128)S(1)} %all_to_all.15.in_rows), channel_id=1, source_target_pairs={{0,8},{8,0},{1,9},{9,1},{2,10},{10,2},{3,11},{11,3},{4,12},{12,4},... | collective-permute-start | bytes 884744 | tf_op jit(solution)/shard_map/ppermute | solution.py:436
  79.8 25.9 %collective-permute-start.10 = (f32[8,72,128]{2,1,0:T(8,128)S(1)}, f32[8,72,128]{2,1,0:T(8,128)S(1)}, u32[]{:S(2)}, u32[]{:S(2)}) collective-permute-start(f32[8,72,128]{2,1,0:T(8,128)S(1)} %all_to_all.15.in_rows), channel_id=1, source_target_pairs={{8,16},{16,8},{9,17},{17,9},{10,18},{18,10},{11,19},{19,11},{12,20... | collective-permute-start | bytes 884744 | tf_op jit(solution)/shard_map/ppermute | solution.py:436
  81.8 5.6 %collective-permute-start.12 = (f32[192,128]{1,0:T(8,128)S(1)}, f32[192,128]{1,0:T(8,128)S(1)}, u32[]{:S(2)}, u32[]{:S(2)}) collective-permute-start(f32[192,128]{1,0:T(8,128)S(1)} %get-tuple-element.51), channel_id=1, source_target_pairs={{0,1},{1,0},{2,3},{3,2},{4,5},{5,4},{6,7},{7,6},{8,9},{9,8},{10,11... | collective-permute-start | bytes 294920 | tf_op jit(solution)/shard_map/ppermute | solution.py:436
  83.9 7.1 %collective-permute-start.14 = (f32[192,128]{1,0:T(8,128)S(1)}, f32[192,128]{1,0:T(8,128)S(1)}, u32[]{:S(2)}, u32[]{:S(2)}) collective-permute-start(f32[192,128]{1,0:T(8,128)S(1)} %get-tuple-element.52), channel_id=1, source_target_pairs={{7,8},{8,7},{15,16},{16,15},{23,24},{24,23},{31,32},{32,31},{39,40... | collective-permute-start | bytes 294920 | tf_op jit(solution)/shard_map/ppermute | solution.py:436
  85.8 5.2 %collective-permute-start.13 = (f32[192,128]{1,0:T(8,128)S(1)}, f32[192,128]{1,0:T(8,128)S(1)}, u32[]{:S(2)}, u32[]{:S(2)}) collective-permute-start(f32[192,128]{1,0:T(8,128)S(1)} %get-tuple-element.52), channel_id=1, source_target_pairs={{1,2},{2,1},{3,4},{4,3},{5,6},{6,5},{9,10},{10,9},{11,12},{12,11},... | collective-permute-start | bytes 294920 | tf_op jit(solution)/shard_map/ppermute | solution.py:436
  91.2 9.9 %collective-permute-start.15 = (f32[288,128]{1,0:T(8,128)S(1)}, f32[288,128]{1,0:T(8,128)S(1)}, u32[]{:S(2)}, u32[]{:S(2)}) collective-permute-start(f32[288,128]{1,0:T(8,128)S(1)} %get-tuple-element.54), channel_id=1, source_target_pairs={{0,2},{2,0},{1,3},{3,1},{4,6},{6,4},{5,7},{7,5},{8,10},{10,8},{9,1... | collective-permute-start | bytes 442376 | tf_op jit(solution)/shard_map/ppermute | solution.py:436
  93.3 12.4 %collective-permute-start.16 = (f32[288,128]{1,0:T(8,128)S(1)}, f32[288,128]{1,0:T(8,128)S(1)}, u32[]{:S(2)}, u32[]{:S(2)}) collective-permute-start(f32[288,128]{1,0:T(8,128)S(1)} %shard_map.66), channel_id=1, source_target_pairs={{2,4},{4,2},{3,5},{5,3},{6,8},{8,6},{7,9},{9,7},{10,12},{12,10},{1... | collective-permute-start | bytes 442376 | tf_op jit(solution)/shard_map/ppermute | solution.py:436

commit v8 on v7

--- a/solution.py
+++ b/solution.py
@@ -337,9 +337,8 @@
     return first[0:64, :]
 
 
-def image_kernel(device_ref, residual, smoothed, in_rows, across_rows, beside_rows, *refs):
-    *faces, table, direction, image, sums, fine_ghosts, wide, wide_across, wide_own, spread = refs[: 7 + 3 + 5]
-    scratch = refs[7 + 3 + 5 :]
+def correct_kernel(device_ref, smoothed, in_rows, across_rows, beside_rows, direction, changes, *scratch):
+    wide, wide_across, wide_own, spread, *scratch = scratch
     coarse_faces, across = scratch[4], scratch[-1]
     own = coarse_correction(device_ref[0], in_rows, across_rows, beside_rows, scratch)
     sub = lax.broadcasted_iota(jnp.int32, (8, LANES), 0)
@@ -368,7 +367,6 @@
             around = ((above_x + below_x) + (above_y + below_y)) + (above_z + below_z)
             change = centre - RELAX_FINE * (6.0 * centre - around)
             direction[at : at + 8, :] = smoothed[at : at + 8, :] + change
-    read_ghosts(table, faces, fine_ghosts, FINE)
     for face in range(6):
         for i in range(8):
             line = i // 2
@@ -382,9 +380,17 @@
             around = around + jnp.where(sub == 7, high, pltpu.roll(centre, 7, 0))
             around = around + wide_own[32 * face + 8 * line : 32 * face + 8 * line + 8, :]
             at = 64 * face + 8 * i
-            change = centre - RELAX_FINE * (5.0 * centre - around)
-            present = jnp.broadcast_to(table[WINDOW_ROW + face : WINDOW_ROW + face + 1, :], (8, LANES)) >= 0
-            fine_ghosts[at : at + 8, :] = fine_ghosts[at : at + 8, :] + jnp.where(present, change, 0.0)
+            changes[at : at + 8, :] = centre - RELAX_FINE * (5.0 * centre - around)
+
+
+def image_kernel(residual, direction, changes, *refs):
+    *faces, table, image, sums, fine_ghosts = refs
+    read_ghosts(table, faces, fine_ghosts, FINE)
+    for face in range(6):
+        present = jnp.broadcast_to(table[WINDOW_ROW + face : WINDOW_ROW + face + 1, :], (8, LANES)) >= 0
+        for at in range(64 * face, 64 * face + 64, 8):
+            change = jnp.where(present, changes[at : at + 8, :], 0.0)
+            fine_ghosts[at : at + 8, :] = fine_ghosts[at : at + 8, :] + change
     zero = jnp.zeros((8, LANES), jnp.float32)
     parts = [zero] * 5
     for x in range(8):
@@ -424,7 +430,8 @@
     for row in range(0, 512, 8):
         solution[row : row + 8, :] = step_size * direction[row : row + 8, :]
         left[row : row + 8, :] = residual[row : row + 8, :] - step_size * image[row : row + 8, :]
-    norm[...] = jnp.sqrt(old_square - 2.0 * step_size * cross_term + step_size * step_size * image_square)
+    root = jnp.sqrt(old_square - 2.0 * step_size * cross_term + step_size * step_size * image_square)
+    norm[0] = jnp.max(root)
 
 
 def swap(block, distance, offset, keep=lambda low: True):
@@ -481,22 +488,28 @@
     )
     all_blocks, wide_blocks, near_blocks = 2 * WIDEST + 1, 4 * REACH + 1, 2 * REACH + 1
     exchanged = exchange(FINE, *sides, table)
-    direction, image, sums = call(
-        image_kernel, [fine, fine, f32(lax.axis_size(AXES[1:]), 1, LANES)],
-        device, residual_in, smoothed, *share(blocks), *exchanged,
-        in_specs=[SMEM] + [VMEM] * 12,
+    direction, changes = call(
+        correct_kernel, [fine, f32(2 * FINE, LANES)], device, smoothed, *share(blocks),
+        in_specs=[SMEM] + [VMEM] * 4,
         scratch=[
-            fine_ghosts, scratch(128), scratch(384), scratch(192), scratch(512),
+            scratch(128), scratch(384), scratch(192), scratch(512),
             scratch(64 * all_blocks), scratch(96 * all_blocks), pltpu.VMEM((8 * wide_blocks, LANES), jnp.int32),
             scratch(64), scratch(96 * wide_blocks), scratch(96), *[scratch(64)] * 4,
             scratch(192 * near_blocks), scratch(192),
         ],
     )
+    image, sums = call(
+        image_kernel, [fine, f32(lax.axis_size(AXES[1:]), 1, LANES)],
+        residual_in, direction, changes, *exchanged, scratch=[fine_ghosts],
+    )
     received = lax.all_to_all(sums, AXES[1:], 0, 0, tiled=True)
     (sums,) = call(add_kernel, [f32(lax.axis_size("outer"), 1, LANES)], received)
     received = lax.all_to_all(sums, "outer", 0, 0, tiled=True)
-    solved, left, norm = call(finish_kernel, [fine, fine, f32(8, LANES)], received, residual_in, direction, image)
-    return solved, left, norm[0, 0]
+    solved, left, norm = call(
+        finish_kernel, [fine, fine, f32(1)], received, residual_in, direction, image,
+        out_specs=[VMEM, VMEM, SMEM],
+    )
+    return solved, left, norm.reshape(())
 
 
 def solution(mesh):

time: 156 us -> 153 us (0.981)
  waiting for transfers between devices: 29.4 us -> 26 us
  blocking collectives: 57.6 us -> 59.4 us
  starting transfers between devices: 59.3 us -> 57.7 us
    ppermute x17, waiting for transfers between devices: 29.4 us -> 26 us  [swap(): return lax.ppermute(block, AXES, route)]
    all_to_all x1, blocking collectives: 12.2 us -> 14.6 us  [step(): received = lax.all_to_all(sums, AXES[1:], 0, 0, tiled=True)]
    ppermute x17, starting transfers between devices: 59.3 us -> 57.7 us  [swap(): return lax.ppermute(block, AXES, route)]
    pallas_call x12 -> x13, Pallas kernels: 6.18 us -> 6.16 us  [call(): pl.pallas_call(kernel, out_shape=outs, in_specs=in_specs or [VMEM] * len(...]
  transfers between devices with their start and end apart: 17 -> 17, of which waited for: 8 -> 8; matrix products, arithmetic and copies ran while one was open for 0% -> 0% of each run, Pallas kernels for 0% -> 2%
where the time goes in v8:
time: 153 us; the launch traced here: 152 us
  blocking collectives  59.4 us (39%)
  starting transfers between devices  57.7 us (38%)
  waiting for transfers between devices  26 us (17%)
  Pallas kernels  6.16 us (4%)
  local copies, waits for them, and re-layouts  1.63 us (1%)
    ppermute x17, starting transfers between devices, swap(): return lax.ppermute(block, AXES, route)  57.7 us
    all_to_all x1, blocking collectives, step(): received = lax.all_to_all(sums, 'outer', 0, 0, tiled=True)  32.8 us
    ppermute x17, waiting for transfers between devices, swap(): return lax.ppermute(block, AXES, route)  26 us
    all_to_all x1, blocking collectives, step(): received = lax.all_to_all(sums, AXES[1:], 0, 0, tiled=True)  14.6 us
    all_to_all x1, blocking collectives, share(): in_rows = lax.all_to_all(blocks, 'row', 0, 0, tiled=True)  12.1 us
    pallas_call x13, Pallas kernels, call(): pl.pallas_call(kernel, out_shape=outs, in_specs=in_specs or [VMEM] * len(...  6.16 us
  transfers between devices with their start and end apart: 17, of which 8 were waited for; matrix products, arithmetic and copies ran while one was open for 0% of the time, Pallas kernels for 2%

profile of v8, /device:TPU:1, one launch (start us, length us, event | category | flops | bytes accessed | tf_op | source)
XLA Modules:
  0.0 151.8 jit_solution(17504733684912841496)
XLA Ops:
  2.9 4.0 %collective-permute-start = (f32[192,128]{1,0:T(8,128)S(1)}, f32[192,128]{1,0:T(8,128)S(1)}, u32[]{:S(2)}, u32[]{:S(2)}) collective-permute-start(f32[192,128]{1,0:T(8,128)S(1)} %get-tuple-element.36), channel_id=1, source_target_pairs={{0,1},{1,0},{2,3},{3,2},{4,5},{5,4},{6,7},{7,6},{8,9},{9,8},{10,11... | collective-permute-start | bytes 294920 | tf_op jit(solution)/shard_map/ppermute | solution.py:443
  7.6 5.7 %collective-permute-start.2 = (f32[192,128]{1,0:T(8,128)S(1)}, f32[192,128]{1,0:T(8,128)S(1)}, u32[]{:S(2)}, u32[]{:S(2)}) collective-permute-start(f32[192,128]{1,0:T(8,128)S(1)} %get-tuple-element.37), channel_id=1, source_target_pairs={{7,8},{8,7},{15,16},{16,15},{23,24},{24,23},{31,32},{32,31},{39,40... | collective-permute-start | bytes 294920 | tf_op jit(solution)/shard_map/ppermute | solution.py:443
  13.4 3.0 %collective-permute-done.2.near_across = f32[192,128]{1,0:T(8,128)S(1)} collective-permute-done((f32[192,128]{1,0:T(8,128)S(1)}, f32[192,128]{1,0:T(8,128)S(1)}, u32[]{:S(2)}, u32[]{:S(2)}) %collective-permute-start.2) | collective-permute-done | bytes 98336 | tf_op jit(solution)/shard_map/ppermute | solution.py:443
  16.5 1.9 %collective-permute-start.3 = (f32[288,128]{1,0:T(8,128)S(1)}, f32[288,128]{1,0:T(8,128)S(1)}, u32[]{:S(2)}, u32[]{:S(2)}) collective-permute-start(f32[288,128]{1,0:T(8,128)S(1)} %get-tuple-element.40), channel_id=1, source_target_pairs={{0,2},{2,0},{1,3},{3,1},{4,6},{6,4},{5,7},{7,5},{8,10},{10,8},{9,1... | collective-permute-start | bytes 442376 | tf_op jit(solution)/shard_map/ppermute | solution.py:443
  18.5 6.3 %collective-permute-start.4 = (f32[288,128]{1,0:T(8,128)S(1)}, f32[288,128]{1,0:T(8,128)S(1)}, u32[]{:S(2)}, u32[]{:S(2)}) collective-permute-start(f32[288,128]{1,0:T(8,128)S(1)} %shard_map.60), channel_id=1, source_target_pairs={{2,4},{4,2},{3,5},{5,3},{6,8},{8,6},{7,9},{9,7},{10,12},{12,10},{1... | collective-permute-start | bytes 442376 | tf_op jit(solution)/shard_map/ppermute | solution.py:443
  24.8 6.5 %collective-permute-done.4.refs_5_ = f32[288,128]{1,0:T(8,128)S(1)} collective-permute-done((f32[288,128]{1,0:T(8,128)S(1)}, f32[288,128]{1,0:T(8,128)S(1)}, u32[]{:S(2)}, u32[]{:S(2)}) %collective-permute-start.4) | collective-permute-done | bytes 147488 | tf_op jit(solution)/shard_map/ppermute | solution.py:443
  31.8 1.9 %collective-permute-start.5 = (f32[192,128]{1,0:T(8,128)S(1)}, f32[192,128]{1,0:T(8,128)S(1)}, u32[]{:S(2)}, u32[]{:S(2)}) collective-permute-start(f32[192,128]{1,0:T(8,128)S(1)} %get-tuple-element.44), channel_id=1, source_target_pairs={{0,1},{1,0},{2,3},{3,2},{4,5},{5,4},{6,7},{7,6},{8,9},{9,8},{10,11... | collective-permute-start | bytes 294920 | tf_op jit(solution)/shard_map/ppermute | solution.py:443
  34.4 5.4 %collective-permute-start.7 = (f32[192,128]{1,0:T(8,128)S(1)}, f32[192,128]{1,0:T(8,128)S(1)}, u32[]{:S(2)}, u32[]{:S(2)}) collective-permute-start(f32[192,128]{1,0:T(8,128)S(1)} %get-tuple-element.45), channel_id=1, source_target_pairs={{7,8},{8,7},{15,16},{16,15},{23,24},{24,23},{31,32},{32,31},{39,40... | collective-permute-start | bytes 294920 | tf_op jit(solution)/shard_map/ppermute | solution.py:443
  39.8 2.9 %collective-permute-done.7.near_across = f32[192,128]{1,0:T(8,128)S(1)} collective-permute-done((f32[192,128]{1,0:T(8,128)S(1)}, f32[192,128]{1,0:T(8,128)S(1)}, u32[]{:S(2)}, u32[]{:S(2)}) %collective-permute-start.7) | collective-permute-done | bytes 98336 | tf_op jit(solution)/shard_map/ppermute | solution.py:443
  42.8 1.9 %collective-permute-start.8 = (f32[288,128]{1,0:T(8,128)S(1)}, f32[288,128]{1,0:T(8,128)S(1)}, u32[]{:S(2)}, u32[]{:S(2)}) collective-permute-start(f32[288,128]{1,0:T(8,128)S(1)} %get-tuple-element.47), channel_id=1, source_target_pairs={{0,2},{2,0},{1,3},{3,1},{4,6},{6,4},{5,7},{7,5},{8,10},{10,8},{9,1... | collective-permute-start | bytes 442376 | tf_op jit(solution)/shard_map/ppermute | solution.py:443
  44.8 8.8 %collective-permute-start.9 = (f32[288,128]{1,0:T(8,128)S(1)}, f32[288,128]{1,0:T(8,128)S(1)}, u32[]{:S(2)}, u32[]{:S(2)}) collective-permute-start(f32[288,128]{1,0:T(8,128)S(1)} %shard_map.63), channel_id=1, source_target_pairs={{2,4},{4,2},{3,5},{5,3},{6,8},{8,6},{7,9},{9,7},{10,12},{12,10},{1... | collective-permute-start | bytes 442376 | tf_op jit(solution)/shard_map/ppermute | solution.py:443
  53.7 5.5 %collective-permute-done.9.refs_5_ = f32[288,128]{1,0:T(8,128)S(1)} collective-permute-done((f32[288,128]{1,0:T(8,128)S(1)}, f32[288,128]{1,0:T(8,128)S(1)}, u32[]{:S(2)}, u32[]{:S(2)}) %collective-permute-start.9) | collective-permute-done | bytes 147488 | tf_op jit(solution)/shard_map/ppermute | solution.py:443
  59.7 12.1 %all_to_all.15.in_rows = f32[8,72,128]{2,1,0:T(8,128)S(1)} all-to-all(f32[8,72,128]{2,1,0:T(8,128)S(1)} %get-tuple-element.49), channel_id=1, replica_groups=mesh['outer'=48,'pair'=2,'row'=8] {'row'}, dimensions={0} | all-to-all | bytes 589824 | tf_op jit(solution)/shard_map/all_to_all | solution.py:465
  71.7 6.8 %collective-permute-start.10 = (f32[8,72,128]{2,1,0:T(8,128)S(1)}, f32[8,72,128]{2,1,0:T(8,128)S(1)}, u32[]{:S(2)}, u32[]{:S(2)}) collective-permute-start(f32[8,72,128]{2,1,0:T(8,128)S(1)} %all_to_all.15.in_rows), channel_id=1, source_target_pairs={{8,16},{16,8},{9,17},{17,9},{10,18},{18,10},{11,19},{19,11},{12,20... | collective-permute-start | bytes 884744 | tf_op jit(solution)/shard_map/ppermute | solution.py:443
  78.6 1.9 %collective-permute-start.11 = (f32[8,72,128]{2,1,0:T(8,128)S(1)}, f32[8,72,128]{2,1,0:T(8,128)S(1)}, u32[]{:S(2)}, u32[]{:S(2)}) collective-permute-start(f32[8,72,128]{2,1,0:T(8,128)S(1)} %all_to_all.15.in_rows), channel_id=1, source_target_pairs={{0,8},{8,0},{1,9},{9,1},{2,10},{10,2},{3,11},{11,3},{4,12},{12,4},... | collective-permute-start | bytes 884744 | tf_op jit(solution)/shard_map/ppermute | solution.py:443
  80.5 2.2 %collective-permute-start.12 = (f32[192,128]{1,0:T(8,128)S(1)}, f32[192,128]{1,0:T(8,128)S(1)}, u32[]{:S(2)}, u32[]{:S(2)}) collective-permute-start(f32[192,128]{1,0:T(8,128)S(1)} %get-tuple-element.54), channel_id=1, source_target_pairs={{0,1},{1,0},{2,3},{3,2},{4,5},{5,4},{6,7},{7,6},{8,9},{9,8},{10,11... | collective-permute-start | bytes 294920 | tf_op jit(solution)/shard_map/ppermute | solution.py:443
  83.4 2.8 %collective-permute-start.14 = (f32[192,128]{1,0:T(8,128)S(1)}, f32[192,128]{1,0:T(8,128)S(1)}, u32[]{:S(2)}, u32[]{:S(2)}) collective-permute-start(f32[192,128]{1,0:T(8,128)S(1)} %get-tuple-element.55), channel_id=1, source_target_pairs={{7,8},{8,7},{15,16},{16,15},{23,24},{24,23},{31,32},{32,31},{39,40... | collective-permute-start | bytes 294920 | tf_op jit(solution)/shard_map/ppermute | solution.py:443
  86.2 4.3 %collective-permute-done.14.near_across = f32[192,128]{1,0:T(8,128)S(1)} collective-permute-done((f32[192,128]{1,0:T(8,128)S(1)}, f32[192,128]{1,0:T(8,128)S(1)}, u32[]{:S(2)}, u32[]{:S(2)}) %collective-permute-start.14) | collective-permute-done | bytes 98336 | tf_op jit(solution)/shard_map/ppermute | solution.py:443
  90.6 1.9 %collective-permute-start.15 = (f32[288,128]{1,0:T(8,128)S(1)}, f32[288,128]{1,0:T(8,128)S(1)}, u32[]{:S(2)}, u32[]{:S(2)}) collective-permute-start(f32[288,128]{1,0:T(8,128)S(1)} %get-tuple-element.57), channel_id=1, source_target_pairs={{0,2},{2,0},{1,3},{3,1},{4,6},{6,4},{5,7},{7,5},{8,10},{10,8},{9,1... | collective-permute-start | bytes 442376 | tf_op jit(solution)/shard_map/ppermute | solution.py:443
  92.7 4.2 %collective-permute-start.16 = (f32[288,128]{1,0:T(8,128)S(1)}, f32[288,128]{1,0:T(8,128)S(1)}, u32[]{:S(2)}, u32[]{:S(2)}) collective-permute-start(f32[288,128]{1,0:T(8,128)S(1)} %shard_map.67), channel_id=1, source_target_pairs={{2,4},{4,2},{3,5},{5,3},{6,8},{8,6},{7,9},{9,7},{10,12},{12,10},{1... | collective-permute-start | bytes 442376 | tf_op jit(solution)/shard_map/ppermute | solution.py:443
  96.9 2.1 %shard_map.65 = (f32[512,128]{1,0:T(8,128)S(1)}, f32[384,128]{1,0:T(8,128)S(1)}) custom-call(s32[1]{0:T(128)} %bitcast.device_ref, f32[512,128]{1,0:T(8,128)S(1)} %get-tuple-element.48.smoothed, f32[8,72,128]{2,1,0:T(8,128)S(1)} %all_to_all.15.in_rows, f32[8,72,128]{2,1,0:T(8,128)S(1)} %collective-permute-done.10.across_rows, ...), custom_call_target="tpu_custom_call" | custom-call | tf_op jit(solution)/shard_map/pallas_call | solution.py:47
  100.3 2.5 %collective-permute-done.16.refs_5_ = f32[288,128]{1,0:T(8,128)S(1)} collective-permute-done((f32[288,128]{1,0:T(8,128)S(1)}, f32[288,128]{1,0:T(8,128)S(1)}, u32[]{:S(2)}, u32[]{:S(2)}) %collective-permute-start.16) | collective-permute-done | bytes 147488 | tf_op jit(solution)/shard_map/ppermute | solution.py:443
  103.5 14.6 %all_to_all.16.received = f32[16,1,128]{2,1,0:T(1,128)S(1)} all-to-all(f32[16,1,128]{2,1,0:T(1,128)S(1)} %get-tuple-element.58), channel_id=1, replica_groups=mesh['outer'=48,'pair'=2,'row'=8] {'pair','row'}, dimensions={0} | all-to-all | bytes 16384 | tf_op jit(solution)/shard_map/all_to_all | solution.py:505
  118.0 32.8 %all_to_all.17.received = f32[48,1,128]{2,1,0:T(1,128)S(1)} all-to-all(f32[48,1,128]{2,1,0:T(1,128)S(1)} %shard_map.69), channel_id=1, replica_groups=mesh['outer'=48,'pair'=2,'row'=8] {'outer'}, dimensions={0} | all-to-all | bytes 49152 | tf_op jit(solution)/shard_map/all_to_all | solution.py:507
  (32 shorter events, 9.1 us)
Async XLA Ops:
  0.6 0.7 copy-start.2
  0.7 0.7 copy-start.1
  1.3 0.9 copy-start
  2.9 10.4 %collective-permute-start = (f32[192,128]{1,0:T(8,128)S(1)}, f32[192,128]{1,0:T(8,128)S(1)}, u32[]{:S(2)}, u32[]{:S(2)}) collective-permute-start(f32[192,128]{1,0:T(8,128)S(1)} %get-tuple-element.36), channel_id=1, source_target_pairs={{0,1},{1,0},{2,3},{3,2},{4,5},{5,4},{6,7},{7,6},{8,9},{9,8},{10,11... | collective-permute-start | bytes 294920 | tf_op jit(solution)/shard_map/ppermute | solution.py:443
  7.0 6.4 %collective-permute-start.1 = (f32[192,128]{1,0:T(8,128)S(1)}, f32[192,128]{1,0:T(8,128)S(1)}, u32[]{:S(2)}, u32[]{:S(2)}) collective-permute-start(f32[192,128]{1,0:T(8,128)S(1)} %get-tuple-element.37), channel_id=1, source_target_pairs={{1,2},{2,1},{3,4},{4,3},{5,6},{6,5},{9,10},{10,9},{11,12},{12,11},... | collective-permute-start | bytes 294920 | tf_op jit(solution)/shard_map/ppermute | solution.py:443
  7.6 8.7 %collective-permute-start.2 = (f32[192,128]{1,0:T(8,128)S(1)}, f32[192,128]{1,0:T(8,128)S(1)}, u32[]{:S(2)}, u32[]{:S(2)}) collective-permute-start(f32[192,128]{1,0:T(8,128)S(1)} %get-tuple-element.37), channel_id=1, source_target_pairs={{7,8},{8,7},{15,16},{16,15},{23,24},{24,23},{31,32},{32,31},{39,40... | collective-permute-start | bytes 294920 | tf_op jit(solution)/shard_map/ppermute | solution.py:443
  16.5 8.3 %collective-permute-start.3 = (f32[288,128]{1,0:T(8,128)S(1)}, f32[288,128]{1,0:T(8,128)S(1)}, u32[]{:S(2)}, u32[]{:S(2)}) collective-permute-start(f32[288,128]{1,0:T(8,128)S(1)} %get-tuple-element.40), channel_id=1, source_target_pairs={{0,2},{2,0},{1,3},{3,1},{4,6},{6,4},{5,7},{7,5},{8,10},{10,8},{9,1... | collective-permute-start | bytes 442376 | tf_op jit(solution)/shard_map/ppermute | solution.py:443
  18.5 12.8 %collective-permute-start.4 = (f32[288,128]{1,0:T(8,128)S(1)}, f32[288,128]{1,0:T(8,128)S(1)}, u32[]{:S(2)}, u32[]{:S(2)}) collective-permute-start(f32[288,128]{1,0:T(8,128)S(1)} %shard_map.60), channel_id=1, source_target_pairs={{2,4},{4,2},{3,5},{5,3},{6,8},{8,6},{7,9},{9,7},{10,12},{12,10},{1... | collective-permute-start | bytes 442376 | tf_op jit(solution)/shard_map/ppermute | solution.py:443
  31.8 8.0 %collective-permute-start.5 = (f32[192,128]{1,0:T(8,128)S(1)}, f32[192,128]{1,0:T(8,128)S(1)}, u32[]{:S(2)}, u32[]{:S(2)}) collective-permute-start(f32[192,128]{1,0:T(8,128)S(1)} %get-tuple-element.44), channel_id=1, source_target_pairs={{0,1},{1,0},{2,3},{3,2},{4,5},{5,4},{6,7},{7,6},{8,9},{9,8},{10,11... | collective-permute-start | bytes 294920 | tf_op jit(solution)/shard_map/ppermute | solution.py:443
  33.8 6.1 %collective-permute-start.6 = (f32[192,128]{1,0:T(8,128)S(1)}, f32[192,128]{1,0:T(8,128)S(1)}, u32[]{:S(2)}, u32[]{:S(2)}) collective-permute-start(f32[192,128]{1,0:T(8,128)S(1)} %get-tuple-element.45), channel_id=1, source_target_pairs={{1,2},{2,1},{3,4},{4,3},{5,6},{6,5},{9,10},{10,9},{11,12},{12,11},... | collective-permute-start | bytes 294920 | tf_op jit(solution)/shard_map/ppermute | solution.py:443
  34.4 8.3 %collective-permute-start.7 = (f32[192,128]{1,0:T(8,128)S(1)}, f32[192,128]{1,0:T(8,128)S(1)}, u32[]{:S(2)}, u32[]{:S(2)}) collective-permute-start(f32[192,128]{1,0:T(8,128)S(1)} %get-tuple-element.45), channel_id=1, source_target_pairs={{7,8},{8,7},{15,16},{16,15},{23,24},{24,23},{31,32},{32,31},{39,40... | collective-permute-start | bytes 294920 | tf_op jit(solution)/shard_map/ppermute | solution.py:443
  42.8 10.8 %collective-permute-start.8 = (f32[288,128]{1,0:T(8,128)S(1)}, f32[288,128]{1,0:T(8,128)S(1)}, u32[]{:S(2)}, u32[]{:S(2)}) collective-permute-start(f32[288,128]{1,0:T(8,128)S(1)} %get-tuple-element.47), channel_id=1, source_target_pairs={{0,2},{2,0},{1,3},{3,1},{4,6},{6,4},{5,7},{7,5},{8,10},{10,8},{9,1... | collective-permute-start | bytes 442376 | tf_op jit(solution)/shard_map/ppermute | solution.py:443
  44.8 14.3 %collective-permute-start.9 = (f32[288,128]{1,0:T(8,128)S(1)}, f32[288,128]{1,0:T(8,128)S(1)}, u32[]{:S(2)}, u32[]{:S(2)}) collective-permute-start(f32[288,128]{1,0:T(8,128)S(1)} %shard_map.63), channel_id=1, source_target_pairs={{2,4},{4,2},{3,5},{5,3},{6,8},{8,6},{7,9},{9,7},{10,12},{12,10},{1... | collective-permute-start | bytes 442376 | tf_op jit(solution)/shard_map/ppermute | solution.py:443
  71.7 25.1 %collective-permute-start.10 = (f32[8,72,128]{2,1,0:T(8,128)S(1)}, f32[8,72,128]{2,1,0:T(8,128)S(1)}, u32[]{:S(2)}, u32[]{:S(2)}) collective-permute-start(f32[8,72,128]{2,1,0:T(8,128)S(1)} %all_to_all.15.in_rows), channel_id=1, source_target_pairs={{8,16},{16,8},{9,17},{17,9},{10,18},{18,10},{11,19},{19,11},{12,20... | collective-permute-start | bytes 884744 | tf_op jit(solution)/shard_map/ppermute | solution.py:443
  78.6 18.3 %collective-permute-start.11 = (f32[8,72,128]{2,1,0:T(8,128)S(1)}, f32[8,72,128]{2,1,0:T(8,128)S(1)}, u32[]{:S(2)}, u32[]{:S(2)}) collective-permute-start(f32[8,72,128]{2,1,0:T(8,128)S(1)} %all_to_all.15.in_rows), channel_id=1, source_target_pairs={{0,8},{8,0},{1,9},{9,1},{2,10},{10,2},{3,11},{11,3},{4,12},{12,4},... | collective-permute-start | bytes 884744 | tf_op jit(solution)/shard_map/ppermute | solution.py:443
  80.5 5.7 %collective-permute-start.12 = (f32[192,128]{1,0:T(8,128)S(1)}, f32[192,128]{1,0:T(8,128)S(1)}, u32[]{:S(2)}, u32[]{:S(2)}) collective-permute-start(f32[192,128]{1,0:T(8,128)S(1)} %get-tuple-element.54), channel_id=1, source_target_pairs={{0,1},{1,0},{2,3},{3,2},{4,5},{5,4},{6,7},{7,6},{8,9},{9,8},{10,11... | collective-permute-start | bytes 294920 | tf_op jit(solution)/shard_map/ppermute | solution.py:443
  82.7 3.6 %collective-permute-start.13 = (f32[192,128]{1,0:T(8,128)S(1)}, f32[192,128]{1,0:T(8,128)S(1)}, u32[]{:S(2)}, u32[]{:S(2)}) collective-permute-start(f32[192,128]{1,0:T(8,128)S(1)} %get-tuple-element.55), channel_id=1, source_target_pairs={{1,2},{2,1},{3,4},{4,3},{5,6},{6,5},{9,10},{10,9},{11,12},{12,11},... | collective-permute-start | bytes 294920 | tf_op jit(solution)/shard_map/ppermute | solution.py:443
  83.4 7.1 %collective-permute-start.14 = (f32[192,128]{1,0:T(8,128)S(1)}, f32[192,128]{1,0:T(8,128)S(1)}, u32[]{:S(2)}, u32[]{:S(2)}) collective-permute-start(f32[192,128]{1,0:T(8,128)S(1)} %get-tuple-element.55), channel_id=1, source_target_pairs={{7,8},{8,7},{15,16},{16,15},{23,24},{24,23},{31,32},{32,31},{39,40... | collective-permute-start | bytes 294920 | tf_op jit(solution)/shard_map/ppermute | solution.py:443
  90.6 9.7 %collective-permute-start.15 = (f32[288,128]{1,0:T(8,128)S(1)}, f32[288,128]{1,0:T(8,128)S(1)}, u32[]{:S(2)}, u32[]{:S(2)}) collective-permute-start(f32[288,128]{1,0:T(8,128)S(1)} %get-tuple-element.57), channel_id=1, source_target_pairs={{0,2},{2,0},{1,3},{3,1},{4,6},{6,4},{5,7},{7,5},{8,10},{10,8},{9,1... | collective-permute-start | bytes 442376 | tf_op jit(solution)/shard_map/ppermute | solution.py:443
  92.7 10.1 %collective-permute-start.16 = (f32[288,128]{1,0:T(8,128)S(1)}, f32[288,128]{1,0:T(8,128)S(1)}, u32[]{:S(2)}, u32[]{:S(2)}) collective-permute-start(f32[288,128]{1,0:T(8,128)S(1)} %shard_map.67), channel_id=1, source_target_pairs={{2,4},{4,2},{3,5},{5,3},{6,8},{8,6},{7,9},{9,7},{10,12},{12,10},{1... | collective-permute-start | bytes 442376 | tf_op jit(solution)/shard_map/ppermute | solution.py:443
